TPU v7x, 32 devices: a whole 2x2x4 slice. The times are simulated.
32 devices in a mesh: dom: 16 (over z, y, core), st: 2 (over x).
Axes of the slice: x: 2, y: 2, z: 4, core: 2. Of those that a mesh axis runs over, the one named last changes fastest.
Arguments:
- start_states: bfloat16 [512, 57344], P('st', 'dom'), may hold values from -6 to 6
- stiffness: bfloat16 [512, 512], replicated, may hold values from -1 to 3
- cell_scale: float32 [128], P('dom'), may hold values from 0.5 to 2
- potential: float32 [57344], P('dom'), may hold values from -2 to 2
- connectivity: int32 [128, 512], P('dom'), may hold values from 0 to 3479, as said below
- shared_nodes: int32 [16, 2, 435], P('dom'), may hold values from 0 to 3479, as said below
- filter_bounds: float32 [2], replicated, may hold values from 3 to 60, as said below
Outputs:
- new_states: bfloat16 [512, 57344], P('st', 'dom')
Inputs may be any that keep to these rules, and one draw needn't show every extreme that they name: `connectivity`: for each domain, its cells' entries name every one of its 3480 local nodes; nodes of a domain are numbered in a drawn order; cells of a domain share nodes as hexahedral elements of order 7 do. shared_nodes[d, 1] and shared_nodes[d + 1, 0] list the same mesh nodes in the same order; within one domain the two lists are distinct nodes and disjoint. filter_bounds[0] < filter_bounds[1].
All inputs are finite; a program needn't handle non-finite values.
Results may differ from a plain program's by a relative error of at most 0.0049.
The roundings to bfloat16 on the way count: a program that leaves them out, or rounds other values in their place, can miss the bound.
Values may be sent and summed in bfloat16 or wider, within the bound.
No kernel may reach another device: no remote copies, remote signals or barrier semaphores. Data moves between devices by JAX's collectives and lax.ppermute only.
A program may use at most 64 MiB of HBM per device.

v0:
```python
import jax
import jax.numpy as jnp
from jax import lax
from jax.sharding import PartitionSpec as P

DEGREE = 3
NS_ITERS = 3
LN = 3480


def passed_along(x, axis, by):
    devices = lax.axis_size(axis)
    pairs = [(i, i + by) for i in range(devices) if 0 <= i + by < devices]
    return lax.ppermute(x, axis, pairs)


def inverse_root(gram):
    frobenius = jnp.sqrt(jnp.sum(gram * gram) + 1e-06)
    iterate = gram / frobenius
    identity = jnp.eye(gram.shape[0], dtype=jnp.float32)
    inverse = identity
    for sweep in range(NS_ITERS):
        factor = 1.5 * identity - 0.5 * jnp.dot(inverse, iterate, precision=lax.Precision.HIGHEST)
        iterate = jnp.dot(iterate, factor, precision=lax.Precision.HIGHEST)
        inverse = jnp.dot(factor, inverse, precision=lax.Precision.HIGHEST)
    return (inverse / jnp.sqrt(frobenius)).astype(jnp.bfloat16)


def operate(field, stiffness, cell_scale, potential, connectivity, left_ids, right_ids):
    count = field.shape[0]
    cell_values = field[:, connectivity]
    products = jnp.einsum("scn,nm->scm", cell_values, stiffness, preferred_element_type=jnp.float32)
    products = products * cell_scale[None, :, None]
    assembled = (
        jnp.zeros(field.shape, jnp.float32)
        .at[:, connectivity.reshape(-1)]
        .add(products.reshape(count, -1))
    )
    assembled = assembled + potential[None, :] * field.astype(jnp.float32)
    upper_face = assembled[:, right_ids]
    lower_face = assembled[:, left_ids]
    from_below = passed_along(upper_face.astype(jnp.bfloat16), "dom", 1).astype(upper_face.dtype)
    from_above = passed_along(lower_face, "dom", -1)
    return assembled.at[:, left_ids].add(from_below).at[:, right_ids].add(from_above)


def body(start_states, stiffness, cell_scale, potential, connectivity, shared_nodes, filter_bounds):
    node_ids = jnp.arange(start_states.shape[1])
    inside = (node_ids < LN).astype(jnp.bfloat16)
    states = start_states * inside[None, :]
    left_ids = shared_nodes[0, 0]
    right_ids = shared_nodes[0, 1]

    def apply_hamiltonian(field):
        return operate(field, stiffness, cell_scale, potential, connectivity, left_ids, right_ids)

    center = (filter_bounds[1] + filter_bounds[0]) / 2.0
    half_width = (filter_bounds[1] - filter_bounds[0]) / 2.0
    previous = states
    current = (
        (apply_hamiltonian(states) - center * states.astype(jnp.float32)) / half_width
    ).astype(jnp.bfloat16)
    for degree_step in range(DEGREE - 1):
        following = 2.0 * (
            apply_hamiltonian(current) - center * current.astype(jnp.float32)
        ) / half_width - previous.astype(jnp.float32)
        previous, current = (current, following.astype(jnp.bfloat16))
    keep = jnp.where(lax.axis_index("dom") > 0, 0.0, 1.0).astype(jnp.bfloat16)
    owned = inside.at[left_ids].set(keep)
    block_states = current.shape[0]
    masked = current * owned[None, :]
    partial_rows = lax.dot_general(
        masked,
        lax.all_gather(current, "st", axis=0, tiled=True),
        (((1,), (1,)), ((), ())),
        preferred_element_type=jnp.float32,
    )
    summed_rows = lax.psum(partial_rows, "dom")
    gram = lax.all_gather(summed_rows, "st", axis=0, tiled=True)
    coeffs = inverse_root(gram)
    columns = lax.dynamic_slice_in_dim(coeffs, lax.axis_index("st") * block_states, block_states, 1)
    rotated = lax.dot_general(
        columns,
        lax.all_gather(current, "st", axis=0, tiled=True),
        (((0,), (0,)), ((), ())),
        preferred_element_type=jnp.float32,
    )
    return rotated.astype(jnp.bfloat16)


def solution(mesh):
    placed = (P("st", "dom"), P(), P("dom"), P("dom"), P("dom", None), P("dom", None, None), P())
    return jax.shard_map(
        body, mesh=mesh, in_specs=placed, out_specs=P("st", "dom"), check_vma=False
    )
```

profile of v0, /device:TPU:0, one launch (start us, length us, event | category | flops | bytes accessed | tf_op | source)
XLA Modules:
  0.0 507.8 jit_solution(1948329430281153978)
XLA Ops:
  6.6 3.9 copy.12
  10.5 4.8 convert_multiply_fusion.3
  15.3 16.9 %gather_fusion = bf16[4096,256]{1,0:T(8,128)(2,1)} fusion(bf16[256,3584]{0,1:T(8,128)(2,1)S(1)} %get-tuple-element.10, s32[4096]{0:T(1024)S(1)} %broadcast_clamp_fusion), kind=kCustom, calls=%fused_computation | custom fusion | bytes 4210688 | tf_op jit(solution)/shard_map/gather | solution.py:31
  32.3 3.9 copy.13
  36.2 4.8 convolution_multiply_fusion.2
  41.0 5.4 %copy.14 = f32[256,8,512]{0,2,1:T(8,128)} copy(f32[256,8,512]{2,0,1:T(8,128)} %convolution_multiply_fusion.2) | data formatting | bytes 8388608 | tf_op jit(solution)/shard_map/mul | solution.py:33
  46.4 26.7 %scatter_fusion = f32[256,3584]{0,1:T(8,128)} fusion(f32[256,3584]{0,1:T(8,128)} %get-tuple-element.9, s32[4096]{0:T(1024)S(1)} %bitcast.100, f32[4096,256]{1,0:T(8,128)} %bitcast.88), kind=kCustom, calls=%fused_computation.9 | custom fusion | flops 1048576 | bytes 12599296 | tf_op jit(solution)/shard_map/scatter-add | solution.py:37
  73.1 3.8 gather_fusion.2
  76.9 1.3 collective-permute-start.1
  78.2 3.7 gather_fusion.1
  82.0 3.0 collective-permute-start
  85.0 0.6 fusion.45
  88.3 0.0 collective-permute-done
  88.3 6.6 %scatter_custom_fusion.1 = f32[256,3584]{0,1:T(8,128)} fusion(f32[256,3584]{0,1:T(8,128)} %scatter_fusion, s32[435]{0:T(512)S(1)} %bitcast.107, bf16[256,435]{0,1:T(8,128)(2,1)S(1)} %collective-permute-done), kind=kCustom, calls=%fused_computation.74 | custom fusion | flops 222720 | bytes 3895296 | tf_op jit(solution)/shard_map/scatter-add | solution.py:44
  94.9 0.0 collective-permute-done.1
  94.9 6.8 %scatter_custom_fusion.2 = f32[256,3584]{0,1:T(8,128)} fusion(f32[256,3584]{0,1:T(8,128)} %scatter_custom_fusion.1, s32[435]{0:T(512)S(1)} %bitcast.112, f32[256,435]{0,1:T(8,128)S(1)} %collective-permute-done.1), kind=kCustom, calls=%fused_computation.72 | custom fusion | flops 111360 | bytes 4120576 | tf_op jit(solution)/shard_map/scatter-add | solution.py:44
  101.7 4.5 convert_multiply_fusion.1
  106.2 16.9 %gather_fusion.3 = bf16[4096,256]{1,0:T(8,128)(2,1)} fusion(bf16[256,3584]{0,1:T(8,128)(2,1)S(1)} %get-tuple-element.8, s32[4096]{0:T(1024)S(1)} %broadcast_clamp_fusion), kind=kCustom, calls=%fused_computation.3 | custom fusion | bytes 4210688 | tf_op jit(solution)/shard_map/gather | solution.py:31
  123.1 3.9 copy.15
  127.0 4.8 convolution_multiply_fusion.1
  131.9 5.3 %copy.16 = f32[256,8,512]{0,2,1:T(8,128)} copy(f32[256,8,512]{2,0,1:T(8,128)} %convolution_multiply_fusion.1) | data formatting | bytes 8388608 | tf_op jit(solution)/shard_map/mul | solution.py:33
  137.2 26.7 %scatter_fusion.1 = f32[256,3584]{0,1:T(8,128)} fusion(f32[256,3584]{0,1:T(8,128)} %get-tuple-element.7, s32[4096]{0:T(1024)S(1)} %bitcast.101, f32[4096,256]{1,0:T(8,128)} %bitcast.90), kind=kCustom, calls=%fused_computation.12 | custom fusion | flops 1048576 | bytes 12599296 | tf_op jit(solution)/shard_map/scatter-add | solution.py:37
  163.9 3.7 gather_fusion.5
  167.6 1.3 collective-permute-start.3
  168.9 3.7 gather_fusion.4
  172.7 5.8 %collective-permute-start.2 = (bf16[256,435]{0,1:T(8,128)(2,1)S(1)}, bf16[256,435]{0,1:T(8,128)(2,1)}, u32[]{:S(2)}, u32[]{:S(2)}) collective-permute-start(bf16[256,435]{0,1:T(8,128)(2,1)S(1)} %bitcast.99), channel_id=1, source_target_pairs={{0,2},{2,4},{4,6},{6,8},{8,10},{10,12},{12,14},{14,16},{16,18},{18... | collective-permute-start | bytes 668168 | tf_op jit(solution)/shard_map/ppermute | solution.py:14
  178.5 0.6 collective-permute-done.2
  179.0 6.9 %scatter_custom_fusion.4 = f32[256,3584]{0,1:T(8,128)} fusion(f32[256,3584]{0,1:T(8,128)} %scatter_fusion.1, s32[435]{0:T(512)S(1)} %bitcast.108, bf16[256,435]{0,1:T(8,128)(2,1)} %collective-permute-done.2), kind=kCustom, calls=%fused_computation.70 | custom fusion | flops 222720 | bytes 3895296 | tf_op jit(solution)/shard_map/scatter-add | solution.py:44
  186.0 17.8 %scatter_custom_fusion.5 = f32[256,3584]{0,1:T(8,128)} fusion(f32[256,3584]{0,1:T(8,128)} %scatter_custom_fusion.4, s32[435]{0:T(512)} %bitcast.113, f32[256,435]{0,1:T(8,128)S(1)} %collective-permute-done.3), kind=kCustom, calls=%fused_computation.68 | custom fusion | flops 111360 | bytes 4115456 | tf_op jit(solution)/shard_map/scatter-add | solution.py:44
  203.8 5.0 convert_multiply_fusion.5
  208.8 17.6 %gather_fusion.6 = bf16[4096,256]{1,0:T(8,128)(2,1)} fusion(bf16[256,3584]{0,1:T(8,128)(2,1)} %get-tuple-element.6, s32[4096]{0:T(1024)S(1)} %broadcast_clamp_fusion), kind=kCustom, calls=%fused_computation.6 | custom fusion | bytes 4210688 | tf_op jit(solution)/shard_map/gather | solution.py:31
  226.4 3.9 copy.17
  230.3 4.8 convolution_multiply_fusion
  235.2 5.3 %copy.18 = f32[256,8,512]{0,2,1:T(8,128)} copy(f32[256,8,512]{2,0,1:T(8,128)} %convolution_multiply_fusion) | data formatting | bytes 8388608 | tf_op jit(solution)/shard_map/mul | solution.py:33
  240.5 26.7 %scatter_fusion.2 = f32[256,3584]{0,1:T(8,128)} fusion(f32[256,3584]{0,1:T(8,128)} %get-tuple-element.5, s32[4096]{0:T(1024)S(1)} %bitcast.102, f32[4096,256]{1,0:T(8,128)} %bitcast.89), kind=kCustom, calls=%fused_computation.15 | custom fusion | flops 1048576 | bytes 12599296 | tf_op jit(solution)/shard_map/scatter-add | solution.py:37
  267.2 3.7 gather_fusion.8
  270.9 1.3 collective-permute-start.5
  272.2 3.7 gather_fusion.7
  276.0 8.0 %collective-permute-start.4 = (bf16[256,435]{0,1:T(8,128)(2,1)S(1)}, bf16[256,435]{0,1:T(8,128)(2,1)}, u32[]{:S(2)}, u32[]{:S(2)}) collective-permute-start(bf16[256,435]{0,1:T(8,128)(2,1)S(1)} %bitcast.98), channel_id=1, source_target_pairs={{0,2},{2,4},{4,6},{6,8},{8,10},{10,12},{12,14},{14,16},{16,18},{18... | collective-permute-start | bytes 668168 | tf_op jit(solution)/shard_map/ppermute | solution.py:14
  284.0 0.6 collective-permute-done.4
  284.5 6.9 %scatter_custom_fusion.7 = f32[256,3584]{0,1:T(8,128)} fusion(f32[256,3584]{0,1:T(8,128)} %scatter_fusion.2, s32[435]{0:T(512)S(1)} %bitcast.109, bf16[256,435]{0,1:T(8,128)(2,1)} %collective-permute-done.4), kind=kCustom, calls=%fused_computation.66 | custom fusion | flops 222720 | bytes 3895296 | tf_op jit(solution)/shard_map/scatter-add | solution.py:44
  291.4 0.0 collective-permute-done.5
  291.4 6.7 %scatter_custom_fusion.8 = f32[256,3584]{0,1:T(8,128)} fusion(f32[256,3584]{0,1:T(8,128)} %scatter_custom_fusion.7, s32[435]{0:T(512)} %bitcast.114, f32[256,435]{0,1:T(8,128)S(1)} %collective-permute-done.5), kind=kCustom, calls=%fused_computation.64 | custom fusion | flops 111360 | bytes 4115456 | tf_op jit(solution)/shard_map/scatter-add | solution.py:44
  298.1 4.7 fusion.10
  302.9 0.0 all-gather.3.cloned.1.call-update
  302.9 0.0 all-reduce.2.cloned.1.call-start
  303.0 3.3 scatter_fusion.3
  306.3 55.6 %all-gather.3.cloned.1.call-done = bf16[512,3584]{0,1:T(8,128)(2,1)} async-done(((bf16[256,3584]{0,1:T(8,128)(2,1)}), bf16[512,3584]{0,1:T(8,128)(2,1)}) %all-gather.3.cloned.1.call-update) | async-done | bytes 3670032 | tf_op jit(solution)/shard_map/all_gather | solution.py:74
  361.9 5.0 fusion.14
  366.9 0.0 all-reduce.2.cloned.1.call-update
  366.9 0.3 all-gather.5.cloned.1.call-start
  367.2 90.6 %all-reduce.2.cloned.1.call-done = f32[256,512]{1,0:T(8,128)} async-done(((f32[256,512]{1,0:T(8,128)}), f32[256,512]{1,0:T(8,128)}) %all-reduce.2.cloned.1.call-update) | async-done | bytes 524304 | tf_op jit(solution)/shard_map/psum | solution.py:78
  457.7 0.0 all-gather.5.cloned.1.call-update
  457.8 23.3 %all-gather.5.cloned.1.call-done = f32[512,512]{1,0:T(8,128)} async-done(((f32[256,512]{1,0:T(8,128)}), f32[512,512]{1,0:T(8,128)}) %all-gather.5.cloned.1.call-update) | async-done | bytes 1048592 | tf_op jit(solution)/shard_map/all_gather | solution.py:79
  481.1 2.1 multiply_reduce_fusion
  483.9 2.4 select_subtract_fusion.2
  486.3 1.0 fusion.16
  487.3 1.9 fusion.37
  489.1 1.8 select_subtract_fusion.1
  491.0 1.8 fusion.46
  492.9 1.8 fusion.47
  494.8 1.8 select_subtract_fusion
  496.6 1.8 fusion.48
  498.5 2.4 convolution_convert_fusion
  (36 shorter events, 0.1 us)
Async XLA Ops:
  6.5 29.7 %copy-start = (bf16[512,512]{1,0:T(8,128)(2,1)S(1)}, bf16[512,512]{1,0:T(8,128)(2,1)}, u32[]{:S(2)}) copy-start(bf16[512,512]{1,0:T(8,128)(2,1)} %param.8) | copy-start | bytes 1572868
  6.5 3.9 copy-start.5
  6.5 4.0 copy-start.4
  6.5 355.4 %all-gather.3.cloned.1.call-start = ((), (), s32[]{:S(2)}) async-start(), calls=%async_computation | async-start | bytes 5505024 | tf_op jit(solution)/shard_map/all_gather | solution.py:74
  15.3 16.9 %copy-start.1 = (bf16[256,3584]{0,1:T(8,128)(2,1)}, bf16[256,3584]{0,1:T(8,128)(2,1)S(1)}, u32[]{:S(2)}) copy-start(bf16[256,3584]{0,1:T(8,128)(2,1)S(1)} %get-tuple-element.10) | copy-start | bytes 5505028
  32.3 4.0 copy-start.7
  41.0 5.4 %copy-start.9 = (s32[1,2,435]{2,1,0:T(2,128)S(1)}, s32[1,2,435]{2,1,0:T(2,128)}, u32[]{:S(2)}) copy-start(s32[1,2,435]{2,1,0:T(2,128)} %param.12) | copy-start | bytes 10444
  46.4 48.5 %copy-start.6 = (s32[435,1]{0,1:T(1,128)}, s32[435,1]{0,1:T(1,128)S(1)}, u32[]{:S(2)}) copy-start(s32[435,1]{0,1:T(1,128)S(1)} %get-tuple-element.11) | copy-start | bytes 5224
  73.1 11.9 %copy-start.10 = (f32[2]{0:T(128)S(1)}, f32[2]{0:T(128)}, u32[]{:S(2)}) copy-start(f32[2]{0:T(128)} %param.13) | copy-start | bytes 28
  76.9 18.0 %collective-permute-start.1 = (f32[256,435]{0,1:T(8,128)S(1)}, f32[256,435]{0,1:T(8,128)S(1)}, u32[]{:S(2)}, u32[]{:S(2)}) collective-permute-start(f32[256,435]{0,1:T(8,128)S(1)} %bitcast.94), channel_id=1, source_target_pairs={{2,0},{4,2},{6,4},{8,6},{10,8},{12,10},{14,12},{16,14},{18,16},{20... | collective-permute-start | bytes 1336328 | tf_op jit(solution)/shard_map/ppermute | solution.py:14
  82.0 6.3 %collective-permute-start = (bf16[256,435]{0,1:T(8,128)(2,1)S(1)}, bf16[256,435]{0,1:T(8,128)(2,1)S(1)}, u32[]{:S(2)}, u32[]{:S(2)}) collective-permute-start(bf16[256,435]{0,1:T(8,128)(2,1)S(1)} %bitcast.97), channel_id=1, source_target_pairs={{0,2},{2,4},{4,6},{6,8},{8,10},{10,12},{12,14},{14,16},{16,18},{18... | collective-permute-start | bytes 668168 | tf_op jit(solution)/shard_map/ppermute | solution.py:14
  167.6 18.3 %collective-permute-start.3 = (f32[256,435]{0,1:T(8,128)S(1)}, f32[256,435]{0,1:T(8,128)S(1)}, u32[]{:S(2)}, u32[]{:S(2)}) collective-permute-start(f32[256,435]{0,1:T(8,128)S(1)} %bitcast.96), channel_id=1, source_target_pairs={{2,0},{4,2},{6,4},{8,6},{10,8},{12,10},{14,12},{16,14},{18,16},{20... | collective-permute-start | bytes 1336328 | tf_op jit(solution)/shard_map/ppermute | solution.py:14
  172.7 6.4 %collective-permute-start.2 = (bf16[256,435]{0,1:T(8,128)(2,1)S(1)}, bf16[256,435]{0,1:T(8,128)(2,1)}, u32[]{:S(2)}, u32[]{:S(2)}) collective-permute-start(bf16[256,435]{0,1:T(8,128)(2,1)S(1)} %bitcast.99), channel_id=1, source_target_pairs={{0,2},{2,4},{4,6},{6,8},{8,10},{10,12},{12,14},{14,16},{16,18},{18... | collective-permute-start | bytes 668168 | tf_op jit(solution)/shard_map/ppermute | solution.py:14
  226.4 4.0 copy-start.8
  270.9 20.5 %collective-permute-start.5 = (f32[256,435]{0,1:T(8,128)S(1)}, f32[256,435]{0,1:T(8,128)S(1)}, u32[]{:S(2)}, u32[]{:S(2)}) collective-permute-start(f32[256,435]{0,1:T(8,128)S(1)} %bitcast.95), channel_id=1, source_target_pairs={{2,0},{4,2},{6,4},{8,6},{10,8},{12,10},{14,12},{16,14},{18,16},{20... | collective-permute-start | bytes 1336328 | tf_op jit(solution)/shard_map/ppermute | solution.py:14
  276.0 8.5 %collective-permute-start.4 = (bf16[256,435]{0,1:T(8,128)(2,1)S(1)}, bf16[256,435]{0,1:T(8,128)(2,1)}, u32[]{:S(2)}, u32[]{:S(2)}) collective-permute-start(bf16[256,435]{0,1:T(8,128)(2,1)S(1)} %bitcast.98), channel_id=1, source_target_pairs={{0,2},{2,4},{4,6},{6,8},{8,10},{10,12},{12,14},{14,16},{16,18},{18... | collective-permute-start | bytes 668168 | tf_op jit(solution)/shard_map/ppermute | solution.py:14
  302.9 59.0 %copy-start.2 = (bf16[256,3584]{0,1:T(8,128)(2,1)S(1)}, bf16[256,3584]{0,1:T(8,128)(2,1)}, u32[]{:S(2)}) copy-start(bf16[256,3584]{0,1:T(8,128)(2,1)} %fusion.10) | copy-start | bytes 5505028
  302.9 154.8 %all-reduce.2.cloned.1.call-start = ((), (), s32[]{:S(2)}) async-start(), calls=%async_computation.1 | async-start | bytes 1048576 | tf_op jit(solution)/shard_map/psum | solution.py:78
  366.9 114.1 %all-gather.5.cloned.1.call-start = ((), (), s32[]{:S(2)}) async-start(), calls=%async_computation.2 | async-start | bytes 1572864 | tf_op jit(solution)/shard_map/all_gather | solution.py:79
  483.8 3.4 copy-start.3
  494.8 3.7 copy-start.11
Sparse Core Ops, SparseCore 0:
  303.0 58.8 all-gather.2
  367.0 90.6 all-reduce.1
  459.3 21.7 all-gather.4
where the time goes:
time: 518 us; the launch traced here: 508 us
  waiting for transfers between devices  171 us (33%)
  other arithmetic  153 us (30%)
  local copies, waits for them, and re-layouts  110 us (21%)
  matrix products  36.3 us (7%)
  starting transfers between devices  21 us (4%)
  between operations  17.2 us (3%)
    psum x1, waiting for transfers between devices, body(): summed_rows = lax.psum(partial_rows, 'dom')  90.6 us
    scatter-add x3, other arithmetic, operate(): assembled = jnp.zeros(field.shape, jnp.float32).at[:, connectivity.reshap...  80.1 us
    gather x6, local copies, waits for them, and re-layouts, operate(): cell_values = field[:, connectivity]  63.2 us
    all_gather x1, waiting for transfers between devices, body(): lax.all_gather(current, 'st', axis=0, tiled=True)  55.6 us
    scatter-add x6, other arithmetic, operate(): assembled.at[:, left_ids].add(from_below).at[:, right_ids].add(from_above)  51.7 us
    all_gather x1, waiting for transfers between devices, body(): gram = lax.all_gather(summed_rows, 'st', axis=0, tiled=True)  23.3 us
    ppermute x6, starting transfers between devices, passed_along(): return lax.ppermute(x, axis, pairs)  20.7 us
    mul x3, local copies, waits for them, and re-layouts, operate(): products = products * cell_scale[None, :, None]  16.1 us
  transfers between devices with their start and end apart: 9, of which 5 were waited for; matrix products, arithmetic and copies ran while one was open for 7% of the time, Pallas kernels for 0%

commit v1 on v0

v1 whole, which is shorter than its diff:
```python
import functools
import jax
import jax.numpy as jnp
from jax import lax
from jax.experimental import pallas as pl
from jax.experimental.pallas import tpu as pltpu
from jax.sharding import PartitionSpec as P

DEGREE = 3
NS_ITERS = 3
LN = 3480
LANES = 128
BATCH = 16


def passed_along(x, axis, by):
    devices = lax.axis_size(axis)
    pairs = [(i, i + by) for i in range(devices) if 0 <= i + by < devices]
    return lax.ppermute(x, axis, pairs)


def inverse_root(gram):
    frobenius = jnp.sqrt(jnp.sum(gram * gram) + 1e-06)
    iterate = gram / frobenius
    identity = jnp.eye(gram.shape[0], dtype=jnp.float32)
    inverse = identity
    for sweep in range(NS_ITERS):
        factor = 1.5 * identity - 0.5 * jnp.dot(inverse, iterate, precision=lax.Precision.HIGHEST)
        iterate = jnp.dot(iterate, factor, precision=lax.Precision.HIGHEST)
        inverse = jnp.dot(factor, inverse, precision=lax.Precision.HIGHEST)
    return (inverse / jnp.sqrt(frobenius)).astype(jnp.bfloat16)


def batches(count, body):
    whole, rest = divmod(count, BATCH)

    def step(g, carry):
        body(pl.multiple_of(g * BATCH, BATCH), BATCH)
        return carry

    lax.fori_loop(0, whole, step, 0)
    if rest:
        body(whole * BATCH, rest)


def add_faces(field, faces, wide, ids, scale):
    count = ids.shape[1]
    tiles = field.shape[1] and wide.shape[0] // count
    for side in range(2):
        wide[...] = faces[side].astype(jnp.float32) * scale

        def add(base, size):
            rows = [pl.ds(ids[side, base + i] * tiles, tiles) for i in range(size)]
            old = [field[row, :] for row in rows]
            new = [old[i] + wide[pl.ds((base + i) * tiles, tiles), :] for i in range(size)]
            for i in range(size):
                field[rows[i], :] = new[i]

        batches(count, add)


def apply_kernel(first, *refs):
    if first:
        (conn, ids, scales, coef, pot_rows, pot, stiff, start,
         out, rounded, faces, field, total, gathered, products, wide) = refs
    else:
        (conn, ids, scales, coef, pot_rows, pot, stiff, before, older, came,
         out, rounded, faces, field, total, gathered, products, wide) = refs
    cells, dofs = conn.shape
    count = ids.shape[1]
    tiles = gathered.shape[0] // dofs
    nodes = field.shape[0] // tiles
    if first:
        width = 512
        for k in range(nodes // width):
            piece = start[:, k * width:(k + 1) * width].astype(jnp.float32)
            node = lax.broadcasted_iota(jnp.int32, piece.shape, 1) + k * width
            turned = jnp.where(node < LN, piece, 0.0).T
            for j in range(tiles):
                field[pl.ds(k * width * tiles + j, width, tiles), :] = turned[:, j * LANES:(j + 1) * LANES]
    else:
        field[...] = before[...]
        add_faces(field, came, wide, ids, coef[2])
        field[...] = field[...].astype(jnp.bfloat16).astype(jnp.float32)
    rounded[...] = field[...].astype(jnp.bfloat16)
    total[...] = pot[...] * field[...]

    def gather(cell, base):
        for i in range(BATCH):
            row = conn[cell, base + i] * tiles
            gathered[pl.ds((base + i) * tiles, tiles), :] = field[pl.ds(row, tiles), :]

    def scatter(cell, base):
        rows = [pl.ds(conn[cell, base + i] * tiles, tiles) for i in range(BATCH)]
        old = [total[row, :] for row in rows]
        new = [old[i] + products[pl.ds((base + i) * tiles, tiles), :] for i in range(BATCH)]
        for i in range(BATCH):
            total[rows[i], :] = new[i]

    def one_cell(cell, carry):
        def get(g, c):
            gather(cell, pl.multiple_of(g * BATCH, BATCH))
            return c

        lax.fori_loop(0, dofs // BATCH, get, 0)
        values = jnp.concatenate(
            [gathered[pl.ds(j, dofs, tiles), :].astype(jnp.bfloat16) for j in range(tiles)], axis=1)
        result = jnp.dot(stiff[...], values, preferred_element_type=jnp.float32) * scales[cell]
        for j in range(tiles):
            products[pl.ds(j, dofs, tiles), :] = result[:, j * LANES:(j + 1) * LANES]

        def put(g, c):
            scatter(cell, pl.multiple_of(g * BATCH, BATCH))
            return c

        lax.fori_loop(0, dofs // BATCH, put, 0)
        return carry

    lax.fori_loop(0, cells, one_cell, 0)

    for side in range(2):
        def take(base, size):
            for i in range(size):
                wide[pl.ds((base + i) * tiles, tiles), :] = total[pl.ds(ids[side, base + i] * tiles, tiles), :]

        batches(count, take)
        faces[side] = wide[...].astype(faces.dtype)
    value = coef[1] * (total[...] - coef[0] * field[...])
    if not first:
        value = value - older[...].astype(jnp.float32)
    out[...] = value


def finish_kernel(ids, coef, before, came, out, field, wide):
    count = ids.shape[1]
    tiles = wide.shape[0] // count
    nodes = field.shape[0] // tiles
    field[...] = before[...]
    add_faces(field, came, wide, ids, coef[2])
    width = 512
    for k in range(nodes // width):
        piece = jnp.concatenate(
            [field[pl.ds(k * width * tiles + j, width, tiles), :] for j in range(tiles)], axis=1)
        out[:, k * width:(k + 1) * width] = piece.T.astype(jnp.bfloat16)


SMEM = pl.BlockSpec(memory_space=pltpu.SMEM)
VMEM = pl.BlockSpec(memory_space=pltpu.VMEM)


def apply_call(first, conn, ids, scales, coef, pot, stiff, *fields):
    cells, dofs = conn.shape
    count = ids.shape[1]
    rows = pot.shape[0]
    f32, bf16 = jnp.float32, jnp.bfloat16
    states = fields[0].shape[0] if first else None
    tiles = states // LANES if first else fields[2].shape[1] // count
    out_shape = (
        jax.ShapeDtypeStruct((rows, LANES), f32),
        jax.ShapeDtypeStruct((rows, LANES), bf16),
        jax.ShapeDtypeStruct((2, count * tiles, LANES), bf16),
    )
    return pl.pallas_call(
        functools.partial(apply_kernel, first),
        out_shape=out_shape,
        in_specs=[SMEM] * 4 + [SMEM] + [VMEM] * (2 + len(fields)),
        out_specs=[VMEM] * 3,
        scratch_shapes=[
            pltpu.VMEM((rows, LANES), f32),
            pltpu.VMEM((rows, LANES), f32),
            pltpu.VMEM((dofs * tiles, LANES), f32),
            pltpu.VMEM((dofs * tiles, LANES), f32),
            pltpu.VMEM((count * tiles, LANES), f32),
        ],
        compiler_params=pltpu.CompilerParams(vmem_limit_bytes=40 * 1024 * 1024),
    )(conn, ids, scales, coef, coef, pot, stiff, *fields)


def body(start_states, stiffness, cell_scale, potential, connectivity, shared_nodes, filter_bounds):
    nodes = start_states.shape[1]
    block_states = start_states.shape[0]
    tiles = pl.cdiv(block_states, LANES)
    states = tiles * LANES
    start_states = jnp.pad(start_states, ((0, states - block_states), (0, 0)))
    rows = nodes * tiles
    ids = shared_nodes[0]
    pot = jnp.broadcast_to(potential[:, None, None], (nodes, tiles, LANES)).reshape(rows, LANES)
    stiff = stiffness.T
    center = (filter_bounds[1] + filter_bounds[0]) / 2.0
    inv = 2.0 / (filter_bounds[1] - filter_bounds[0])

    def exchange(faces):
        below = passed_along(faces[1], "dom", 1)
        above = passed_along(faces[0], "dom", -1)
        return jnp.stack([below, above])

    first = jnp.stack([center, inv, inv])
    second = jnp.stack([center, 2 * inv, inv])
    later = jnp.stack([center, 2 * inv, 2 * inv])
    value, older, faces = apply_call(True, connectivity, ids, cell_scale, first, pot, stiff, start_states)
    for degree_step in range(DEGREE - 1):
        coef = second if degree_step == 0 else later
        value, newer, faces = apply_call(
            False, connectivity, ids, cell_scale, coef, pot, stiff, value, older, exchange(faces))
        older = newer
    current = pl.pallas_call(
        finish_kernel,
        out_shape=jax.ShapeDtypeStruct((states, nodes), jnp.bfloat16),
        in_specs=[SMEM, SMEM, VMEM, VMEM],
        out_specs=VMEM,
        scratch_shapes=[pltpu.VMEM((rows, LANES), jnp.float32),
                        pltpu.VMEM((ids.shape[1] * tiles, LANES), jnp.float32)],
        compiler_params=pltpu.CompilerParams(vmem_limit_bytes=40 * 1024 * 1024),
    )(ids, later, value, exchange(faces))[:block_states]
    left_ids = ids[0]
    inside = (jnp.arange(nodes) < LN).astype(jnp.bfloat16)
    keep = jnp.where(lax.axis_index("dom") > 0, 0.0, 1.0).astype(jnp.bfloat16)
    owned = inside.at[left_ids].set(keep)
    masked = current * owned[None, :]
    partial_rows = lax.dot_general(
        masked,
        lax.all_gather(current, "st", axis=0, tiled=True),
        (((1,), (1,)), ((), ())),
        preferred_element_type=jnp.float32,
    )
    summed_rows = lax.psum(partial_rows, "dom")
    gram = lax.all_gather(summed_rows, "st", axis=0, tiled=True)
    coeffs = inverse_root(gram)
    columns = lax.dynamic_slice_in_dim(coeffs, lax.axis_index("st") * block_states, block_states, 1)
    rotated = lax.dot_general(
        columns,
        lax.all_gather(current, "st", axis=0, tiled=True),
        (((0,), (0,)), ((), ())),
        preferred_element_type=jnp.float32,
    )
    return rotated.astype(jnp.bfloat16)


def solution(mesh):
    placed = (P("st", "dom"), P(), P("dom"), P("dom"), P("dom", None), P("dom", None, None), P())
    return jax.shard_map(
        body, mesh=mesh, in_specs=placed, out_specs=P("st", "dom"), check_vma=False
    )
```

time: 518 us -> 365 us (0.70); the launches traced: 508 us -> 364 us
  other arithmetic: 153 us -> 2.46 us
  Pallas kernels: 0 us -> 117 us
  local copies, waits for them, and re-layouts: 110 us -> 12.5 us
  matrix products: 36.3 us -> 21.3 us
    scatter-add x9 -> x0, other arithmetic: 132 us -> none  [the longest x3 80.1 us: operate(): assembled = jnp.zeros(field.shape, jnp.float32).at[:, connectivity.reshap...]
    pallas_call x0 -> x4, Pallas kernels: none -> 117 us  [the longest x3 112 us: apply_call(): pl.pallas_call(functools.partial(apply_kernel, first), out_shape=out_shap...]
    gather x12 -> x0, local copies, waits for them, and re-layouts: 85.7 us -> none  [the longest x6 63.2 us: operate(): cell_values = field[:, connectivity]]
    mul x3 -> x0, local copies, waits for them, and re-layouts: 16.1 us -> none  [operate(): products = products * cell_scale[None, :, None]]
    dot_general x3 -> x0, matrix products: 14.4 us -> none  [operate(): jnp.einsum('scn,nm->scm', cell_values, stiffness, preferred_element_type=...]
    mul x3 -> x0, other arithmetic: 14.4 us -> none  [operate(): assembled = assembled + potential[None, :] * field.astype(jnp.float32)]
  transfers between devices with their start and end apart: 9 -> 9, of which waited for: 5 -> 6; matrix products, arithmetic and copies ran while one was open for 7% -> 1% of each run, Pallas kernels for 0% -> 0%
where the time goes in v1:
time: 365 us; the launch traced here: 364 us
  waiting for transfers between devices  171 us (47%)
  Pallas kernels  117 us (32%)
  starting transfers between devices  23.2 us (6%)
  matrix products  21.3 us (6%)
  between operations  16.7 us (5%)
  local copies, waits for them, and re-layouts  12.5 us (3%)
    pallas_call x3, Pallas kernels, apply_call(): pl.pallas_call(functools.partial(apply_kernel, first), out_shape=out_shap...  112 us
    psum x1, waiting for transfers between devices, body(): summed_rows = lax.psum(partial_rows, 'dom')  90.8 us
    all_gather x1, waiting for transfers between devices, body(): lax.all_gather(current, 'st', axis=0, tiled=True)  54.2 us
    all_gather x1, waiting for transfers between devices, body(): gram = lax.all_gather(summed_rows, 'st', axis=0, tiled=True)  23.3 us
    ppermute x6, starting transfers between devices, passed_along(): return lax.ppermute(x, axis, pairs)  23.2 us
  transfers between devices with their start and end apart: 9, of which 6 were waited for; matrix products, arithmetic and copies ran while one was open for 1% of the time, Pallas kernels for 0%

profile of v1, /device:TPU:0, one launch (start us, length us, event | category | flops | bytes accessed | tf_op | source)
XLA Modules:
  0.0 364.4 jit_solution(15776477920791405510)
XLA Ops:
  6.5 0.0 all-gather.3.cloned.1.call-start
  6.5 1.4 fusion.10
  10.5 0.0 copy-start.7
  10.5 1.3 broadcast_in_dim.15
  11.8 1.0 broadcast_in_dim.16
  12.7 0.0 copy-done.7
  12.7 0.2 copy.9
  13.0 0.1 maximum_maximum_fusion.refs_3_.refs_4_
  13.1 0.0 copy-start.2
  13.1 0.0 copy-start.3
  13.1 0.0 copy-start.4
  13.1 0.0 copy-start.5
  13.1 1.0 broadcast_in_dim.17.refs_5_
  14.1 0.5 copy-done.2
  14.6 0.0 copy-done.3
  14.6 0.0 copy-done.4
  14.6 0.0 copy-done.5
  14.6 34.0 %shard_map.73 = (f32[7168,128]{1,0:T(8,128)S(1)}, bf16[7168,128]{1,0:T(8,128)(2,1)S(1)}, bf16[2,870,128]{2,1,0:T(8,128)(2,1)S(1)}) custom-call(s32[8,512]{1,0:T(8,128)S(1)} %copy-done.3, s32[2,435]{1,0:T(2,128)S(1)} %bitcast.40, f32[8]{0:T(128)S(1)} %copy-done.5, f32[3]{0:T(128)S(1)} %maximum_maximum_fusion.refs_3_.refs_4_, ...), custom_call_target="tpu_custom_call" | custom-call | tf_op jit(solution)/shard_map/pallas_call | solution.py:163
  48.6 0.0 copy-start.1
  48.6 1.8 copy-done.1
  50.4 1.3 collective-permute-start.1
  51.7 3.0 collective-permute-start
  54.8 0.1 pad_maximum_fusion.5.refs_3_.refs_4_
  54.9 0.0 collective-permute-done.1
  54.9 1.0 collective-permute-done
  55.9 38.5 %shard_map.74 = (f32[7168,128]{1,0:T(8,128)S(1)}, bf16[7168,128]{1,0:T(8,128)(2,1)S(1)}, bf16[2,870,128]{2,1,0:T(8,128)(2,1)S(1)}) custom-call(s32[8,512]{1,0:T(8,128)S(1)} %copy-done.3, s32[2,435]{1,0:T(2,128)S(1)} %bitcast.41, f32[8]{0:T(128)S(1)} %copy-done.5, f32[3]{0:T(128)S(1)} %pad_maximum_fusion.5.refs_3_.refs_4_, ...), custom_call_target="tpu_custom_call" | custom-call | tf_op jit(solution)/shard_map/pallas_call | solution.py:163
  94.4 0.0 copy-start
  94.4 1.8 copy-done
  96.2 1.3 collective-permute-start.3
  97.5 8.3 %collective-permute-start.2 = (bf16[870,128]{1,0:T(8,128)(2,1)S(1)}, bf16[870,128]{1,0:T(8,128)(2,1)S(1)}, u32[]{:S(2)}, u32[]{:S(2)}) collective-permute-start(bf16[870,128]{1,0:T(8,128)(2,1)S(1)} %get-tuple-element.23), channel_id=1, source_target_pairs={{0,2},{2,4},{4,6},{6,8},{8,10},{10,12},{12,14},{14,16},{16,18},{18... | collective-permute-start | bytes 668168 | tf_op jit(solution)/shard_map/ppermute | solution.py:19
  105.9 0.1 pad_maximum_fusion.3.refs_3_.refs_4_.coef
  105.9 0.0 collective-permute-done.3
  105.9 1.0 collective-permute-done.2
  107.0 39.1 %shard_map.75 = (f32[7168,128]{1,0:T(8,128)S(1)}, bf16[7168,128]{1,0:T(8,128)(2,1)}, bf16[2,870,128]{2,1,0:T(8,128)(2,1)S(1)}) custom-call(s32[8,512]{1,0:T(8,128)S(1)} %copy-done.3, s32[2,435]{1,0:T(2,128)S(1)} %bitcast.42, f32[8]{0:T(128)S(1)} %copy-done.5, f32[3]{0:T(128)S(1)} %pad_maximum_fusion.3.refs_3_.refs_4_.coef, ...), custom_call_target="tpu_custom_call" | custom-call | tf_op jit(solution)/shard_map/pallas_call | solution.py:163
  146.1 1.3 collective-permute-start.5
  147.4 7.9 %collective-permute-start.4 = (bf16[870,128]{1,0:T(8,128)(2,1)S(1)}, bf16[870,128]{1,0:T(8,128)(2,1)S(1)}, u32[]{:S(2)}, u32[]{:S(2)}) collective-permute-start(bf16[870,128]{1,0:T(8,128)(2,1)S(1)} %get-tuple-element.21), channel_id=1, source_target_pairs={{0,2},{2,4},{4,6},{6,8},{8,10},{10,12},{12,14},{14,16},{16,18},{18... | collective-permute-start | bytes 668168 | tf_op jit(solution)/shard_map/ppermute | solution.py:19
  155.3 0.0 collective-permute-done.5
  155.3 0.9 collective-permute-done.4
  156.2 5.3 %shard_map.76 = bf16[256,3584]{1,0:T(8,128)(2,1)} custom-call(s32[2,435]{1,0:T(2,128)S(1)} %bitcast.43, f32[3]{0:T(128)S(1)} %pad_maximum_fusion.3.refs_3_.refs_4_.coef, f32[7168,128]{1,0:T(8,128)S(1)} %get-tuple-element.19.before, bf16[2,870,128]{2,1,0:T(8,128)(2,1)S(1)} %pad_maximum_fusion.2.came), custom_call_target="tpu_custom_call" | custom-call | tf_op jit(solution)/shard_map/pallas_call | solution.py:206
  161.5 0.0 all-gather.3.cloned.1.call-update
  161.6 0.0 all-reduce.2.cloned.1.call-start
  161.7 3.3 scatter_fusion
  165.0 54.2 %all-gather.3.cloned.1.call-done = bf16[512,3584]{1,0:T(8,128)(2,1)} async-done(((bf16[256,3584]{1,0:T(8,128)(2,1)}), bf16[512,3584]{1,0:T(8,128)(2,1)}) %all-gather.3.cloned.1.call-update) | async-done | bytes 3670032 | tf_op jit(solution)/shard_map/all_gather | solution.py:222
  219.2 4.5 %fusion = f32[256,512]{1,0:T(8,128)} fusion(bf16[512,3584]{1,0:T(8,128)(2,1)} %all-gather.3.cloned.1.call-done, bf16[256,3584]{1,0:T(8,128)(2,1)} %shard_map.76, bf16[3584]{0:T(1024)(128)(2,1)S(1)} %scatter_fusion), kind=kOutput, calls=%fused_computation.2 | convolution fusion | flops 940441600 | bytes 6036480 | tf_op jit(solution)/shard_map/dot_general | solution.py:220
  223.7 0.0 all-reduce.2.cloned.1.call-update
  223.8 0.0 all-gather.5.cloned.1.call-start
  223.8 90.8 %all-reduce.2.cloned.1.call-done = f32[256,512]{1,0:T(8,128)} async-done(((f32[256,512]{1,0:T(8,128)}), f32[256,512]{1,0:T(8,128)}) %all-reduce.2.cloned.1.call-update) | async-done | bytes 524304 | tf_op jit(solution)/shard_map/psum | solution.py:226
  314.6 0.0 all-gather.5.cloned.1.call-update
  314.6 23.3 %all-gather.5.cloned.1.call-done = f32[512,512]{1,0:T(8,128)} async-done(((f32[256,512]{1,0:T(8,128)}), f32[512,512]{1,0:T(8,128)}) %all-gather.5.cloned.1.call-update) | async-done | bytes 1048592 | tf_op jit(solution)/shard_map/all_gather | solution.py:227
  337.9 2.1 multiply_reduce_fusion
  340.7 2.3 select_subtract_fusion.2
  343.1 0.0 copy-start.6
  343.1 1.0 fusion.2
  344.0 0.2 copy-done.6
  344.3 1.9 fusion.5
  346.2 1.8 select_subtract_fusion.1
  348.0 1.8 fusion.11
  349.9 1.8 fusion.12
  351.8 0.0 copy-start.8
  351.8 1.9 select_subtract_fusion
  353.6 1.9 fusion.13
  355.5 0.0 copy-done.8
  355.5 2.4 convolution_convert_fusion
  (9 shorter events, 0.2 us)
Async XLA Ops:
  6.5 212.7 %all-gather.3.cloned.1.call-start = ((), (), s32[]{:S(2)}) async-start(), calls=%async_computation | async-start | bytes 5505024 | tf_op jit(solution)/shard_map/all_gather | solution.py:222
  10.5 2.3 copy-start.7
  13.1 1.5 copy-start.2
  13.1 1.5 copy-start.3
  13.1 1.5 copy-start.4
  13.1 1.5 copy-start.5
  48.6 1.8 copy-start.1
  50.4 4.4 %collective-permute-start.1 = (bf16[870,128]{1,0:T(8,128)(2,1)S(1)}, bf16[870,128]{1,0:T(8,128)(2,1)S(1)}, u32[]{:S(2)}, u32[]{:S(2)}) collective-permute-start(bf16[870,128]{1,0:T(8,128)(2,1)S(1)} %get-tuple-element.26), channel_id=1, source_target_pairs={{2,0},{4,2},{6,4},{8,6},{10,8},{12,10},{14,12},{16,14},{18,16},{20... | collective-permute-start | bytes 668168 | tf_op jit(solution)/shard_map/ppermute | solution.py:19
  51.7 4.1 %collective-permute-start = (bf16[870,128]{1,0:T(8,128)(2,1)S(1)}, bf16[870,128]{1,0:T(8,128)(2,1)S(1)}, u32[]{:S(2)}, u32[]{:S(2)}) collective-permute-start(bf16[870,128]{1,0:T(8,128)(2,1)S(1)} %get-tuple-element.25), channel_id=1, source_target_pairs={{0,2},{2,4},{4,6},{6,8},{8,10},{10,12},{12,14},{14,16},{16,18},{18... | collective-permute-start | bytes 668168 | tf_op jit(solution)/shard_map/ppermute | solution.py:19
  94.4 1.8 copy-start
  96.2 9.7 %collective-permute-start.3 = (bf16[870,128]{1,0:T(8,128)(2,1)S(1)}, bf16[870,128]{1,0:T(8,128)(2,1)S(1)}, u32[]{:S(2)}, u32[]{:S(2)}) collective-permute-start(bf16[870,128]{1,0:T(8,128)(2,1)S(1)} %get-tuple-element.24), channel_id=1, source_target_pairs={{2,0},{4,2},{6,4},{8,6},{10,8},{12,10},{14,12},{16,14},{18,16},{20... | collective-permute-start | bytes 668168 | tf_op jit(solution)/shard_map/ppermute | solution.py:19
  97.5 9.4 %collective-permute-start.2 = (bf16[870,128]{1,0:T(8,128)(2,1)S(1)}, bf16[870,128]{1,0:T(8,128)(2,1)S(1)}, u32[]{:S(2)}, u32[]{:S(2)}) collective-permute-start(bf16[870,128]{1,0:T(8,128)(2,1)S(1)} %get-tuple-element.23), channel_id=1, source_target_pairs={{0,2},{2,4},{4,6},{6,8},{8,10},{10,12},{12,14},{14,16},{16,18},{18... | collective-permute-start | bytes 668168 | tf_op jit(solution)/shard_map/ppermute | solution.py:19
  146.1 9.2 %collective-permute-start.5 = (bf16[870,128]{1,0:T(8,128)(2,1)S(1)}, bf16[870,128]{1,0:T(8,128)(2,1)S(1)}, u32[]{:S(2)}, u32[]{:S(2)}) collective-permute-start(bf16[870,128]{1,0:T(8,128)(2,1)S(1)} %get-tuple-element.22), channel_id=1, source_target_pairs={{2,0},{4,2},{6,4},{8,6},{10,8},{12,10},{14,12},{16,14},{18,16},{20... | collective-permute-start | bytes 668168 | tf_op jit(solution)/shard_map/ppermute | solution.py:19
  147.4 8.8 %collective-permute-start.4 = (bf16[870,128]{1,0:T(8,128)(2,1)S(1)}, bf16[870,128]{1,0:T(8,128)(2,1)S(1)}, u32[]{:S(2)}, u32[]{:S(2)}) collective-permute-start(bf16[870,128]{1,0:T(8,128)(2,1)S(1)} %get-tuple-element.21), channel_id=1, source_target_pairs={{0,2},{2,4},{4,6},{6,8},{8,10},{10,12},{12,14},{14,16},{16,18},{18... | collective-permute-start | bytes 668168 | tf_op jit(solution)/shard_map/ppermute | solution.py:19
  161.6 153.1 %all-reduce.2.cloned.1.call-start = ((), (), s32[]{:S(2)}) async-start(), calls=%async_computation.1 | async-start | bytes 1048576 | tf_op jit(solution)/shard_map/psum | solution.py:226
  223.8 114.2 %all-gather.5.cloned.1.call-start = ((), (), s32[]{:S(2)}) async-start(), calls=%async_computation.2 | async-start | bytes 1572864 | tf_op jit(solution)/shard_map/all_gather | solution.py:227
  343.1 1.2 copy-start.6
  351.8 3.7 %copy-start.8 = (bf16[512,3584]{1,0:T(8,128)(2,1)S(1)}, bf16[512,3584]{1,0:T(8,128)(2,1)}, u32[]{:S(2)}) copy-start(bf16[512,3584]{1,0:T(8,128)(2,1)} %all-gather.3.cloned.1.call-done) | copy-start | bytes 11010052
Sparse Core Ops, SparseCore 0:
  161.7 57.4 all-gather.2
  223.9 90.6 all-reduce.1
  316.2 21.7 all-gather.4

commit v2 on v1

--- a/solution.py
+++ b/solution.py
@@ -44,13 +44,13 @@
 
 
 def add_faces(field, faces, wide, ids, scale):
-    count = ids.shape[1]
-    tiles = field.shape[1] and wide.shape[0] // count
+    count = ids.shape[0] // 2
+    tiles = wide.shape[0] // count
     for side in range(2):
         wide[...] = faces[side].astype(jnp.float32) * scale
 
         def add(base, size):
-            rows = [pl.ds(ids[side, base + i] * tiles, tiles) for i in range(size)]
+            rows = [pl.ds(ids[side * count + base + i], tiles) for i in range(size)]
             old = [field[row, :] for row in rows]
             new = [old[i] + wide[pl.ds((base + i) * tiles, tiles), :] for i in range(size)]
             for i in range(size):
@@ -61,13 +61,14 @@
 
 def apply_kernel(first, *refs):
     if first:
-        (conn, ids, scales, coef, pot_rows, pot, stiff, start,
+        (conn, ids, scales, coef, pot, stiff, start,
          out, rounded, faces, field, total, gathered, products, wide) = refs
     else:
-        (conn, ids, scales, coef, pot_rows, pot, stiff, before, older, came,
+        (conn, ids, scales, coef, pot, stiff, before, older, came,
          out, rounded, faces, field, total, gathered, products, wide) = refs
-    cells, dofs = conn.shape
-    count = ids.shape[1]
+    dofs = stiff.shape[0]
+    cells = conn.shape[0] // dofs
+    count = ids.shape[0] // 2
     tiles = gathered.shape[0] // dofs
     nodes = field.shape[0] // tiles
     if first:
@@ -87,11 +88,11 @@
 
     def gather(cell, base):
         for i in range(BATCH):
-            row = conn[cell, base + i] * tiles
+            row = conn[cell * dofs + base + i]
             gathered[pl.ds((base + i) * tiles, tiles), :] = field[pl.ds(row, tiles), :]
 
     def scatter(cell, base):
-        rows = [pl.ds(conn[cell, base + i] * tiles, tiles) for i in range(BATCH)]
+        rows = [pl.ds(conn[cell * dofs + base + i], tiles) for i in range(BATCH)]
         old = [total[row, :] for row in rows]
         new = [old[i] + products[pl.ds((base + i) * tiles, tiles), :] for i in range(BATCH)]
         for i in range(BATCH):
@@ -121,7 +122,7 @@
     for side in range(2):
         def take(base, size):
             for i in range(size):
-                wide[pl.ds((base + i) * tiles, tiles), :] = total[pl.ds(ids[side, base + i] * tiles, tiles), :]
+                wide[pl.ds((base + i) * tiles, tiles), :] = total[pl.ds(ids[side * count + base + i], tiles), :]
 
         batches(count, take)
         faces[side] = wide[...].astype(faces.dtype)
@@ -131,10 +132,11 @@
     out[...] = value
 
 
-def finish_kernel(ids, coef, before, came, out, field, wide):
-    count = ids.shape[1]
+def finish_kernel(ids, coef, part, before, came, owned, out, own_half, other_half, gram, field, wide):
+    count = ids.shape[0] // 2
     tiles = wide.shape[0] // count
-    nodes = field.shape[0] // tiles
+    states, nodes = out.shape
+    half = nodes // 2
     field[...] = before[...]
     add_faces(field, came, wide, ids, coef[2])
     width = 512
@@ -142,19 +144,100 @@
         piece = jnp.concatenate(
             [field[pl.ds(k * width * tiles + j, width, tiles), :] for j in range(tiles)], axis=1)
         out[:, k * width:(k + 1) * width] = piece.T.astype(jnp.bfloat16)
+    start = pl.multiple_of(part[0] * half, LANES)
+    away = pl.multiple_of((1 - part[0]) * half, LANES)
+    own_half[...] = out[:, pl.ds(start, half)]
+    other_half[...] = out[:, pl.ds(away, half)]
+    gram[...] = lax.dot_general(
+        out[...] * owned[...], out[...], (((1,), (1,)), ((), ())), preferred_element_type=jnp.float32)
+
+
+def cross_kernel(part, mine, came, owned, out):
+    half = mine.shape[1]
+    start = pl.multiple_of(part[0] * half, LANES)
+    masked = mine[...] * owned[:, pl.ds(start, half)]
+    dims = (((1,), (1,)), ((), ()))
+
+    @pl.when(part[0] == 0)
+    def _():
+        out[...] = lax.dot_general(masked, came[...], dims, preferred_element_type=jnp.float32)
+
+    @pl.when(part[0] != 0)
+    def _():
+        out[...] = lax.dot_general(came[...], masked, dims, preferred_element_type=jnp.float32)
+
+
+def split(x):
+    high = x.astype(jnp.bfloat16)
+    return high, (x - high.astype(jnp.float32)).astype(jnp.bfloat16)
+
+
+def product(a, b):
+    def dot(x, y):
+        return jnp.dot(x, y, preferred_element_type=jnp.float32)
+
+    return dot(a[0], b[0]) + (dot(a[0], b[1]) + dot(a[1], b[0]))
+
+
+def root_kernel(part, blocks, out, gram, held):
+    size = blocks.shape[1]
+    cross = blocks[2]
+    gram[:size, :size] = blocks[0]
+    gram[size:, size:] = blocks[1]
+    gram[:size, size:] = cross
+    gram[size:, :size] = cross.T
+    whole = gram[...]
+    scale = jnp.sqrt(jnp.sum(whole * whole, keepdims=True) + 1e-06)
+    start = pl.multiple_of(part[0] * size, LANES)
+    row = lax.broadcasted_iota(jnp.int32, whole.shape, 0)
+    column = lax.broadcasted_iota(jnp.int32, whole.shape, 1)
+    diagonal = jnp.where(row == column, 1.5, 0.0)
+    iterate = split(whole / scale)
+    factor = diagonal - 0.5 * (whole / scale)
+    inverse = split(factor)
+    for sweep in range(1, NS_ITERS):
+        iterate = split(product(iterate, split(factor)))
+        factor = diagonal - 0.5 * product(inverse, iterate)
+        if sweep == NS_ITERS - 1:
+            held[0] = inverse[0]
+            held[1] = inverse[1]
+            columns = held[0, :, pl.ds(start, size)], held[1, :, pl.ds(start, size)]
+            result = product(split(factor), columns)
+        else:
+            inverse = split(product(split(factor), inverse))
+    out[...] = (result / jnp.sqrt(scale)).astype(jnp.bfloat16)
+
+
+def rotate_kernel(part, columns, mine, first, rest_a, rest_b, out):
+    states, nodes = out.shape
+    half = nodes // 2
+    dims = (((0,), (0,)), ((), ()))
+    own = columns[pl.ds(pl.multiple_of(part[0] * states, states), states), :]
+    other = columns[pl.ds(pl.multiple_of((1 - part[0]) * states, states), states), :]
+
+    def part_of(base, came):
+        width = came.shape[1]
+        value = lax.dot_general(own, mine[:, pl.ds(base, width)], dims, preferred_element_type=jnp.float32)
+        value += lax.dot_general(other, came[...], dims, preferred_element_type=jnp.float32)
+        out[:, pl.ds(base, width)] = value.astype(out.dtype)
+
+    part_of(pl.multiple_of(part[0] * half, LANES), first)
+    away = (1 - part[0]) * half
+    part_of(pl.multiple_of(away, LANES), rest_a)
+    part_of(pl.multiple_of(away + rest_a.shape[1], LANES), rest_b)
 
 
 SMEM = pl.BlockSpec(memory_space=pltpu.SMEM)
 VMEM = pl.BlockSpec(memory_space=pltpu.VMEM)
+LIMIT = pltpu.CompilerParams(vmem_limit_bytes=40 * 1024 * 1024)
 
 
 def apply_call(first, conn, ids, scales, coef, pot, stiff, *fields):
-    cells, dofs = conn.shape
-    count = ids.shape[1]
+    dofs = stiff.shape[0]
+    count = ids.shape[0] // 2
     rows = pot.shape[0]
     f32, bf16 = jnp.float32, jnp.bfloat16
-    states = fields[0].shape[0] if first else None
-    tiles = states // LANES if first else fields[2].shape[1] // count
+    tiles = fields[0].shape[0] // LANES if first else fields[2].shape[1] // count
     out_shape = (
         jax.ShapeDtypeStruct((rows, LANES), f32),
         jax.ShapeDtypeStruct((rows, LANES), bf16),
@@ -163,7 +246,7 @@
     return pl.pallas_call(
         functools.partial(apply_kernel, first),
         out_shape=out_shape,
-        in_specs=[SMEM] * 4 + [SMEM] + [VMEM] * (2 + len(fields)),
+        in_specs=[SMEM] * 4 + [VMEM] * (2 + len(fields)),
         out_specs=[VMEM] * 3,
         scratch_shapes=[
             pltpu.VMEM((rows, LANES), f32),
@@ -172,22 +255,122 @@
             pltpu.VMEM((dofs * tiles, LANES), f32),
             pltpu.VMEM((count * tiles, LANES), f32),
         ],
-        compiler_params=pltpu.CompilerParams(vmem_limit_bytes=40 * 1024 * 1024),
-    )(conn, ids, scales, coef, coef, pot, stiff, *fields)
+        compiler_params=LIMIT,
+        name="apply",
+    )(conn, ids, scales, coef, pot, stiff, *fields)
+
+
+def groups_of(devices):
+    bits = devices.bit_length() - 1
+    return [list(range(b, min(b + 2, bits))) if b else [0] for b in [0] + list(range(1, bits, 2))][:bits]
+
+
+def plan(group):
+    for m in range(1, 1 << len(group)):
+        yield m, sum(((m >> i) & 1) << bit for i, bit in enumerate(group))
+
+
+def code_of(group):
+    at = lax.axis_index("dom")
+    return sum(((at >> bit) & 1) << i for i, bit in enumerate(group))
+
+
+def sum_scatter(x):
+    devices = lax.axis_size("dom")
+    for group in groups_of(devices):
+        size = x.shape[-2] >> len(group)
+        code = code_of(group)
+        came = [
+            lax.ppermute(
+                lax.dynamic_slice_in_dim(x, (code ^ m) * size, size, x.ndim - 2),
+                "dom", [(i, i ^ mask) for i in range(devices)])
+            for m, mask in plan(group)
+        ]
+        x = lax.dynamic_slice_in_dim(x, code * size, size, x.ndim - 2)
+        for y in came:
+            x = x + y
+    return x
+
+
+def gather_all(x):
+    devices = lax.axis_size("dom")
+    for group in reversed(groups_of(devices)):
+        size = x.shape[-2]
+        code = code_of(group)
+        pieces = [(0, x)] + [
+            (m, lax.ppermute(x, "dom", [(i, i ^ mask) for i in range(devices)])) for m, mask in plan(group)
+        ]
+        x = jnp.zeros(x.shape[:-2] + (size << len(group), x.shape[-1]), x.dtype)
+        for m, piece in pieces:
+            x = lax.dynamic_update_slice_in_dim(x, piece, (code ^ m) * size, x.ndim - 2)
+    return x
+
+
+def rotate_pair(current, own_half, other_half, gram, owned, part):
+    states, nodes = current.shape
+    f32, bf16 = jnp.float32, jnp.bfloat16
+    swap = [(0, 1), (1, 0)]
+    came = lax.ppermute(other_half, "st", swap)
+    own_sum = sum_scatter(gram)
+    cross = pl.pallas_call(
+        cross_kernel,
+        out_shape=jax.ShapeDtypeStruct((states, states), f32),
+        in_specs=[SMEM, VMEM, VMEM, VMEM], out_specs=VMEM, compiler_params=LIMIT, name="cross",
+    )(part, own_half, came, owned)
+    quarter = nodes // 4 // LANES * LANES
+    rest, cross = lax.optimization_barrier((own_half, cross))
+    rest_a = lax.ppermute(rest[:, :quarter], "st", swap)
+    cross_sum = sum_scatter(cross)
+    rest_a, cross_sum = lax.optimization_barrier((rest_a, cross_sum))
+    pair = jnp.stack([own_sum, cross_sum])
+    theirs = lax.ppermute(pair, "st", swap)
+    later, theirs = lax.optimization_barrier((rest[:, quarter:], theirs))
+    rest_b = lax.ppermute(later, "st", swap)
+    lower = part[0] == 0
+    blocks = gather_all(jnp.stack([
+        jnp.where(lower, pair[0], theirs[0]), jnp.where(lower, theirs[0], pair[0]), pair[1] + theirs[1]]))
+    columns = pl.pallas_call(
+        root_kernel,
+        out_shape=jax.ShapeDtypeStruct((2 * states, states), bf16),
+        in_specs=[SMEM, VMEM], out_specs=VMEM,
+        scratch_shapes=[pltpu.VMEM((2 * states, 2 * states), f32), pltpu.VMEM((2, 2 * states, 2 * states), bf16)],
+        compiler_params=LIMIT, name="root",
+    )(part, blocks)
+    return pl.pallas_call(
+        rotate_kernel,
+        out_shape=jax.ShapeDtypeStruct((states, nodes), bf16),
+        in_specs=[SMEM] + [VMEM] * 5, out_specs=VMEM, compiler_params=LIMIT, name="rotate",
+    )(part, columns, current, came, rest_a, rest_b)
+
+
+def rotate_any(current, owned):
+    states = current.shape[0]
+    whole = lax.all_gather(current, "st", axis=0, tiled=True)
+    rows = lax.dot_general(
+        current * owned, whole, (((1,), (1,)), ((), ())), preferred_element_type=jnp.float32)
+    gram = lax.all_gather(lax.psum(rows, "dom"), "st", axis=0, tiled=True)
+    columns = lax.dynamic_slice_in_dim(inverse_root(gram), lax.axis_index("st") * states, states, 1)
+    rotated = lax.dot_general(
+        columns, whole, (((0,), (0,)), ((), ())), preferred_element_type=jnp.float32)
+    return rotated.astype(jnp.bfloat16)
 
 
 def body(start_states, stiffness, cell_scale, potential, connectivity, shared_nodes, filter_bounds):
-    nodes = start_states.shape[1]
-    block_states = start_states.shape[0]
+    block_states, nodes = start_states.shape
     tiles = pl.cdiv(block_states, LANES)
     states = tiles * LANES
     start_states = jnp.pad(start_states, ((0, states - block_states), (0, 0)))
     rows = nodes * tiles
-    ids = shared_nodes[0]
+    conn = connectivity.reshape(-1) * tiles
+    ids = shared_nodes.reshape(-1) * tiles
     pot = jnp.broadcast_to(potential[:, None, None], (nodes, tiles, LANES)).reshape(rows, LANES)
     stiff = stiffness.T
     center = (filter_bounds[1] + filter_bounds[0]) / 2.0
     inv = 2.0 / (filter_bounds[1] - filter_bounds[0])
+    part = lax.axis_index("st").reshape(1)
+    inside = (jnp.arange(nodes) < LN).astype(jnp.bfloat16)
+    keep = jnp.where(lax.axis_index("dom") > 0, 0.0, 1.0).astype(jnp.bfloat16)
+    owned = inside.at[shared_nodes[0, 0]].set(keep)[None, :]
 
     def exchange(faces):
         below = passed_along(faces[1], "dom", 1)
@@ -197,43 +380,28 @@
     first = jnp.stack([center, inv, inv])
     second = jnp.stack([center, 2 * inv, inv])
     later = jnp.stack([center, 2 * inv, 2 * inv])
-    value, older, faces = apply_call(True, connectivity, ids, cell_scale, first, pot, stiff, start_states)
+    value, older, faces = apply_call(True, conn, ids, cell_scale, first, pot, stiff, start_states)
     for degree_step in range(DEGREE - 1):
         coef = second if degree_step == 0 else later
         value, newer, faces = apply_call(
-            False, connectivity, ids, cell_scale, coef, pot, stiff, value, older, exchange(faces))
+            False, conn, ids, cell_scale, coef, pot, stiff, value, older, exchange(faces))
         older = newer
-    current = pl.pallas_call(
+    half = jax.ShapeDtypeStruct((states, nodes // 2), jnp.bfloat16)
+    current, own_half, other_half, gram = pl.pallas_call(
         finish_kernel,
-        out_shape=jax.ShapeDtypeStruct((states, nodes), jnp.bfloat16),
-        in_specs=[SMEM, SMEM, VMEM, VMEM],
-        out_specs=VMEM,
+        out_shape=(jax.ShapeDtypeStruct((states, nodes), jnp.bfloat16), half, half,
+                   jax.ShapeDtypeStruct((states, states), jnp.float32)),
+        in_specs=[SMEM] * 3 + [VMEM] * 3,
+        out_specs=[VMEM] * 4,
         scratch_shapes=[pltpu.VMEM((rows, LANES), jnp.float32),
-                        pltpu.VMEM((ids.shape[1] * tiles, LANES), jnp.float32)],
-        compiler_params=pltpu.CompilerParams(vmem_limit_bytes=40 * 1024 * 1024),
-    )(ids, later, value, exchange(faces))[:block_states]
-    left_ids = ids[0]
-    inside = (jnp.arange(nodes) < LN).astype(jnp.bfloat16)
-    keep = jnp.where(lax.axis_index("dom") > 0, 0.0, 1.0).astype(jnp.bfloat16)
-    owned = inside.at[left_ids].set(keep)
-    masked = current * owned[None, :]
-    partial_rows = lax.dot_general(
-        masked,
-        lax.all_gather(current, "st", axis=0, tiled=True),
-        (((1,), (1,)), ((), ())),
-        preferred_element_type=jnp.float32,
-    )
-    summed_rows = lax.psum(partial_rows, "dom")
-    gram = lax.all_gather(summed_rows, "st", axis=0, tiled=True)
-    coeffs = inverse_root(gram)
-    columns = lax.dynamic_slice_in_dim(coeffs, lax.axis_index("st") * block_states, block_states, 1)
-    rotated = lax.dot_general(
-        columns,
-        lax.all_gather(current, "st", axis=0, tiled=True),
-        (((0,), (0,)), ((), ())),
-        preferred_element_type=jnp.float32,
-    )
-    return rotated.astype(jnp.bfloat16)
+                        pltpu.VMEM((ids.shape[0] // 2 * tiles, LANES), jnp.float32)],
+        compiler_params=LIMIT,
+        name="finish",
+    )(ids, later, part, value, exchange(faces), owned)
+    devices = lax.axis_size("dom")
+    if lax.axis_size("st") == 2 and states == block_states and devices & (devices - 1) == 0:
+        return rotate_pair(current, own_half, other_half, gram, owned, part)
+    return rotate_any(current[:block_states], owned)
 
 
 def solution(mesh):

time: 365 us -> 190 us (0.52)
  waiting for transfers between devices: 171 us -> 42.6 us
  Pallas kernels: 117 us -> 73 us
  starting transfers between devices: 23.2 us -> 49.5 us
  matrix products: 21.3 us -> 0 us
  between operations: 16.7 us -> 3.1 us
  local copies, waits for them, and re-layouts: 12.5 us -> 20 us
    psum x1 -> x0, waiting for transfers between devices: 90.8 us -> none  [body(): summed_rows = lax.psum(partial_rows, 'dom')]
    all_gather x2 -> x0, waiting for transfers between devices: 77.5 us -> none  [the longest x1 54.2 us: body(): lax.all_gather(current, 'st', axis=0, tiled=True)]
    pallas_call x3, Pallas kernels: 112 us -> 60.7 us  [apply_call(): pl.pallas_call(functools.partial(apply_kernel, first), out_shape=out_shap...]
    ppermute x0 -> x19, waiting for transfers between devices: none -> 36.5 us  [the longest x1 11.1 us: rotate_pair(): came = lax.ppermute(other_half, 'st', swap)]
    ppermute x0 -> x19, starting transfers between devices: none -> 30.4 us  [the longest x10 19.5 us: sum_scatter(): lax.ppermute(lax.dynamic_slice_in_dim(x, (code ^ m) * size, size, x.ndim...]
    dot_general x10 -> x0, matrix products: 21.3 us -> none  [the longest x3 6.02 us: inverse_root(): jnp.dot(inverse, iterate, precision=lax.Precision.HIGHEST)]
    pallas_call x1 -> x4, Pallas kernels: 5.31 us -> 12.4 us  [the longest x1 5.91 us: rotate_pair(): pl.pallas_call(root_kernel, out_shape=jax.ShapeDtypeStruct((2 * states, s...]
    unnamed x19 -> x28, local copies, waits for them, and re-layouts: 4.52 us -> 11.4 us
  transfers between devices with their start and end apart: 9 -> 25, of which waited for: 6 -> 14; matrix products, arithmetic and copies ran while one was open for 1% -> 2% of each run, Pallas kernels for 0% -> 3%
where the time goes in v2:
time: 190 us; the launch traced here: 189 us
  Pallas kernels  73 us (38%)
  starting transfers between devices  49.5 us (26%)
  waiting for transfers between devices  42.6 us (22%)
  local copies, waits for them, and re-layouts  20 us (11%)
  between operations  3.1 us (2%)
    pallas_call x3, Pallas kernels, apply_call(): pl.pallas_call(functools.partial(apply_kernel, first), out_shape=out_shap...  60.7 us
    ppermute x10, starting transfers between devices, sum_scatter(): lax.ppermute(lax.dynamic_slice_in_dim(x, (code ^ m) * size, size, x.ndim...  19.5 us
    ppermute x6, starting transfers between devices, passed_along(): return lax.ppermute(x, axis, pairs)  19.2 us
    unnamed x28, local copies, waits for them, and re-layouts  11.4 us
    ppermute x1, waiting for transfers between devices, rotate_pair(): came = lax.ppermute(other_half, 'st', swap)  11.1 us
    ppermute x5, waiting for transfers between devices, gather_all(): lax.ppermute(x, 'dom', [(i, i ^ mask) for i in range(devices)])  7.71 us
    ppermute x6, waiting for transfers between devices, passed_along(): return lax.ppermute(x, axis, pairs)  6.1 us
    pallas_call x1, Pallas kernels, rotate_pair(): pl.pallas_call(root_kernel, out_shape=jax.ShapeDtypeStruct((2 * states, s...  5.91 us
  transfers between devices with their start and end apart: 25, of which 14 were waited for; matrix products, arithmetic and copies ran while one was open for 2% of the time, Pallas kernels for 3%

profile of v2, /device:TPU:0, one launch (start us, length us, event | category | flops | bytes accessed | tf_op | source)
XLA Modules:
  0.0 189.4 jit_solution(14813219771587685962)
XLA Ops:
  0.0 1.3 fusion.5
  3.9 0.7 broadcast_multiply_fusion
  4.6 0.1 mul.64.refs_1_.ids
  4.7 1.3 broadcast_in_dim.29
  6.0 0.9 broadcast_in_dim.30
  7.0 0.2 copy.9
  7.3 0.1 maximum_maximum_fusion.refs_3_
  7.3 1.0 broadcast_in_dim.31.refs_4_
  8.4 0.5 copy-done.6
  8.8 17.8 %apply.3 = (f32[7168,128]{1,0:T(8,128)S(1)}, bf16[7168,128]{1,0:T(8,128)(2,1)S(1)}, bf16[2,870,128]{2,1,0:T(8,128)(2,1)S(1)}) custom-call(s32[4096]{0:T(1024)S(1)} %bitcast.48, s32[870]{0:T(1024)S(1)} %mul.64.refs_1_.ids, f32[8]{0:T(128)S(1)} %copy-done.9, f32[3]{0:T(128)S(1)} %maximum_maximum_fusion.refs_3_, f32[7168,128]{1,0:T(8,128)S(1)} %broadcast_in_dim.31.refs_4_, ...), custom_call_target="tpu_custom_call" | custom-call | tf_op jit(solution)/shard_map/apply/pallas_call | solution.py:246
  26.7 1.8 copy-done.4
  28.5 2.4 %collective-permute-start = (bf16[870,128]{1,0:T(8,128)(2,1)S(1)}, bf16[870,128]{1,0:T(8,128)(2,1)S(1)}, u32[]{:S(2)}, u32[]{:S(2)}) collective-permute-start(bf16[870,128]{1,0:T(8,128)(2,1)S(1)} %get-tuple-element.47), channel_id=1, source_target_pairs={{0,2},{2,4},{4,6},{6,8},{8,10},{10,12},{12,14},{14,16},{16,18},{18... | collective-permute-start | bytes 668168 | tf_op jit(solution)/shard_map/ppermute | solution.py:19
  30.9 1.3 collective-permute-start.1
  32.2 0.1 pad_maximum_fusion.7.refs_3_
  32.3 4.1 %collective-permute-done.1 = bf16[870,128]{1,0:T(8,128)(2,1)S(1)} collective-permute-done((bf16[870,128]{1,0:T(8,128)(2,1)S(1)}, bf16[870,128]{1,0:T(8,128)(2,1)S(1)}, u32[]{:S(2)}, u32[]{:S(2)}) %collective-permute-start.1) | collective-permute-done | bytes 222752 | tf_op jit(solution)/shard_map/ppermute | solution.py:19
  36.4 2.0 %copy-done.1 = f32[7168,128]{1,0:T(8,128)S(1)} copy-done((f32[7168,128]{1,0:T(8,128)S(1)}, f32[7168,128]{1,0:T(8,128)}, u32[]{:S(2)}) %copy-start.1) | copy-done | bytes 3670040
  38.4 21.1 %apply.4 = (f32[7168,128]{1,0:T(8,128)S(1)}, bf16[7168,128]{1,0:T(8,128)(2,1)S(1)}, bf16[2,870,128]{2,1,0:T(8,128)(2,1)S(1)}) custom-call(s32[4096]{0:T(1024)S(1)} %bitcast.49, s32[870]{0:T(1024)S(1)} %mul.64.refs_1_.ids, f32[8]{0:T(128)S(1)} %copy-done.9, f32[3]{0:T(128)S(1)} %pad_maximum_fusion.7.refs_3_, f32[7168,128]{1,0:T(8,128)S(1)} %copy-done.1, ...), custom_call_target="tpu_custom_call" | custom-call | tf_op jit(solution)/shard_map/apply/pallas_call | solution.py:246
  59.6 1.8 copy-done.5
  61.4 6.3 %collective-permute-start.2 = (bf16[870,128]{1,0:T(8,128)(2,1)S(1)}, bf16[870,128]{1,0:T(8,128)(2,1)S(1)}, u32[]{:S(2)}, u32[]{:S(2)}) collective-permute-start(bf16[870,128]{1,0:T(8,128)(2,1)S(1)} %get-tuple-element.45), channel_id=1, source_target_pairs={{0,2},{2,4},{4,6},{6,8},{8,10},{10,12},{12,14},{14,16},{16,18},{18... | collective-permute-start | bytes 668168 | tf_op jit(solution)/shard_map/ppermute | solution.py:19
  67.7 1.3 collective-permute-start.3
  69.0 0.1 pad_maximum_fusion.5.refs_3_.coef
  69.1 2.0 %collective-permute-done.3 = bf16[870,128]{1,0:T(8,128)(2,1)S(1)} collective-permute-done((bf16[870,128]{1,0:T(8,128)(2,1)S(1)}, bf16[870,128]{1,0:T(8,128)(2,1)S(1)}, u32[]{:S(2)}, u32[]{:S(2)}) %collective-permute-start.3) | collective-permute-done | bytes 222752 | tf_op jit(solution)/shard_map/ppermute | solution.py:19
  71.2 21.7 %apply.5 = (f32[7168,128]{1,0:T(8,128)S(1)}, bf16[7168,128]{1,0:T(8,128)(2,1)}, bf16[2,870,128]{2,1,0:T(8,128)(2,1)S(1)}) custom-call(s32[4096]{0:T(1024)S(1)} %bitcast.50, s32[870]{0:T(1024)S(1)} %mul.64.refs_1_.ids, f32[8]{0:T(128)S(1)} %copy-done.9, f32[3]{0:T(128)S(1)} %pad_maximum_fusion.5.refs_3_.coef, f32[7168,128]{1,0:T(8,128)S(1)} %copy-done.1, ...), custom_call_target="tpu_custom_call" | custom-call | tf_op jit(solution)/shard_map/apply/pallas_call | solution.py:246
  92.9 1.8 copy-done.2
  94.7 6.6 %collective-permute-start.4 = (bf16[870,128]{1,0:T(8,128)(2,1)S(1)}, bf16[870,128]{1,0:T(8,128)(2,1)S(1)}, u32[]{:S(2)}, u32[]{:S(2)}) collective-permute-start(bf16[870,128]{1,0:T(8,128)(2,1)S(1)} %get-tuple-element.43), channel_id=1, source_target_pairs={{0,2},{2,4},{4,6},{6,8},{8,10},{10,12},{12,14},{14,16},{16,18},{18... | collective-permute-start | bytes 668168 | tf_op jit(solution)/shard_map/ppermute | solution.py:19
  101.3 1.3 collective-permute-start.5
  102.7 3.5 %scatter_fusion = bf16[3584]{0:T(1024)(128)(2,1)S(1)} fusion(bf16[3584]{0:T(1024)(128)(2,1)S(1)} %fusion.3, s32[435]{0:T(512)S(1)} %bitcast.59, bf16[435]{0:T(512)(128)(2,1)S(1)} %broadcast.21), kind=kCustom, calls=%fused_computation | custom fusion | bytes 4350 | tf_op jit(solution)/shard_map/scatter | solution.py:373
  106.3 2.0 %copy-done.3 = f32[7168,128]{1,0:T(8,128)S(1)} copy-done((f32[7168,128]{1,0:T(8,128)S(1)}, f32[7168,128]{1,0:T(8,128)}, u32[]{:S(2)}) %copy-start.3) | copy-done | bytes 3670040
  108.3 3.5 %finish.1 = (bf16[256,3584]{1,0:T(8,128)(2,1)S(1)}, bf16[256,1792]{1,0:T(8,128)(2,1)S(1)}, bf16[256,1792]{1,0:T(8,128)(2,1)S(1)}, f32[256,256]{1,0:T(8,128)S(1)}) custom-call(s32[870]{0:T(1024)S(1)} %mul.64.refs_1_.ids, f32[3]{0:T(128)S(1)} %pad_maximum_fusion.5.refs_3_.coef, s32[1]{0:T(128)} %bitcast.part, f32[7168,128]{1,0:T(8,128)S(1)} %copy-done.3, ...), custom_call_target="tpu_custom_call" | custom-call | tf_op jit(solution)/shard_map/finish/pallas_call | solution.py:390
  111.8 1.2 copy-done.7
  113.0 1.5 collective-permute-start.11
  114.6 3.1 %collective-permute-start.6 = (f32[128,256]{1,0:T(8,128)S(1)}, f32[128,256]{1,0:T(8,128)S(1)}, u32[]{:S(2)}, u32[]{:S(2)}) collective-permute-start(f32[128,256]{1,0:T(8,128)S(1)} %constant_dynamic-slice_fusion.9), channel_id=1, source_target_pairs={{0,2},{2,0},{4,6},{6,4},{8,10},{10,8},{12,14},{14,12},{16,18},{18,... | collective-permute-start | bytes 393224 | tf_op jit(solution)/shard_map/ppermute | solution.py:284
  117.6 1.0 collective-permute-done.6
  118.7 2.6 %collective-permute-start.7 = (f32[32,256]{1,0:T(8,128)S(1)}, f32[32,256]{1,0:T(8,128)S(1)}, u32[]{:S(2)}, u32[]{:S(2)}) collective-permute-start(f32[32,256]{1,0:T(8,128)S(1)} %get-tuple-element.49), channel_id=1, source_target_pairs={{0,4},{2,6},{4,0},{6,2},{8,12},{10,14},{12,8},{14,10},{16,20},{18,... | collective-permute-start | bytes 98312 | tf_op jit(solution)/shard_map/ppermute | solution.py:284
  121.3 1.6 collective-permute-start.8
  122.9 11.1 %collective-permute-done.11.came.first = bf16[256,1792]{1,0:T(8,128)(2,1)S(1)} collective-permute-done((bf16[256,1792]{1,0:T(8,128)(2,1)S(1)}, bf16[256,1792]{1,0:T(8,128)(2,1)S(1)}, u32[]{:S(2)}, u32[]{:S(2)}) %collective-permute-start.11) | collective-permute-done | bytes 917536 | tf_op jit(solution)/shard_map/ppermute | solution.py:313
  133.9 0.5 cross.1
  134.5 2.2 %collective-permute-start.13 = (f32[128,256]{1,0:T(8,128)S(1)}, f32[128,256]{1,0:T(8,128)S(1)}, u32[]{:S(2)}, u32[]{:S(2)}) collective-permute-start(f32[128,256]{1,0:T(8,128)S(1)} %constant_dynamic-slice_fusion.4), channel_id=1, source_target_pairs={{0,2},{2,0},{4,6},{6,4},{8,10},{10,8},{12,14},{14,12},{16,18},{18,... | collective-permute-start | bytes 393224 | tf_op jit(solution)/shard_map/ppermute | solution.py:284
  136.8 5.2 %collective-permute-start.10 = (f32[16,256]{1,0:T(8,128)S(1)}, f32[16,256]{1,0:T(8,128)S(1)}, u32[]{:S(2)}, u32[]{:S(2)}) collective-permute-start(f32[16,256]{1,0:T(8,128)S(1)} %constant_dynamic-slice_fusion.5), channel_id=1, source_target_pairs={{0,16},{2,18},{4,20},{6,22},{8,24},{10,26},{12,28},{14,30},{16,0},... | collective-permute-start | bytes 49160 | tf_op jit(solution)/shard_map/ppermute | solution.py:284
  142.0 0.7 collective-permute-start.14
  142.7 0.7 collective-permute-start.15
  143.4 2.2 %collective-permute-start.16 = (f32[32,256]{1,0:T(8,128)S(1)}, f32[32,256]{1,0:T(8,128)S(1)}, u32[]{:S(2)}, u32[]{:S(2)}) collective-permute-start(f32[32,256]{1,0:T(8,128)S(1)} %get-tuple-element.53), channel_id=1, source_target_pairs={{0,12},{2,14},{4,8},{6,10},{8,4},{10,6},{12,0},{14,2},{16,28},{18,... | collective-permute-start | bytes 98312 | tf_op jit(solution)/shard_map/ppermute | solution.py:284
  145.6 0.1 fusion.4
  145.7 1.5 collective-permute-start.12
  147.2 1.0 collective-permute-done.16
  148.3 1.3 collective-permute-start.17
  149.5 3.4 %collective-permute-done.17 = f32[16,256]{1,0:T(8,128)S(1)} collective-permute-done((f32[16,256]{1,0:T(8,128)S(1)}, f32[16,256]{1,0:T(8,128)S(1)}, u32[]{:S(2)}, u32[]{:S(2)}) %collective-permute-start.17) | collective-permute-done | bytes 16416 | tf_op jit(solution)/shard_map/ppermute | solution.py:284
  153.0 4.5 %collective-permute-done.12.rest_a = bf16[256,896]{1,0:T(8,128)(2,1)S(1)} collective-permute-done((bf16[256,896]{1,0:T(8,128)(2,1)S(1)}, bf16[256,896]{1,0:T(8,128)(2,1)S(1)}, u32[]{:S(2)}, u32[]{:S(2)}) %collective-permute-start.12) | collective-permute-done | bytes 458784 | tf_op jit(solution)/shard_map/ppermute | solution.py:322
  157.5 1.5 collective-permute-start.18
  159.0 2.5 %collective-permute-done.18 = f32[2,16,256]{2,1,0:T(8,128)S(1)} collective-permute-done((f32[2,16,256]{2,1,0:T(8,128)S(1)}, f32[2,16,256]{2,1,0:T(8,128)S(1)}, u32[]{:S(2)}, u32[]{:S(2)}) %collective-permute-start.18) | collective-permute-done | bytes 32800 | tf_op jit(solution)/shard_map/ppermute | solution.py:326
  161.5 1.2 collective-permute-start.19
  162.7 3.9 %collective-permute-done.19 = f32[3,16,256]{2,1,0:T(8,128)S(1)} collective-permute-done((f32[3,16,256]{2,1,0:T(8,128)S(1)}, f32[3,16,256]{2,1,0:T(8,128)S(1)}, u32[]{:S(2)}, u32[]{:S(2)}) %collective-permute-start.19) | collective-permute-done | bytes 49184 | tf_op jit(solution)/shard_map/ppermute | solution.py:301
  166.6 0.3 collective-permute-start.20
  166.9 1.5 collective-permute-start.21
  168.4 1.7 collective-permute-start.22
  170.2 1.1 collective-permute-done.20
  171.3 0.2 collective-permute-done.21
  171.6 2.4 %collective-permute-done.22 = f32[3,32,256]{2,1,0:T(8,128)S(1)} collective-permute-done((f32[3,32,256]{2,1,0:T(8,128)S(1)}, f32[3,32,256]{2,1,0:T(8,128)S(1)}, u32[]{:S(2)}, u32[]{:S(2)}) %collective-permute-start.22) | collective-permute-done | bytes 98336 | tf_op jit(solution)/shard_map/ppermute | solution.py:301
  174.0 0.1 collective-permute-start.23
  174.0 1.5 collective-permute-start.24
  175.7 0.1 collective-permute-done.23
  175.8 5.9 %root.1.columns = bf16[512,256]{1,0:T(8,128)(2,1)S(1)} custom-call(s32[1]{0:T(128)} %bitcast.part, f32[3,256,256]{2,1,0:T(8,128)S(1)} %constant_dynamic-update-slice_fusion.blocks), custom_call_target="tpu_custom_call" | custom-call | tf_op jit(solution)/shard_map/root/pallas_call | solution.py:332
  181.7 5.3 %collective-permute-done.24.rest_b = bf16[256,896]{1,0:T(8,128)(2,1)S(1)} collective-permute-done((bf16[256,896]{1,0:T(8,128)(2,1)S(1)}, bf16[256,896]{1,0:T(8,128)(2,1)S(1)}, u32[]{:S(2)}, u32[]{:S(2)}) %collective-permute-start.24) | collective-permute-done | bytes 458784 | tf_op jit(solution)/shard_map/ppermute | solution.py:328
  187.0 2.5 %rotate.1 = bf16[256,3584]{1,0:T(8,128)(2,1)} custom-call(s32[1]{0:T(128)} %bitcast.part, bf16[512,256]{1,0:T(8,128)(2,1)S(1)} %root.1.columns, bf16[256,3584]{1,0:T(8,128)(2,1)S(1)} %copy-done.8, bf16[256,1792]{1,0:T(8,128)(2,1)S(1)} %collective-permute-done.11.came.first, bf16[256,896]{1,0:T(8,128)(2,1)S(1)} %collective-permute-done.12.rest_a, ...), custom_call_target="tpu_custom_call" | custom-call | tf_op jit(solution)/shard_map/rotate/pallas_call | solution.py:339
  (68 shorter events, 0.7 us)
Async XLA Ops:
  4.7 2.3 %copy-start.10 = (bf16[512,512]{1,0:T(8,128)(2,1)S(1)}, bf16[512,512]{1,0:T(8,128)(2,1)}, u32[]{:S(2)}) copy-start(bf16[512,512]{1,0:T(8,128)(2,1)} %param.8) | copy-start | bytes 1572868
  6.0 1.2 copy-start.11
  7.3 1.5 copy-start.6
  7.3 1.5 copy-start.9
  8.3 18.3 %copy-start = (f32[7168,128]{1,0:T(8,128)}, f32[7168,128]{1,0:T(8,128)S(1)}, u32[]{:S(2)}) copy-start(f32[7168,128]{1,0:T(8,128)S(1)} %broadcast_in_dim.31.refs_4_) | copy-start | bytes 11010052
  26.6 1.8 copy-start.4
  28.5 3.8 %collective-permute-start = (bf16[870,128]{1,0:T(8,128)(2,1)S(1)}, bf16[870,128]{1,0:T(8,128)(2,1)S(1)}, u32[]{:S(2)}, u32[]{:S(2)}) collective-permute-start(bf16[870,128]{1,0:T(8,128)(2,1)S(1)} %get-tuple-element.47), channel_id=1, source_target_pairs={{0,2},{2,4},{4,6},{6,8},{8,10},{10,12},{12,14},{14,16},{16,18},{18... | collective-permute-start | bytes 668168 | tf_op jit(solution)/shard_map/ppermute | solution.py:19
  30.9 5.5 %collective-permute-start.1 = (bf16[870,128]{1,0:T(8,128)(2,1)S(1)}, bf16[870,128]{1,0:T(8,128)(2,1)S(1)}, u32[]{:S(2)}, u32[]{:S(2)}) collective-permute-start(bf16[870,128]{1,0:T(8,128)(2,1)S(1)} %get-tuple-element.48), channel_id=1, source_target_pairs={{2,0},{4,2},{6,4},{8,6},{10,8},{12,10},{14,12},{16,14},{18,16},{20... | collective-permute-start | bytes 668168 | tf_op jit(solution)/shard_map/ppermute | solution.py:19
  36.4 2.0 %copy-start.1 = (f32[7168,128]{1,0:T(8,128)S(1)}, f32[7168,128]{1,0:T(8,128)}, u32[]{:S(2)}) copy-start(f32[7168,128]{1,0:T(8,128)} %copy-done) | copy-start | bytes 11010052
  59.6 1.8 copy-start.5
  61.4 7.7 %collective-permute-start.2 = (bf16[870,128]{1,0:T(8,128)(2,1)S(1)}, bf16[870,128]{1,0:T(8,128)(2,1)S(1)}, u32[]{:S(2)}, u32[]{:S(2)}) collective-permute-start(bf16[870,128]{1,0:T(8,128)(2,1)S(1)} %get-tuple-element.45), channel_id=1, source_target_pairs={{0,2},{2,4},{4,6},{6,8},{8,10},{10,12},{12,14},{14,16},{16,18},{18... | collective-permute-start | bytes 668168 | tf_op jit(solution)/shard_map/ppermute | solution.py:19
  67.7 3.4 %collective-permute-start.3 = (bf16[870,128]{1,0:T(8,128)(2,1)S(1)}, bf16[870,128]{1,0:T(8,128)(2,1)S(1)}, u32[]{:S(2)}, u32[]{:S(2)}) collective-permute-start(bf16[870,128]{1,0:T(8,128)(2,1)S(1)} %get-tuple-element.46), channel_id=1, source_target_pairs={{2,0},{4,2},{6,4},{8,6},{10,8},{12,10},{14,12},{16,14},{18,16},{20... | collective-permute-start | bytes 668168 | tf_op jit(solution)/shard_map/ppermute | solution.py:19
  71.2 31.5 %copy-start.12 = (s32[1,2,435]{2,1,0:T(2,128)S(1)}, s32[1,2,435]{2,1,0:T(2,128)}, u32[]{:S(2)}) copy-start(s32[1,2,435]{2,1,0:T(2,128)} %param.12) | copy-start | bytes 10444
  92.9 1.8 copy-start.2
  94.7 11.4 %collective-permute-start.4 = (bf16[870,128]{1,0:T(8,128)(2,1)S(1)}, bf16[870,128]{1,0:T(8,128)(2,1)S(1)}, u32[]{:S(2)}, u32[]{:S(2)}) collective-permute-start(bf16[870,128]{1,0:T(8,128)(2,1)S(1)} %get-tuple-element.43), channel_id=1, source_target_pairs={{0,2},{2,4},{4,6},{6,8},{8,10},{10,12},{12,14},{14,16},{16,18},{18... | collective-permute-start | bytes 668168 | tf_op jit(solution)/shard_map/ppermute | solution.py:19
  101.3 4.9 %collective-permute-start.5 = (bf16[870,128]{1,0:T(8,128)(2,1)S(1)}, bf16[870,128]{1,0:T(8,128)(2,1)S(1)}, u32[]{:S(2)}, u32[]{:S(2)}) collective-permute-start(bf16[870,128]{1,0:T(8,128)(2,1)S(1)} %get-tuple-element.44), channel_id=1, source_target_pairs={{2,0},{4,2},{6,4},{8,6},{10,8},{12,10},{14,12},{16,14},{18,16},{20... | collective-permute-start | bytes 668168 | tf_op jit(solution)/shard_map/ppermute | solution.py:19
  106.3 2.0 %copy-start.3 = (f32[7168,128]{1,0:T(8,128)S(1)}, f32[7168,128]{1,0:T(8,128)}, u32[]{:S(2)}) copy-start(f32[7168,128]{1,0:T(8,128)} %copy-done.2) | copy-start | bytes 11010052
  111.8 1.2 copy-start.7
  113.0 20.9 %collective-permute-start.11 = (bf16[256,1792]{1,0:T(8,128)(2,1)S(1)}, bf16[256,1792]{1,0:T(8,128)(2,1)S(1)}, u32[]{:S(2)}, u32[]{:S(2)}) collective-permute-start(bf16[256,1792]{1,0:T(8,128)(2,1)S(1)} %get-tuple-element.33), channel_id=1, source_target_pairs={{0,1},{1,0},{2,3},{3,2},{4,5},{5,4},{6,7},{7,6},{8,9},{9,8},{10,11... | collective-permute-start | bytes 2752520 | tf_op jit(solution)/shard_map/ppermute | solution.py:313
  114.6 4.1 %collective-permute-start.6 = (f32[128,256]{1,0:T(8,128)S(1)}, f32[128,256]{1,0:T(8,128)S(1)}, u32[]{:S(2)}, u32[]{:S(2)}) collective-permute-start(f32[128,256]{1,0:T(8,128)S(1)} %constant_dynamic-slice_fusion.9), channel_id=1, source_target_pairs={{0,2},{2,0},{4,6},{6,4},{8,10},{10,8},{12,14},{14,12},{16,18},{18,... | collective-permute-start | bytes 393224 | tf_op jit(solution)/shard_map/ppermute | solution.py:284
  118.7 18.0 %collective-permute-start.7 = (f32[32,256]{1,0:T(8,128)S(1)}, f32[32,256]{1,0:T(8,128)S(1)}, u32[]{:S(2)}, u32[]{:S(2)}) collective-permute-start(f32[32,256]{1,0:T(8,128)S(1)} %get-tuple-element.49), channel_id=1, source_target_pairs={{0,4},{2,6},{4,0},{6,2},{8,12},{10,14},{12,8},{14,10},{16,20},{18,... | collective-permute-start | bytes 98312 | tf_op jit(solution)/shard_map/ppermute | solution.py:284
  121.3 15.4 %collective-permute-start.8 = (f32[32,256]{1,0:T(8,128)S(1)}, f32[32,256]{1,0:T(8,128)S(1)}, u32[]{:S(2)}, u32[]{:S(2)}) collective-permute-start(f32[32,256]{1,0:T(8,128)S(1)} %get-tuple-element.51), channel_id=1, source_target_pairs={{0,8},{2,10},{4,12},{6,14},{8,0},{10,2},{12,4},{14,6},{16,24},{18,... | collective-permute-start | bytes 98312 | tf_op jit(solution)/shard_map/ppermute | solution.py:284
  122.8 13.9 %collective-permute-start.9 = (f32[32,256]{1,0:T(8,128)S(1)}, f32[32,256]{1,0:T(8,128)S(1)}, u32[]{:S(2)}, u32[]{:S(2)}) collective-permute-start(f32[32,256]{1,0:T(8,128)S(1)} %get-tuple-element.50), channel_id=1, source_target_pairs={{0,12},{2,14},{4,8},{6,10},{8,4},{10,6},{12,0},{14,2},{16,28},{18,... | collective-permute-start | bytes 98312 | tf_op jit(solution)/shard_map/ppermute | solution.py:284
  134.5 7.5 %collective-permute-start.13 = (f32[128,256]{1,0:T(8,128)S(1)}, f32[128,256]{1,0:T(8,128)S(1)}, u32[]{:S(2)}, u32[]{:S(2)}) collective-permute-start(f32[128,256]{1,0:T(8,128)S(1)} %constant_dynamic-slice_fusion.4), channel_id=1, source_target_pairs={{0,2},{2,0},{4,6},{6,4},{8,10},{10,8},{12,14},{14,12},{16,18},{18,... | collective-permute-start | bytes 393224 | tf_op jit(solution)/shard_map/ppermute | solution.py:284
  136.8 12.8 %collective-permute-start.10 = (f32[16,256]{1,0:T(8,128)S(1)}, f32[16,256]{1,0:T(8,128)S(1)}, u32[]{:S(2)}, u32[]{:S(2)}) collective-permute-start(f32[16,256]{1,0:T(8,128)S(1)} %constant_dynamic-slice_fusion.5), channel_id=1, source_target_pairs={{0,16},{2,18},{4,20},{6,22},{8,24},{10,26},{12,28},{14,30},{16,0},... | collective-permute-start | bytes 49160 | tf_op jit(solution)/shard_map/ppermute | solution.py:284
  142.0 5.2 %collective-permute-start.14 = (f32[32,256]{1,0:T(8,128)S(1)}, f32[32,256]{1,0:T(8,128)S(1)}, u32[]{:S(2)}, u32[]{:S(2)}) collective-permute-start(f32[32,256]{1,0:T(8,128)S(1)} %get-tuple-element.52), channel_id=1, source_target_pairs={{0,4},{2,6},{4,0},{6,2},{8,12},{10,14},{12,8},{14,10},{16,20},{18,... | collective-permute-start | bytes 98312 | tf_op jit(solution)/shard_map/ppermute | solution.py:284
  142.7 4.5 %collective-permute-start.15 = (f32[32,256]{1,0:T(8,128)S(1)}, f32[32,256]{1,0:T(8,128)S(1)}, u32[]{:S(2)}, u32[]{:S(2)}) collective-permute-start(f32[32,256]{1,0:T(8,128)S(1)} %get-tuple-element.54), channel_id=1, source_target_pairs={{0,8},{2,10},{4,12},{6,14},{8,0},{10,2},{12,4},{14,6},{16,24},{18,... | collective-permute-start | bytes 98312 | tf_op jit(solution)/shard_map/ppermute | solution.py:284
  143.4 4.8 %collective-permute-start.16 = (f32[32,256]{1,0:T(8,128)S(1)}, f32[32,256]{1,0:T(8,128)S(1)}, u32[]{:S(2)}, u32[]{:S(2)}) collective-permute-start(f32[32,256]{1,0:T(8,128)S(1)} %get-tuple-element.53), channel_id=1, source_target_pairs={{0,12},{2,14},{4,8},{6,10},{8,4},{10,6},{12,0},{14,2},{16,28},{18,... | collective-permute-start | bytes 98312 | tf_op jit(solution)/shard_map/ppermute | solution.py:284
  145.7 11.8 %collective-permute-start.12 = (bf16[256,896]{1,0:T(8,128)(2,1)S(1)}, bf16[256,896]{1,0:T(8,128)(2,1)S(1)}, u32[]{:S(2)}, u32[]{:S(2)}) collective-permute-start(bf16[256,896]{1,0:T(8,128)(2,1)S(1)} %get-tuple-element.42), channel_id=1, source_target_pairs={{0,1},{1,0},{2,3},{3,2},{4,5},{5,4},{6,7},{7,6},{8,9},{9,8},{10,11... | collective-permute-start | bytes 1376264 | tf_op jit(solution)/shard_map/ppermute | solution.py:322
  148.3 4.7 %collective-permute-start.17 = (f32[16,256]{1,0:T(8,128)S(1)}, f32[16,256]{1,0:T(8,128)S(1)}, u32[]{:S(2)}, u32[]{:S(2)}) collective-permute-start(f32[16,256]{1,0:T(8,128)S(1)} %constant_dynamic-slice_fusion), channel_id=1, source_target_pairs={{0,16},{2,18},{4,20},{6,22},{8,24},{10,26},{12,28},{14,30},{16,0},... | collective-permute-start | bytes 49160 | tf_op jit(solution)/shard_map/ppermute | solution.py:284
  157.5 3.9 %collective-permute-start.18 = (f32[2,16,256]{2,1,0:T(8,128)S(1)}, f32[2,16,256]{2,1,0:T(8,128)S(1)}, u32[]{:S(2)}, u32[]{:S(2)}) collective-permute-start(f32[2,16,256]{2,1,0:T(8,128)S(1)} %pad_maximum_fusion.4), channel_id=1, source_target_pairs={{0,1},{1,0},{2,3},{3,2},{4,5},{5,4},{6,7},{7,6},{8,9},{9,8},{10,11... | collective-permute-start | bytes 98312 | tf_op jit(solution)/shard_map/ppermute | solution.py:326
  161.5 5.2 %collective-permute-start.19 = (f32[3,16,256]{2,1,0:T(8,128)S(1)}, f32[3,16,256]{2,1,0:T(8,128)S(1)}, u32[]{:S(2)}, u32[]{:S(2)}) collective-permute-start(f32[3,16,256]{2,1,0:T(8,128)S(1)} %get-tuple-element.55), channel_id=1, source_target_pairs={{0,16},{2,18},{4,20},{6,22},{8,24},{10,26},{12,28},{14,30},{16,0},... | collective-permute-start | bytes 147464 | tf_op jit(solution)/shard_map/ppermute | solution.py:301
  166.6 4.7 %collective-permute-start.20 = (f32[3,32,256]{2,1,0:T(8,128)S(1)}, f32[3,32,256]{2,1,0:T(8,128)S(1)}, u32[]{:S(2)}, u32[]{:S(2)}) collective-permute-start(f32[3,32,256]{2,1,0:T(8,128)S(1)} %constant_dynamic-update-slice_fusion.6), channel_id=1, source_target_pairs={{0,4},{2,6},{4,0},{6,2},{8,12},{10,14},{12,8},{14,10},{16,20},{18,... | collective-permute-start | bytes 294920 | tf_op jit(solution)/shard_map/ppermute | solution.py:301
  166.9 4.6 %collective-permute-start.21 = (f32[3,32,256]{2,1,0:T(8,128)S(1)}, f32[3,32,256]{2,1,0:T(8,128)S(1)}, u32[]{:S(2)}, u32[]{:S(2)}) collective-permute-start(f32[3,32,256]{2,1,0:T(8,128)S(1)} %constant_dynamic-update-slice_fusion.6), channel_id=1, source_target_pairs={{0,8},{2,10},{4,12},{6,14},{8,0},{10,2},{12,4},{14,6},{16,24},{18,... | collective-permute-start | bytes 294920 | tf_op jit(solution)/shard_map/ppermute | solution.py:301
  168.4 5.5 %collective-permute-start.22 = (f32[3,32,256]{2,1,0:T(8,128)S(1)}, f32[3,32,256]{2,1,0:T(8,128)S(1)}, u32[]{:S(2)}, u32[]{:S(2)}) collective-permute-start(f32[3,32,256]{2,1,0:T(8,128)S(1)} %constant_dynamic-update-slice_fusion.6), channel_id=1, source_target_pairs={{0,12},{2,14},{4,8},{6,10},{8,4},{10,6},{12,0},{14,2},{16,28},{18,... | collective-permute-start | bytes 294920 | tf_op jit(solution)/shard_map/ppermute | solution.py:301
  171.6 15.4 %copy-start.8 = (bf16[256,3584]{1,0:T(8,128)(2,1)S(1)}, bf16[256,3584]{1,0:T(8,128)(2,1)}, u32[]{:S(2)}) copy-start(bf16[256,3584]{1,0:T(8,128)(2,1)} %copy-done.7) | copy-start | bytes 5505028
  174.0 1.8 collective-permute-start.23
  174.0 12.9 %collective-permute-start.24 = (bf16[256,896]{1,0:T(8,128)(2,1)S(1)}, bf16[256,896]{1,0:T(8,128)(2,1)S(1)}, u32[]{:S(2)}, u32[]{:S(2)}) collective-permute-start(bf16[256,896]{1,0:T(8,128)(2,1)S(1)} %get-tuple-element.40), channel_id=1, source_target_pairs={{0,1},{1,0},{2,3},{3,2},{4,5},{5,4},{6,7},{7,6},{8,9},{9,8},{10,11... | collective-permute-start | bytes 1376264 | tf_op jit(solution)/shard_map/ppermute | solution.py:328

commit v3 on v2

v3 whole, which is shorter than its diff:
```python
import functools
import jax
import jax.numpy as jnp
from jax import lax
from jax.experimental import pallas as pl
from jax.experimental.pallas import tpu as pltpu
from jax.sharding import PartitionSpec as P

DEGREE = 3
NS_ITERS = 3
LN = 3480
LANES = 128
BATCH = 32
SPAN = 256
WIDTH = 256


def passed_along(x, axis, by):
    devices = lax.axis_size(axis)
    pairs = [(i, i + by) for i in range(devices) if 0 <= i + by < devices]
    return lax.ppermute(x, axis, pairs)


def inverse_root(gram):
    frobenius = jnp.sqrt(jnp.sum(gram * gram) + 1e-06)
    iterate = gram / frobenius
    identity = jnp.eye(gram.shape[0], dtype=jnp.float32)
    inverse = identity
    for sweep in range(NS_ITERS):
        factor = 1.5 * identity - 0.5 * jnp.dot(inverse, iterate, precision=lax.Precision.HIGHEST)
        iterate = jnp.dot(iterate, factor, precision=lax.Precision.HIGHEST)
        inverse = jnp.dot(factor, inverse, precision=lax.Precision.HIGHEST)
    return (inverse / jnp.sqrt(frobenius)).astype(jnp.bfloat16)


def batches(count, size, body):
    whole, rest = divmod(count, size)

    def step(g, carry):
        body(pl.multiple_of(g * size, size), size)
        return carry

    lax.fori_loop(0, whole, step, 0)
    if rest:
        body(whole * size, rest)


def add_faces(field, came, wide, ids, scale):
    count = ids.shape[0] // 2
    tiles = wide.shape[0] // count
    for side in range(2):
        wide[...] = came[side][...].astype(jnp.float32) * scale

        def add(base, size):
            rows = [pl.ds(ids[side * count + base + i], tiles) for i in range(size)]
            old = [field[row, :] for row in rows]
            new = [old[i] + wide[pl.ds((base + i) * tiles, tiles), :] for i in range(size)]
            for i in range(size):
                field[rows[i], :] = new[i]

        batches(count, BATCH, add)


def slope(bounds, times):
    return (2.0 * times) / jnp.full((1, LANES), bounds[1] - bounds[0], jnp.float32)


def apply_kernel(step, *refs):
    if step == 0:
        (conn, ids, scales, bounds, pot_row, stiff, start,
         field, rounded, below, above, pot, total, gathered, products, wide) = refs
    else:
        (conn, ids, scales, bounds, pot, stiff, before, older, came_low, came_high,
         field, rounded, below, above, total, gathered, products, wide) = refs
    dofs = stiff.shape[0]
    cells = conn.shape[0] // dofs
    count = ids.shape[0] // 2
    tiles = gathered.shape[0] // dofs
    nodes = field.shape[0] // tiles
    if step == 0:
        width = 512
        for k in range(nodes // width):
            piece = start[:, k * width:(k + 1) * width].astype(jnp.float32)
            node = lax.broadcasted_iota(jnp.int32, piece.shape, 1) + k * width
            turned = jnp.where(node < LN, piece, 0.0).T
            spread = jnp.broadcast_to(pot_row[:, k * width:(k + 1) * width], (LANES, width)).T
            for j in range(tiles):
                field[pl.ds(k * width * tiles + j, width, tiles), :] = turned[:, j * LANES:(j + 1) * LANES]
                pot[pl.ds(k * width * tiles + j, width, tiles), :] = spread
    else:
        add_faces(field, (came_low, came_high), wide, ids, slope(bounds, min(step, 2)))

    def begin(g, carry):
        rows = pl.ds(pl.multiple_of(g * SPAN, SPAN), SPAN)
        low = field[rows, :].astype(jnp.bfloat16)
        rounded[rows, :] = low
        total[rows, :] = pot[rows, :] * low.astype(jnp.float32)
        return carry

    lax.fori_loop(0, field.shape[0] // SPAN, begin, 0)

    def gather(cell, base, size):
        for i in range(size):
            row = conn[cell * dofs + base + i]
            gathered[pl.ds((base + i) * tiles, tiles), :] = field[pl.ds(row, tiles), :]

    def scatter_and_gather(cell, following, base, size):
        rows = [pl.ds(conn[cell * dofs + base + i], tiles) for i in range(size)]
        old = [total[row, :] for row in rows]
        new = [old[i] + products[pl.ds((base + i) * tiles, tiles), :] for i in range(size)]
        for i in range(size):
            total[rows[i], :] = new[i]
        gather(following, base, size)

    batches(dofs, BATCH, functools.partial(gather, 0))

    def one_cell(cell, carry):
        values = jnp.concatenate(
            [gathered[pl.ds(j, dofs, tiles), :].astype(jnp.bfloat16) for j in range(tiles)], axis=1)
        result = jnp.dot(stiff[...], values, preferred_element_type=jnp.float32) * scales[cell]
        for j in range(tiles):
            products[pl.ds(j, dofs, tiles), :] = result[:, j * LANES:(j + 1) * LANES]
        following = jnp.minimum(cell + 1, cells - 1)
        batches(dofs, BATCH, functools.partial(scatter_and_gather, cell, following))
        return carry

    lax.fori_loop(0, cells, one_cell, 0)

    for side, faces in enumerate((below, above)):
        def take(base, size):
            for i in range(size):
                wide[pl.ds((base + i) * tiles, tiles), :] = total[pl.ds(ids[side * count + base + i], tiles), :]

        batches(count, BATCH, take)
        faces[...] = wide[...].astype(faces.dtype)
    center = (bounds[1] + bounds[0]) * 0.5
    rate = slope(bounds, min(step + 1, 2))

    def end(g, carry):
        rows = pl.ds(pl.multiple_of(g * SPAN, SPAN), SPAN)
        value = rate * (total[rows, :] - center * rounded[rows, :].astype(jnp.float32))
        if step:
            value = value - older[rows, :].astype(jnp.float32)
        field[rows, :] = value
        return carry

    lax.fori_loop(0, field.shape[0] // SPAN, end, 0)


def node_rows(field, start, width, tiles):
    return jnp.concatenate(
        [field[pl.ds(start * tiles + j, width, tiles), :] for j in range(tiles)], axis=1)


def send_kernel(ids, bounds, at, before, came_low, came_high, field, away, wide):
    count = ids.shape[0] // 2
    tiles = wide.shape[0] // count
    half = away.shape[0]
    add_faces(field, (came_low, came_high), wide, ids, slope(bounds, 2))
    start = (1 - at[0]) * half
    width = WIDTH
    for k in range(half // width):
        away[k * width:(k + 1) * width, :] = node_rows(
            field, start + k * width, width, tiles).astype(away.dtype)


def turn_kernel(ids, at, before, field, turned, own, own_masked, gram):
    count = ids.shape[0] // 2
    states, nodes = turned.shape
    tiles = states // LANES
    half = own.shape[0]
    start = pl.multiple_of(at[0] * half, LANES)
    width = WIDTH
    for k in range(half // width):
        own[k * width:(k + 1) * width, :] = node_rows(
            field, start + k * width, width, tiles).astype(own.dtype)
    for k in range(nodes // width):
        turned[:, k * width:(k + 1) * width] = node_rows(field, k * width, width, tiles).T.astype(turned.dtype)

    @pl.when(at[1] > 0)
    def _():
        def drop(base, size):
            for i in range(size):
                field[pl.ds(ids[base + i], tiles), :] = jnp.zeros((tiles, LANES), jnp.float32)

        batches(count, BATCH, drop)

    for k in range(half // width):
        own_masked[:, k * width:(k + 1) * width] = node_rows(
            field, start + k * width, width, tiles).T.astype(own_masked.dtype)
    total = jnp.zeros(gram.shape, jnp.float32)
    for k in range(nodes // width):
        total += jnp.dot(turned[:, k * width:(k + 1) * width],
                         node_rows(field, k * width, width, tiles).astype(turned.dtype),
                         preferred_element_type=jnp.float32)
    gram[...] = total


def cross_kernel(at, mine, came, out):
    value = jnp.dot(mine[...], came[...], preferred_element_type=jnp.float32)

    @pl.when(at[0] == 0)
    def _():
        out[...] = value

    @pl.when(at[0] != 0)
    def _():
        out[...] = value.T


def split(x):
    high = x.astype(jnp.bfloat16)
    return high, (x - high.astype(jnp.float32)).astype(jnp.bfloat16)


def product(a, b):
    def dot(x, y):
        return jnp.dot(x, y, preferred_element_type=jnp.float32)

    return dot(a[0], b[0]) + (dot(a[0], b[1]) + dot(a[1], b[0]))


def root_kernel(at, blocks, out, gram, held):
    size = blocks.shape[1]
    cross = blocks[2]
    gram[:size, :size] = blocks[0]
    gram[size:, size:] = blocks[1]
    gram[:size, size:] = cross
    gram[size:, :size] = cross.T
    whole = gram[...]
    scale = jnp.sqrt(jnp.sum(whole * whole, keepdims=True) + 1e-06)
    start = pl.multiple_of(at[0] * size, LANES)
    row = lax.broadcasted_iota(jnp.int32, whole.shape, 0)
    column = lax.broadcasted_iota(jnp.int32, whole.shape, 1)
    diagonal = jnp.where(row == column, 1.5, 0.0)
    iterate = split(whole / scale)
    factor = diagonal - 0.5 * (whole / scale)
    inverse = split(factor)
    for sweep in range(1, NS_ITERS):
        iterate = split(product(iterate, split(factor)))
        factor = diagonal - 0.5 * product(inverse, iterate)
        if sweep == NS_ITERS - 1:
            held[0] = inverse[0]
            held[1] = inverse[1]
            columns = held[0, :, pl.ds(start, size)], held[1, :, pl.ds(start, size)]
            result = product(split(factor), columns)
        else:
            inverse = split(product(split(factor), inverse))
    out[...] = (result / jnp.sqrt(scale)).astype(jnp.bfloat16)


def rotate_kernel(at, columns, turned, first, rest_a, rest_b, out):
    states, nodes = out.shape
    half = nodes // 2
    own = columns[pl.ds(pl.multiple_of(at[0] * states, states), states), :]
    other = columns[pl.ds(pl.multiple_of((1 - at[0]) * states, states), states), :]

    def part_of(base, came):
        width = came.shape[0]
        base = pl.multiple_of(base, LANES)
        value = lax.dot_general(
            own, turned[:, pl.ds(base, width)], (((0,), (0,)), ((), ())), preferred_element_type=jnp.float32)
        value += lax.dot_general(
            other, came[...], (((0,), (1,)), ((), ())), preferred_element_type=jnp.float32)
        out[:, pl.ds(base, width)] = value.astype(out.dtype)

    part_of(at[0] * half, first)
    away = (1 - at[0]) * half
    part_of(away, rest_a)
    part_of(away + rest_a.shape[0], rest_b)


SMEM = pl.BlockSpec(memory_space=pltpu.SMEM)
VMEM = pl.BlockSpec(memory_space=pltpu.VMEM)
def limit(mib):
    return pltpu.CompilerParams(vmem_limit_bytes=mib * 1024 * 1024)


def struct(shape, dtype=jnp.float32):
    return jax.ShapeDtypeStruct(shape, dtype)


def apply_call(step, tables, pot, stiff, *fields):
    conn, ids = tables[:2]
    dofs = stiff.shape[0]
    count = ids.shape[0] // 2
    f32, bf16 = jnp.float32, jnp.bfloat16
    if step == 0:
        tiles = fields[0].shape[0] // LANES
        rows = fields[0].shape[1] * tiles
    else:
        rows = pot.shape[0]
        tiles = fields[2].shape[0] // count
    face = struct((count * tiles, LANES), bf16)
    out_shape = [struct((rows, LANES)), struct((rows, LANES), bf16), face, face]
    if step == 0:
        out_shape.append(struct((rows, LANES)))
    return pl.pallas_call(
        functools.partial(apply_kernel, step),
        out_shape=out_shape,
        in_specs=[SMEM] * 4 + [VMEM] * (2 + len(fields)),
        out_specs=[VMEM] * len(out_shape),
        scratch_shapes=[
            pltpu.VMEM((rows, LANES), f32),
            pltpu.VMEM((dofs * tiles, LANES), f32),
            pltpu.VMEM((dofs * tiles, LANES), f32),
            pltpu.VMEM((count * tiles, LANES), f32),
        ],
        input_output_aliases={6: 0} if step else {},
        compiler_params=limit(26),
        name="apply",
    )(*tables, pot, stiff, *fields)


def groups_of(devices):
    bits = devices.bit_length() - 1
    return [list(range(b, min(b + 2, bits))) if b else [0] for b in [0] + list(range(1, bits, 2))][:bits]


def plan(group):
    for m in range(1, 1 << len(group)):
        yield m, sum(((m >> i) & 1) << bit for i, bit in enumerate(group))


def code_of(group):
    at = lax.axis_index("dom")
    return sum(((at >> bit) & 1) << i for i, bit in enumerate(group))


def sum_scatter(x):
    devices = lax.axis_size("dom")
    for group in groups_of(devices):
        size = x.shape[-2] >> len(group)
        code = code_of(group)
        came = [
            lax.ppermute(
                lax.dynamic_slice_in_dim(x, (code ^ m) * size, size, x.ndim - 2),
                "dom", [(i, i ^ mask) for i in range(devices)])
            for m, mask in plan(group)
        ]
        x = lax.dynamic_slice_in_dim(x, code * size, size, x.ndim - 2)
        for y in came:
            x = x + y
    return x


def gather_all(x):
    devices = lax.axis_size("dom")
    for group in reversed(groups_of(devices)):
        size = x.shape[-2]
        code = code_of(group)
        pieces = [(0, x)] + [
            (m, lax.ppermute(x, "dom", [(i, i ^ mask) for i in range(devices)])) for m, mask in plan(group)
        ]
        x = jnp.zeros(x.shape[:-2] + (size << len(group), x.shape[-1]), x.dtype)
        for m, piece in pieces:
            x = lax.dynamic_update_slice_in_dim(x, piece, (code ^ m) * size, x.ndim - 2)
    return x


def rotate_pair(field, away, ids, at, states, nodes):
    f32, bf16 = jnp.float32, jnp.bfloat16
    swap = [(0, 1), (1, 0)]
    half = nodes // 2
    came = lax.ppermute(away, "st", swap)
    _, turned, own, own_masked, gram = pl.pallas_call(
        turn_kernel,
        out_shape=[struct(field.shape), struct((states, nodes), bf16), struct((half, states), bf16),
                   struct((states, half), bf16), struct((states, states))],
        in_specs=[SMEM, SMEM, VMEM], out_specs=[VMEM] * 5,
        input_output_aliases={2: 0},
        compiler_params=limit(26), name="turn",
        cost_estimate=pl.CostEstimate(flops=4 * 10**9, bytes_accessed=10**7, transcendentals=0),
    )(ids, at, field)
    own_sum = sum_scatter(gram)
    cross = pl.pallas_call(
        cross_kernel,
        out_shape=struct((states, states)),
        in_specs=[SMEM, VMEM, VMEM], out_specs=VMEM, compiler_params=limit(16), name="cross",
    )(at, own_masked, came)
    first_rows = half // 4 // LANES * LANES
    rest, cross = lax.optimization_barrier((own, cross))
    rest_a = lax.ppermute(rest[:first_rows], "st", swap)
    cross_sum = sum_scatter(cross)
    pair = jnp.stack([own_sum, cross_sum])
    theirs = lax.ppermute(pair, "st", swap)
    later, theirs = lax.optimization_barrier((rest[first_rows:], theirs))
    rest_b = lax.ppermute(later, "st", swap)
    lower = at[0] == 0
    blocks = gather_all(jnp.stack([
        jnp.where(lower, pair[0], theirs[0]), jnp.where(lower, theirs[0], pair[0]), pair[1] + theirs[1]]))
    columns = pl.pallas_call(
        root_kernel,
        out_shape=struct((2 * states, states), bf16),
        in_specs=[SMEM, VMEM], out_specs=VMEM,
        scratch_shapes=[pltpu.VMEM((2 * states, 2 * states), f32), pltpu.VMEM((2, 2 * states, 2 * states), bf16)],
        compiler_params=limit(26), name="root",
    )(at, blocks)
    return pl.pallas_call(
        rotate_kernel,
        out_shape=struct((states, nodes), bf16),
        in_specs=[SMEM] + [VMEM] * 5, out_specs=VMEM, compiler_params=limit(26), name="rotate",
    )(at, columns, turned, came, rest_a, rest_b)


def rotate_any(current, owned):
    states = current.shape[0]
    whole = lax.all_gather(current, "st", axis=0, tiled=True)
    rows = lax.dot_general(
        current * owned, whole, (((1,), (1,)), ((), ())), preferred_element_type=jnp.float32)
    gram = lax.all_gather(lax.psum(rows, "dom"), "st", axis=0, tiled=True)
    columns = lax.dynamic_slice_in_dim(inverse_root(gram), lax.axis_index("st") * states, states, 1)
    rotated = lax.dot_general(
        columns, whole, (((0,), (0,)), ((), ())), preferred_element_type=jnp.float32)
    return rotated.astype(jnp.bfloat16)


def body(start_states, stiffness, cell_scale, potential, connectivity, shared_nodes, filter_bounds):
    block_states, nodes = start_states.shape
    tiles = pl.cdiv(block_states, LANES)
    states = tiles * LANES
    if states != block_states:
        start_states = jnp.pad(start_states, ((0, states - block_states), (0, 0)))
    conn = connectivity.reshape(-1) * tiles
    ids = shared_nodes.reshape(-1) * tiles
    tables = conn, ids, cell_scale, filter_bounds
    stiff = stiffness.T
    at = jnp.stack([lax.axis_index("st"), lax.axis_index("dom")])

    def exchange(low, high):
        return passed_along(high, "dom", 1), passed_along(low, "dom", -1)

    field, older, low, high, pot = apply_call(0, tables, potential[None, :], stiff, start_states)
    for step in range(1, DEGREE):
        field, newer, low, high = apply_call(
            step, tables, pot, stiff, field, older, *exchange(low, high))
        older = newer
    field, away = pl.pallas_call(
        send_kernel,
        out_shape=[struct(field.shape), struct((nodes // 2, states), jnp.bfloat16)],
        in_specs=[SMEM] * 3 + [VMEM] * 3,
        out_specs=[VMEM] * 2,
        scratch_shapes=[pltpu.VMEM((ids.shape[0] // 2 * tiles, LANES), jnp.float32)],
        input_output_aliases={3: 0},
        compiler_params=limit(16),
        name="send",
    )(ids, filter_bounds, at, field, *exchange(low, high))
    devices = lax.axis_size("dom")
    if lax.axis_size("st") == 2 and states == block_states and devices & (devices - 1) == 0:
        return rotate_pair(field, away, ids, at, states, nodes)
    current = field.reshape(nodes, states).T.astype(jnp.bfloat16)[:block_states]
    inside = (jnp.arange(nodes) < LN).astype(jnp.bfloat16)
    keep = jnp.where(lax.axis_index("dom") > 0, 0.0, 1.0).astype(jnp.bfloat16)
    owned = inside.at[shared_nodes[0, 0]].set(keep)[None, :]
    return rotate_any(current, owned)


def solution(mesh):
    placed = (P("st", "dom"), P(), P("dom"), P("dom"), P("dom", None), P("dom", None, None), P())
    return jax.shard_map(
        body, mesh=mesh, in_specs=placed, out_specs=P("st", "dom"), check_vma=False
    )
```

time: 190 us -> 175 us (0.921)
  waiting for transfers between devices: 42.6 us -> 22.2 us
  starting transfers between devices: 49.5 us -> 57.2 us
  between operations: 3.1 us -> 0.33 us
  local copies, waits for them, and re-layouts: 20 us -> 17.9 us
    ppermute x2, waiting for transfers between devices: 15.6 us -> 2.28 us  [the longest x1 2.28 us: rotate_pair(): came = lax.ppermute(away, 'st', swap)]
    ppermute x10, starting transfers between devices: 19.5 us -> 25.4 us  [sum_scatter(): lax.ppermute(lax.dynamic_slice_in_dim(x, (code ^ m) * size, size, x.ndim...]
    ppermute x1, waiting for transfers between devices: 5.26 us -> 0.01 us  [rotate_pair(): rest_b = lax.ppermute(later, 'st', swap)]
    scatter x1 -> x0, local copies, waits for them, and re-layouts: 3.49 us -> none  [body(): owned = inside.at[shared_nodes[0, 0]].set(keep)[None, :]]
    unnamed x28 -> x22, local copies, waits for them, and re-layouts: 11.4 us -> 14.8 us
    broadcast_in_dim x5 -> x1, local copies, waits for them, and re-layouts: 3.26 us -> 0.73 us  [body(): potential[None, :]]
    ppermute x5, waiting for transfers between devices: 7.71 us -> 5.48 us  [gather_all(): lax.ppermute(x, 'dom', [(i, i ^ mask) for i in range(devices)])]
    ppermute x6, waiting for transfers between devices: 6.1 us -> 8.22 us  [passed_along(): return lax.ppermute(x, axis, pairs)]
  transfers between devices with their start and end apart: 25 -> 25, of which waited for: 14 -> 13; matrix products, arithmetic and copies ran while one was open for 2% -> 1% of each run, Pallas kernels for 3% -> 5%
where the time goes in v3:
time: 175 us; the launch traced here: 174 us
  Pallas kernels  74.8 us (43%)
  starting transfers between devices  57.2 us (33%)
  waiting for transfers between devices  22.2 us (13%)
  local copies, waits for them, and re-layouts  17.9 us (10%)
    pallas_call x3, Pallas kernels, apply_call(): pl.pallas_call(functools.partial(apply_kernel, step), out_shape=out_shape...  58.8 us
    ppermute x10, starting transfers between devices, sum_scatter(): lax.ppermute(lax.dynamic_slice_in_dim(x, (code ^ m) * size, size, x.ndim...  25.4 us
    ppermute x6, starting transfers between devices, passed_along(): return lax.ppermute(x, axis, pairs)  19.2 us
    unnamed x22, local copies, waits for them, and re-layouts  14.8 us
    ppermute x6, waiting for transfers between devices, passed_along(): return lax.ppermute(x, axis, pairs)  8.22 us
    pallas_call x1, Pallas kernels, rotate_pair(): pl.pallas_call(root_kernel, out_shape=struct((2 * states, states), bf16),...  6.44 us
    ppermute x5, starting transfers between devices, gather_all(): lax.ppermute(x, 'dom', [(i, i ^ mask) for i in range(devices)])  6.08 us
    ppermute x5, waiting for transfers between devices, gather_all(): lax.ppermute(x, 'dom', [(i, i ^ mask) for i in range(devices)])  5.48 us
  transfers between devices with their start and end apart: 25, of which 13 were waited for; matrix products, arithmetic and copies ran while one was open for 1% of the time, Pallas kernels for 5%

profile of v3, /device:TPU:0, one launch (start us, length us, event | category | flops | bytes accessed | tf_op | source)
XLA Modules:
  0.0 174.1 jit_solution(3524967852026664725)
XLA Ops:
  0.0 0.7 broadcast_multiply_fusion
  0.7 0.1 mul.58.refs_1_.ids
  0.8 1.3 copy.12
  2.0 0.7 multiply_bitcast_fusion
  2.8 0.7 broadcast_in_dim.15.refs_4_
  3.5 1.5 copy-done.4
  5.0 0.7 copy-done.8
  5.7 0.7 copy-done.9
  6.3 18.3 %apply.3 = (f32[7168,128]{1,0:T(8,128)S(1)}, bf16[7168,128]{1,0:T(8,128)(2,1)S(1)}, bf16[870,128]{1,0:T(8,128)(2,1)S(1)}, bf16[870,128]{1,0:T(8,128)(2,1)S(1)}, f32[7168,128]{1,0:T(8,128)S(1)}) custom-call(s32[4096]{0:T(1024)S(1)} %bitcast.29, s32[870]{0:T(1024)S(1)} %mul.58.refs_1_.ids, f32[8]{0:T(128)S(1)} %copy-done.9, f32[2]{0:T(128)S(1)} %copy-done.8, ...), custom_call_target="tpu_custom_call" | custom-call | tf_op jit(solution)/shard_map/apply/pallas_call | solution.py:298
  24.6 2.4 %collective-permute-start = (bf16[870,128]{1,0:T(8,128)(2,1)S(1)}, bf16[870,128]{1,0:T(8,128)(2,1)S(1)}, u32[]{:S(2)}, u32[]{:S(2)}) collective-permute-start(bf16[870,128]{1,0:T(8,128)(2,1)S(1)} %get-tuple-element.30), channel_id=1, source_target_pairs={{0,2},{2,4},{4,6},{6,8},{8,10},{10,12},{12,14},{14,16},{16,18},{18... | collective-permute-start | bytes 668168 | tf_op jit(solution)/shard_map/ppermute | solution.py:21
  27.0 1.3 collective-permute-start.1
  28.4 4.2 %collective-permute-done.1.refs_9_ = bf16[870,128]{1,0:T(8,128)(2,1)S(1)} collective-permute-done((bf16[870,128]{1,0:T(8,128)(2,1)S(1)}, bf16[870,128]{1,0:T(8,128)(2,1)S(1)}, u32[]{:S(2)}, u32[]{:S(2)}) %collective-permute-start.1) | collective-permute-done | bytes 222752 | tf_op jit(solution)/shard_map/ppermute | solution.py:21
  32.5 19.6 %apply.4 = (f32[7168,128]{1,0:T(8,128)S(1)}, bf16[7168,128]{1,0:T(8,128)(2,1)S(1)}, bf16[870,128]{1,0:T(8,128)(2,1)S(1)}, bf16[870,128]{1,0:T(8,128)(2,1)S(1)}) custom-call(s32[4096]{0:T(1024)S(1)} %bitcast.30, s32[870]{0:T(1024)S(1)} %mul.58.refs_1_.ids, f32[8]{0:T(128)S(1)} %copy-done.9, f32[2]{0:T(128)S(1)} %copy-done.8, ...), custom_call_target="tpu_custom_call", output_to_operand_aliasing={{0}: (6, {})} | custom-call | tf_op jit(solution)/shard_map/apply/pallas_call | solution.py:298
  52.2 6.3 %collective-permute-start.2 = (bf16[870,128]{1,0:T(8,128)(2,1)S(1)}, bf16[870,128]{1,0:T(8,128)(2,1)S(1)}, u32[]{:S(2)}, u32[]{:S(2)}) collective-permute-start(bf16[870,128]{1,0:T(8,128)(2,1)S(1)} %get-tuple-element.34), channel_id=1, source_target_pairs={{0,2},{2,4},{4,6},{6,8},{8,10},{10,12},{12,14},{14,16},{16,18},{18... | collective-permute-start | bytes 668168 | tf_op jit(solution)/shard_map/ppermute | solution.py:21
  58.5 1.3 collective-permute-start.3
  59.8 2.1 %collective-permute-done.3.refs_9_ = bf16[870,128]{1,0:T(8,128)(2,1)S(1)} collective-permute-done((bf16[870,128]{1,0:T(8,128)(2,1)S(1)}, bf16[870,128]{1,0:T(8,128)(2,1)S(1)}, u32[]{:S(2)}, u32[]{:S(2)}) %collective-permute-start.3) | collective-permute-done | bytes 222752 | tf_op jit(solution)/shard_map/ppermute | solution.py:21
  61.9 20.9 %apply.5 = (f32[7168,128]{1,0:T(8,128)S(1)}, bf16[7168,128]{1,0:T(8,128)(2,1)}, bf16[870,128]{1,0:T(8,128)(2,1)S(1)}, bf16[870,128]{1,0:T(8,128)(2,1)S(1)}) custom-call(s32[4096]{0:T(1024)S(1)} %bitcast.31, s32[870]{0:T(1024)S(1)} %mul.58.refs_1_.ids, f32[8]{0:T(128)S(1)} %copy-done.9, f32[2]{0:T(128)S(1)} %copy-done.8, ...), custom_call_target="tpu_custom_call", output_to_operand_aliasing={{0}: (6, {})} | custom-call | tf_op jit(solution)/shard_map/apply/pallas_call | solution.py:298
  82.7 1.8 %copy-done = f32[7168,128]{1,0:T(8,128)} copy-done((f32[7168,128]{1,0:T(8,128)}, f32[7168,128]{1,0:T(8,128)S(1)}, u32[]{:S(2)}) %copy-start) | copy-done | bytes 3670040
  84.5 6.6 %collective-permute-start.4 = (bf16[870,128]{1,0:T(8,128)(2,1)S(1)}, bf16[870,128]{1,0:T(8,128)(2,1)S(1)}, u32[]{:S(2)}, u32[]{:S(2)}) collective-permute-start(bf16[870,128]{1,0:T(8,128)(2,1)S(1)} %get-tuple-element.37), channel_id=1, source_target_pairs={{0,2},{2,4},{4,6},{6,8},{8,10},{10,12},{12,14},{14,16},{16,18},{18... | collective-permute-start | bytes 668168 | tf_op jit(solution)/shard_map/ppermute | solution.py:21
  91.1 1.3 collective-permute-start.5
  92.5 0.1 pad_add_fusion.at
  92.5 2.0 %collective-permute-done.5.came_high = bf16[870,128]{1,0:T(8,128)(2,1)S(1)} collective-permute-done((bf16[870,128]{1,0:T(8,128)(2,1)S(1)}, bf16[870,128]{1,0:T(8,128)(2,1)S(1)}, u32[]{:S(2)}, u32[]{:S(2)}) %collective-permute-start.5) | collective-permute-done | bytes 222752 | tf_op jit(solution)/shard_map/ppermute | solution.py:21
  94.5 2.0 %copy-done.1 = f32[7168,128]{1,0:T(8,128)S(1)} copy-done((f32[7168,128]{1,0:T(8,128)S(1)}, f32[7168,128]{1,0:T(8,128)}, u32[]{:S(2)}) %copy-start.1) | copy-done | bytes 3670040
  96.6 3.6 %send.1 = (f32[7168,128]{1,0:T(8,128)S(1)}, bf16[1792,256]{1,0:T(8,128)(2,1)}) custom-call(s32[870]{0:T(1024)S(1)} %mul.58.refs_1_.ids, f32[2]{0:T(128)S(1)} %copy-done.8, s32[2]{0:T(128)S(1)} %pad_add_fusion.at, f32[7168,128]{1,0:T(8,128)S(1)} %copy-done.1, bf16[870,128]{1,0:T(8,128)(2,1)S(1)} %collective-permute-done.4.came_low, ...), custom_call_target="tpu_custom_call", output_to_operand_aliasing={{0}: (3, {})} | custom-call | tf_op jit(solution)/shard_map/send/pallas_call | solution.py:438
  100.2 1.8 %copy-done.2 = f32[7168,128]{1,0:T(8,128)} copy-done((f32[7168,128]{1,0:T(8,128)}, f32[7168,128]{1,0:T(8,128)S(1)}, u32[]{:S(2)}) %copy-start.2) | copy-done | bytes 3670040
  102.0 1.5 collective-permute-start.11
  103.5 2.0 %copy-done.3 = f32[7168,128]{1,0:T(8,128)S(1)} copy-done((f32[7168,128]{1,0:T(8,128)S(1)}, f32[7168,128]{1,0:T(8,128)}, u32[]{:S(2)}) %copy-start.3) | copy-done | bytes 3670040
  105.5 1.8 %turn.1 = (f32[7168,128]{1,0:T(8,128)S(1)}, bf16[256,3584]{1,0:T(8,128)(2,1)S(1)}, bf16[1792,256]{1,0:T(8,128)(2,1)S(1)}, bf16[256,1792]{1,0:T(8,128)(2,1)S(1)}, f32[256,256]{1,0:T(8,128)S(1)}) custom-call(s32[870]{0:T(1024)S(1)} %mul.58.refs_1_.ids, s32[2]{0:T(128)S(1)} %pad_add_fusion.at, f32[7168,128]{1,0:T(8,128)S(1)} %copy-done.3), custom_call_target="tpu_custom_call", output_to_operand_aliasing={{0}: (2, {})} | custom-call | flops 4000000000 | bytes 10000000 | tf_op jit(solution)/shard_map/turn/pallas_call | solution.py:366
  107.4 0.9 copy-done.5
  108.3 0.9 copy-done.6
  109.2 4.9 %collective-permute-start.6 = (f32[128,256]{1,0:T(8,128)S(1)}, f32[128,256]{1,0:T(8,128)S(1)}, u32[]{:S(2)}, u32[]{:S(2)}) collective-permute-start(f32[128,256]{1,0:T(8,128)S(1)} %constant_dynamic-slice_fusion.9), channel_id=1, source_target_pairs={{0,2},{2,0},{4,6},{6,4},{8,10},{10,8},{12,14},{14,12},{16,18},{18,... | collective-permute-start | bytes 393224 | tf_op jit(solution)/shard_map/ppermute | solution.py:336
  114.1 1.0 collective-permute-done.6
  115.2 2.6 %collective-permute-start.7 = (f32[32,256]{1,0:T(8,128)S(1)}, f32[32,256]{1,0:T(8,128)S(1)}, u32[]{:S(2)}, u32[]{:S(2)}) collective-permute-start(f32[32,256]{1,0:T(8,128)S(1)} %get-tuple-element.49), channel_id=1, source_target_pairs={{0,4},{2,6},{4,0},{6,2},{8,12},{10,14},{12,8},{14,10},{16,20},{18,... | collective-permute-start | bytes 98312 | tf_op jit(solution)/shard_map/ppermute | solution.py:336
  117.8 1.6 collective-permute-start.8
  119.4 2.3 %collective-permute-done.11.came.first = bf16[1792,256]{1,0:T(8,128)(2,1)S(1)} collective-permute-done((bf16[1792,256]{1,0:T(8,128)(2,1)}, bf16[1792,256]{1,0:T(8,128)(2,1)S(1)}, u32[]{:S(2)}, u32[]{:S(2)}) %collective-permute-start.11) | collective-permute-done | bytes 917536 | tf_op jit(solution)/shard_map/ppermute | solution.py:365
  121.6 1.2 copy-done.7
  122.8 1.1 cross.1
  124.0 3.7 %collective-permute-start.12 = (f32[128,256]{1,0:T(8,128)S(1)}, f32[128,256]{1,0:T(8,128)S(1)}, u32[]{:S(2)}, u32[]{:S(2)}) collective-permute-start(f32[128,256]{1,0:T(8,128)S(1)} %constant_dynamic-slice_fusion.4), channel_id=1, source_target_pairs={{0,2},{2,0},{4,6},{6,4},{8,10},{10,8},{12,14},{14,12},{16,18},{18,... | collective-permute-start | bytes 393224 | tf_op jit(solution)/shard_map/ppermute | solution.py:336
  127.7 1.0 collective-permute-done.12
  128.7 4.6 %collective-permute-start.13 = (f32[32,256]{1,0:T(8,128)S(1)}, f32[32,256]{1,0:T(8,128)S(1)}, u32[]{:S(2)}, u32[]{:S(2)}) collective-permute-start(f32[32,256]{1,0:T(8,128)S(1)} %get-tuple-element.52), channel_id=1, source_target_pairs={{0,4},{2,6},{4,0},{6,2},{8,12},{10,14},{12,8},{14,10},{16,20},{18,... | collective-permute-start | bytes 98312 | tf_op jit(solution)/shard_map/ppermute | solution.py:336
  133.3 1.6 collective-permute-start.14
  134.8 1.3 collective-permute-start.15
  136.2 3.0 %collective-permute-start.10 = (f32[16,256]{1,0:T(8,128)S(1)}, f32[16,256]{1,0:T(8,128)S(1)}, u32[]{:S(2)}, u32[]{:S(2)}) collective-permute-start(f32[16,256]{1,0:T(8,128)S(1)} %constant_dynamic-slice_fusion.5), channel_id=1, source_target_pairs={{0,16},{2,18},{4,20},{6,22},{8,24},{10,26},{12,28},{14,30},{16,0},... | collective-permute-start | bytes 49160 | tf_op jit(solution)/shard_map/ppermute | solution.py:336
  139.2 0.6 collective-permute-done.15
  139.8 2.1 %collective-permute-start.16 = (f32[16,256]{1,0:T(8,128)S(1)}, f32[16,256]{1,0:T(8,128)S(1)}, u32[]{:S(2)}, u32[]{:S(2)}) collective-permute-start(f32[16,256]{1,0:T(8,128)S(1)} %constant_dynamic-slice_fusion), channel_id=1, source_target_pairs={{0,16},{2,18},{4,20},{6,22},{8,24},{10,26},{12,28},{14,30},{16,0},... | collective-permute-start | bytes 49160 | tf_op jit(solution)/shard_map/ppermute | solution.py:336
  141.9 2.6 %collective-permute-done.16 = f32[16,256]{1,0:T(8,128)S(1)} collective-permute-done((f32[16,256]{1,0:T(8,128)S(1)}, f32[16,256]{1,0:T(8,128)S(1)}, u32[]{:S(2)}, u32[]{:S(2)}) %collective-permute-start.16) | collective-permute-done | bytes 16416 | tf_op jit(solution)/shard_map/ppermute | solution.py:336
  144.5 1.7 collective-permute-start.17
  146.2 1.2 slice.13
  147.4 1.2 collective-permute-done.17
  148.6 2.5 %collective-permute-start.18 = (f32[3,16,256]{2,1,0:T(8,128)S(1)}, f32[3,16,256]{2,1,0:T(8,128)S(1)}, u32[]{:S(2)}, u32[]{:S(2)}) collective-permute-start(f32[3,16,256]{2,1,0:T(8,128)S(1)} %get-tuple-element.55), channel_id=1, source_target_pairs={{0,16},{2,18},{4,20},{6,22},{8,24},{10,26},{12,28},{14,30},{16,0},... | collective-permute-start | bytes 147464 | tf_op jit(solution)/shard_map/ppermute | solution.py:353
  151.0 1.6 collective-permute-start.24
  152.7 1.6 collective-permute-done.18
  154.2 1.7 collective-permute-start.19
  156.0 0.3 collective-permute-start.20
  156.3 1.5 collective-permute-start.21
  157.9 1.1 collective-permute-done.19
  158.9 1.6 collective-permute-done.20
  160.6 1.2 collective-permute-done.21
  161.8 0.1 collective-permute-start.22
  161.9 0.9 slice.16
  162.8 1.7 collective-permute-start.23
  164.5 0.1 broadcast_in_dim.12
  164.6 6.4 %root.1.columns = bf16[512,256]{1,0:T(8,128)(2,1)S(1)} custom-call(s32[2]{0:T(128)S(1)} %pad_add_fusion.at, f32[3,256,256]{2,1,0:T(8,128)S(1)} %constant_dynamic-update-slice_fusion.blocks), custom_call_target="tpu_custom_call" | custom-call | tf_op jit(solution)/shard_map/root/pallas_call | solution.py:392
  171.1 3.0 %rotate.1 = bf16[256,3584]{1,0:T(8,128)(2,1)} custom-call(s32[2]{0:T(128)S(1)} %pad_add_fusion.at, bf16[512,256]{1,0:T(8,128)(2,1)S(1)} %root.1.columns, bf16[256,3584]{1,0:T(8,128)(2,1)S(1)} %get-tuple-element.47.turned, bf16[1792,256]{1,0:T(8,128)(2,1)S(1)} %collective-permute-done.11.came.first, bf16[384,256]{1,0:T(8,128)(2,1)S(1)} %collective-permute-done.23.rest_a, ...), custom_call_target="tpu_custom_call" | custom-call | tf_op jit(solution)/shard_map/rotate/pallas_call | solution.py:399
  (48 shorter events, 0.4 us)
Async XLA Ops:
  3.5 1.5 copy-start.4
  5.0 0.7 copy-start.8
  5.6 0.7 copy-start.9
  24.6 3.7 %collective-permute-start = (bf16[870,128]{1,0:T(8,128)(2,1)S(1)}, bf16[870,128]{1,0:T(8,128)(2,1)S(1)}, u32[]{:S(2)}, u32[]{:S(2)}) collective-permute-start(bf16[870,128]{1,0:T(8,128)(2,1)S(1)} %get-tuple-element.30), channel_id=1, source_target_pairs={{0,2},{2,4},{4,6},{6,8},{8,10},{10,12},{12,14},{14,16},{16,18},{18... | collective-permute-start | bytes 668168 | tf_op jit(solution)/shard_map/ppermute | solution.py:21
  27.0 5.5 %collective-permute-start.1 = (bf16[870,128]{1,0:T(8,128)(2,1)S(1)}, bf16[870,128]{1,0:T(8,128)(2,1)S(1)}, u32[]{:S(2)}, u32[]{:S(2)}) collective-permute-start(bf16[870,128]{1,0:T(8,128)(2,1)S(1)} %get-tuple-element.31), channel_id=1, source_target_pairs={{2,0},{4,2},{6,4},{8,6},{10,8},{12,10},{14,12},{16,14},{18,16},{20... | collective-permute-start | bytes 668168 | tf_op jit(solution)/shard_map/ppermute | solution.py:21
  52.2 7.6 %collective-permute-start.2 = (bf16[870,128]{1,0:T(8,128)(2,1)S(1)}, bf16[870,128]{1,0:T(8,128)(2,1)S(1)}, u32[]{:S(2)}, u32[]{:S(2)}) collective-permute-start(bf16[870,128]{1,0:T(8,128)(2,1)S(1)} %get-tuple-element.34), channel_id=1, source_target_pairs={{0,2},{2,4},{4,6},{6,8},{8,10},{10,12},{12,14},{14,16},{16,18},{18... | collective-permute-start | bytes 668168 | tf_op jit(solution)/shard_map/ppermute | solution.py:21
  58.5 3.4 %collective-permute-start.3 = (bf16[870,128]{1,0:T(8,128)(2,1)S(1)}, bf16[870,128]{1,0:T(8,128)(2,1)S(1)}, u32[]{:S(2)}, u32[]{:S(2)}) collective-permute-start(bf16[870,128]{1,0:T(8,128)(2,1)S(1)} %get-tuple-element.35), channel_id=1, source_target_pairs={{2,0},{4,2},{6,4},{8,6},{10,8},{12,10},{14,12},{16,14},{18,16},{20... | collective-permute-start | bytes 668168 | tf_op jit(solution)/shard_map/ppermute | solution.py:21
  82.7 1.8 %copy-start = (f32[7168,128]{1,0:T(8,128)}, f32[7168,128]{1,0:T(8,128)S(1)}, u32[]{:S(2)}) copy-start(f32[7168,128]{1,0:T(8,128)S(1)} %get-tuple-element.36.before) | copy-start | bytes 11010052
  84.5 8.0 %collective-permute-start.4 = (bf16[870,128]{1,0:T(8,128)(2,1)S(1)}, bf16[870,128]{1,0:T(8,128)(2,1)S(1)}, u32[]{:S(2)}, u32[]{:S(2)}) collective-permute-start(bf16[870,128]{1,0:T(8,128)(2,1)S(1)} %get-tuple-element.37), channel_id=1, source_target_pairs={{0,2},{2,4},{4,6},{6,8},{8,10},{10,12},{12,14},{14,16},{16,18},{18... | collective-permute-start | bytes 668168 | tf_op jit(solution)/shard_map/ppermute | solution.py:21
  91.1 3.4 %collective-permute-start.5 = (bf16[870,128]{1,0:T(8,128)(2,1)S(1)}, bf16[870,128]{1,0:T(8,128)(2,1)S(1)}, u32[]{:S(2)}, u32[]{:S(2)}) collective-permute-start(bf16[870,128]{1,0:T(8,128)(2,1)S(1)} %get-tuple-element.38), channel_id=1, source_target_pairs={{2,0},{4,2},{6,4},{8,6},{10,8},{12,10},{14,12},{16,14},{18,16},{20... | collective-permute-start | bytes 668168 | tf_op jit(solution)/shard_map/ppermute | solution.py:21
  94.5 2.0 %copy-start.1 = (f32[7168,128]{1,0:T(8,128)S(1)}, f32[7168,128]{1,0:T(8,128)}, u32[]{:S(2)}) copy-start(f32[7168,128]{1,0:T(8,128)} %copy-done) | copy-start | bytes 11010052
  100.2 1.8 %copy-start.2 = (f32[7168,128]{1,0:T(8,128)}, f32[7168,128]{1,0:T(8,128)S(1)}, u32[]{:S(2)}) copy-start(f32[7168,128]{1,0:T(8,128)S(1)} %get-tuple-element.39.before) | copy-start | bytes 11010052
  102.0 19.6 %collective-permute-start.11 = (bf16[1792,256]{1,0:T(8,128)(2,1)}, bf16[1792,256]{1,0:T(8,128)(2,1)S(1)}, u32[]{:S(2)}, u32[]{:S(2)}) collective-permute-start(bf16[1792,256]{1,0:T(8,128)(2,1)} %get-tuple-element.43), channel_id=1, source_target_pairs={{0,1},{1,0},{2,3},{3,2},{4,5},{5,4},{6,7},{7,6},{8,9},{9,8},{10,11... | collective-permute-start | bytes 2752520 | tf_op jit(solution)/shard_map/ppermute | solution.py:365
  103.5 2.0 %copy-start.3 = (f32[7168,128]{1,0:T(8,128)S(1)}, f32[7168,128]{1,0:T(8,128)}, u32[]{:S(2)}) copy-start(f32[7168,128]{1,0:T(8,128)} %copy-done.2) | copy-start | bytes 11010052
  107.3 0.9 copy-start.5
  108.3 0.9 copy-start.6
  109.2 5.9 %collective-permute-start.6 = (f32[128,256]{1,0:T(8,128)S(1)}, f32[128,256]{1,0:T(8,128)S(1)}, u32[]{:S(2)}, u32[]{:S(2)}) collective-permute-start(f32[128,256]{1,0:T(8,128)S(1)} %constant_dynamic-slice_fusion.9), channel_id=1, source_target_pairs={{0,2},{2,0},{4,6},{6,4},{8,10},{10,8},{12,14},{14,12},{16,18},{18,... | collective-permute-start | bytes 393224 | tf_op jit(solution)/shard_map/ppermute | solution.py:336
  115.2 12.5 %collective-permute-start.7 = (f32[32,256]{1,0:T(8,128)S(1)}, f32[32,256]{1,0:T(8,128)S(1)}, u32[]{:S(2)}, u32[]{:S(2)}) collective-permute-start(f32[32,256]{1,0:T(8,128)S(1)} %get-tuple-element.49), channel_id=1, source_target_pairs={{0,4},{2,6},{4,0},{6,2},{8,12},{10,14},{12,8},{14,10},{16,20},{18,... | collective-permute-start | bytes 98312 | tf_op jit(solution)/shard_map/ppermute | solution.py:336
  117.8 9.9 %collective-permute-start.8 = (f32[32,256]{1,0:T(8,128)S(1)}, f32[32,256]{1,0:T(8,128)S(1)}, u32[]{:S(2)}, u32[]{:S(2)}) collective-permute-start(f32[32,256]{1,0:T(8,128)S(1)} %get-tuple-element.51), channel_id=1, source_target_pairs={{0,8},{2,10},{4,12},{6,14},{8,0},{10,2},{12,4},{14,6},{16,24},{18,... | collective-permute-start | bytes 98312 | tf_op jit(solution)/shard_map/ppermute | solution.py:336
  119.4 8.3 %collective-permute-start.9 = (f32[32,256]{1,0:T(8,128)S(1)}, f32[32,256]{1,0:T(8,128)S(1)}, u32[]{:S(2)}, u32[]{:S(2)}) collective-permute-start(f32[32,256]{1,0:T(8,128)S(1)} %get-tuple-element.50), channel_id=1, source_target_pairs={{0,12},{2,14},{4,8},{6,10},{8,4},{10,6},{12,0},{14,2},{16,28},{18,... | collective-permute-start | bytes 98312 | tf_op jit(solution)/shard_map/ppermute | solution.py:336
  121.6 1.2 copy-start.7
  124.0 4.7 %collective-permute-start.12 = (f32[128,256]{1,0:T(8,128)S(1)}, f32[128,256]{1,0:T(8,128)S(1)}, u32[]{:S(2)}, u32[]{:S(2)}) collective-permute-start(f32[128,256]{1,0:T(8,128)S(1)} %constant_dynamic-slice_fusion.4), channel_id=1, source_target_pairs={{0,2},{2,0},{4,6},{6,4},{8,10},{10,8},{12,14},{14,12},{16,18},{18,... | collective-permute-start | bytes 393224 | tf_op jit(solution)/shard_map/ppermute | solution.py:336
  128.7 10.5 %collective-permute-start.13 = (f32[32,256]{1,0:T(8,128)S(1)}, f32[32,256]{1,0:T(8,128)S(1)}, u32[]{:S(2)}, u32[]{:S(2)}) collective-permute-start(f32[32,256]{1,0:T(8,128)S(1)} %get-tuple-element.52), channel_id=1, source_target_pairs={{0,4},{2,6},{4,0},{6,2},{8,12},{10,14},{12,8},{14,10},{16,20},{18,... | collective-permute-start | bytes 98312 | tf_op jit(solution)/shard_map/ppermute | solution.py:336
  133.3 5.9 %collective-permute-start.14 = (f32[32,256]{1,0:T(8,128)S(1)}, f32[32,256]{1,0:T(8,128)S(1)}, u32[]{:S(2)}, u32[]{:S(2)}) collective-permute-start(f32[32,256]{1,0:T(8,128)S(1)} %get-tuple-element.54), channel_id=1, source_target_pairs={{0,8},{2,10},{4,12},{6,14},{8,0},{10,2},{12,4},{14,6},{16,24},{18,... | collective-permute-start | bytes 98312 | tf_op jit(solution)/shard_map/ppermute | solution.py:336
  134.8 4.9 %collective-permute-start.15 = (f32[32,256]{1,0:T(8,128)S(1)}, f32[32,256]{1,0:T(8,128)S(1)}, u32[]{:S(2)}, u32[]{:S(2)}) collective-permute-start(f32[32,256]{1,0:T(8,128)S(1)} %get-tuple-element.53), channel_id=1, source_target_pairs={{0,12},{2,14},{4,8},{6,10},{8,4},{10,6},{12,0},{14,2},{16,28},{18,... | collective-permute-start | bytes 98312 | tf_op jit(solution)/shard_map/ppermute | solution.py:336
  136.2 5.8 %collective-permute-start.10 = (f32[16,256]{1,0:T(8,128)S(1)}, f32[16,256]{1,0:T(8,128)S(1)}, u32[]{:S(2)}, u32[]{:S(2)}) collective-permute-start(f32[16,256]{1,0:T(8,128)S(1)} %constant_dynamic-slice_fusion.5), channel_id=1, source_target_pairs={{0,16},{2,18},{4,20},{6,22},{8,24},{10,26},{12,28},{14,30},{16,0},... | collective-permute-start | bytes 49160 | tf_op jit(solution)/shard_map/ppermute | solution.py:336
  139.8 4.7 %collective-permute-start.16 = (f32[16,256]{1,0:T(8,128)S(1)}, f32[16,256]{1,0:T(8,128)S(1)}, u32[]{:S(2)}, u32[]{:S(2)}) collective-permute-start(f32[16,256]{1,0:T(8,128)S(1)} %constant_dynamic-slice_fusion), channel_id=1, source_target_pairs={{0,16},{2,18},{4,20},{6,22},{8,24},{10,26},{12,28},{14,30},{16,0},... | collective-permute-start | bytes 49160 | tf_op jit(solution)/shard_map/ppermute | solution.py:336
  144.5 4.0 %collective-permute-start.17 = (f32[2,16,256]{2,1,0:T(8,128)S(1)}, f32[2,16,256]{2,1,0:T(8,128)S(1)}, u32[]{:S(2)}, u32[]{:S(2)}) collective-permute-start(f32[2,16,256]{2,1,0:T(8,128)S(1)} %pad_maximum_fusion.1), channel_id=1, source_target_pairs={{0,1},{1,0},{2,3},{3,2},{4,5},{5,4},{6,7},{7,6},{8,9},{9,8},{10,11... | collective-permute-start | bytes 98312 | tf_op jit(solution)/shard_map/ppermute | solution.py:386
  148.6 5.7 %collective-permute-start.18 = (f32[3,16,256]{2,1,0:T(8,128)S(1)}, f32[3,16,256]{2,1,0:T(8,128)S(1)}, u32[]{:S(2)}, u32[]{:S(2)}) collective-permute-start(f32[3,16,256]{2,1,0:T(8,128)S(1)} %get-tuple-element.55), channel_id=1, source_target_pairs={{0,16},{2,18},{4,20},{6,22},{8,24},{10,26},{12,28},{14,30},{16,0},... | collective-permute-start | bytes 147464 | tf_op jit(solution)/shard_map/ppermute | solution.py:353
  151.0 20.1 %collective-permute-start.24 = (bf16[1408,256]{1,0:T(8,128)(2,1)S(1)}, bf16[1408,256]{1,0:T(8,128)(2,1)S(1)}, u32[]{:S(2)}, u32[]{:S(2)}) collective-permute-start(bf16[1408,256]{1,0:T(8,128)(2,1)S(1)} %slice.13), channel_id=1, source_target_pairs={{0,1},{1,0},{2,3},{3,2},{4,5},{5,4},{6,7},{7,6},{8,9},{9,8},{10,11... | collective-permute-start | bytes 2162696 | tf_op jit(solution)/shard_map/ppermute | solution.py:388
  154.2 4.7 %collective-permute-start.19 = (f32[3,32,256]{2,1,0:T(8,128)S(1)}, f32[3,32,256]{2,1,0:T(8,128)S(1)}, u32[]{:S(2)}, u32[]{:S(2)}) collective-permute-start(f32[3,32,256]{2,1,0:T(8,128)S(1)} %constant_dynamic-update-slice_fusion.6), channel_id=1, source_target_pairs={{0,4},{2,6},{4,0},{6,2},{8,12},{10,14},{12,8},{14,10},{16,20},{18,... | collective-permute-start | bytes 294920 | tf_op jit(solution)/shard_map/ppermute | solution.py:353
  156.0 4.6 %collective-permute-start.20 = (f32[3,32,256]{2,1,0:T(8,128)S(1)}, f32[3,32,256]{2,1,0:T(8,128)S(1)}, u32[]{:S(2)}, u32[]{:S(2)}) collective-permute-start(f32[3,32,256]{2,1,0:T(8,128)S(1)} %constant_dynamic-update-slice_fusion.6), channel_id=1, source_target_pairs={{0,8},{2,10},{4,12},{6,14},{8,0},{10,2},{12,4},{14,6},{16,24},{18,... | collective-permute-start | bytes 294920 | tf_op jit(solution)/shard_map/ppermute | solution.py:353
  156.3 5.5 %collective-permute-start.21 = (f32[3,32,256]{2,1,0:T(8,128)S(1)}, f32[3,32,256]{2,1,0:T(8,128)S(1)}, u32[]{:S(2)}, u32[]{:S(2)}) collective-permute-start(f32[3,32,256]{2,1,0:T(8,128)S(1)} %constant_dynamic-update-slice_fusion.6), channel_id=1, source_target_pairs={{0,12},{2,14},{4,8},{6,10},{8,4},{10,6},{12,0},{14,2},{16,28},{18,... | collective-permute-start | bytes 294920 | tf_op jit(solution)/shard_map/ppermute | solution.py:353
  161.8 2.8 %collective-permute-start.22 = (f32[3,128,256]{2,1,0:T(8,128)S(1)}, f32[3,128,256]{2,1,0:T(8,128)S(1)}, u32[]{:S(2)}, u32[]{:S(2)}) collective-permute-start(f32[3,128,256]{2,1,0:T(8,128)S(1)} %constant_dynamic-update-slice_fusion.2), channel_id=1, source_target_pairs={{0,2},{2,0},{4,6},{6,4},{8,10},{10,8},{12,14},{14,12},{16,18},{18,... | collective-permute-start | bytes 1179656 | tf_op jit(solution)/shard_map/ppermute | solution.py:353
  162.8 8.3 %collective-permute-start.23 = (bf16[384,256]{1,0:T(8,128)(2,1)S(1)}, bf16[384,256]{1,0:T(8,128)(2,1)S(1)}, u32[]{:S(2)}, u32[]{:S(2)}) collective-permute-start(bf16[384,256]{1,0:T(8,128)(2,1)S(1)} %slice.16), channel_id=1, source_target_pairs={{0,1},{1,0},{2,3},{3,2},{4,5},{5,4},{6,7},{7,6},{8,9},{9,8},{10,11... | collective-permute-start | bytes 589832 | tf_op jit(solution)/shard_map/ppermute | solution.py:383

commit v4 on v3

--- a/solution.py
+++ b/solution.py
@@ -10,8 +10,8 @@
 NS_ITERS = 3
 LN = 3480
 LANES = 128
-BATCH = 32
-SPAN = 256
+BATCH = 16
+SPAN = 128
 WIDTH = 256
 
 
@@ -45,7 +45,7 @@
         body(whole * size, rest)
 
 
-def add_faces(field, came, wide, ids, scale):
+def add_faces(field, came, wide, ids, scale, pot=None, total=None):
     count = ids.shape[0] // 2
     tiles = wide.shape[0] // count
     for side in range(2):
@@ -55,29 +55,38 @@
             rows = [pl.ds(ids[side * count + base + i], tiles) for i in range(size)]
             old = [field[row, :] for row in rows]
             new = [old[i] + wide[pl.ds((base + i) * tiles, tiles), :] for i in range(size)]
+            if total is not None:
+                diagonal = [pot[rows[i], :] * rounded(new[i]) for i in range(size)]
             for i in range(size):
                 field[rows[i], :] = new[i]
+                if total is not None:
+                    total[rows[i], :] = diagonal[i]
 
         batches(count, BATCH, add)
 
 
+def rounded(x):
+    return x.astype(jnp.bfloat16).astype(jnp.float32)
+
+
 def slope(bounds, times):
-    return (2.0 * times) / jnp.full((1, LANES), bounds[1] - bounds[0], jnp.float32)
+    return (2.0 * times) / jnp.full((1, LANES), bounds[bounds.shape[0] - 1] - bounds[bounds.shape[0] - 2], jnp.float32)
 
 
 def apply_kernel(step, *refs):
     if step == 0:
-        (conn, ids, scales, bounds, pot_row, stiff, start,
-         field, rounded, below, above, pot, total, gathered, products, wide) = refs
+        (conn, ids, scales, at, pot_row, stiff_in, start,
+         field, total, below, above, pot, stiff, gathered, products, wide) = refs
     else:
-        (conn, ids, scales, bounds, pot, stiff, before, older, came_low, came_high,
-         field, rounded, below, above, total, gathered, products, wide) = refs
+        (conn, ids, scales, at, pot, stiff, _, _, came_low, came_high,
+         field, total, below, above, gathered, products, wide) = refs
     dofs = stiff.shape[0]
     cells = conn.shape[0] // dofs
     count = ids.shape[0] // 2
     tiles = gathered.shape[0] // dofs
     nodes = field.shape[0] // tiles
     if step == 0:
+        stiff[...] = stiff_in[...].T
         width = 512
         for k in range(nodes // width):
             piece = start[:, k * width:(k + 1) * width].astype(jnp.float32)
@@ -85,19 +94,13 @@
             turned = jnp.where(node < LN, piece, 0.0).T
             spread = jnp.broadcast_to(pot_row[:, k * width:(k + 1) * width], (LANES, width)).T
             for j in range(tiles):
-                field[pl.ds(k * width * tiles + j, width, tiles), :] = turned[:, j * LANES:(j + 1) * LANES]
-                pot[pl.ds(k * width * tiles + j, width, tiles), :] = spread
+                rows = pl.ds(k * width * tiles + j, width, tiles)
+                value = turned[:, j * LANES:(j + 1) * LANES]
+                field[rows, :] = value
+                pot[rows, :] = spread
+                total[rows, :] = spread * value
     else:
-        add_faces(field, (came_low, came_high), wide, ids, slope(bounds, min(step, 2)))
-
-    def begin(g, carry):
-        rows = pl.ds(pl.multiple_of(g * SPAN, SPAN), SPAN)
-        low = field[rows, :].astype(jnp.bfloat16)
-        rounded[rows, :] = low
-        total[rows, :] = pot[rows, :] * low.astype(jnp.float32)
-        return carry
-
-    lax.fori_loop(0, field.shape[0] // SPAN, begin, 0)
+        add_faces(field, (came_low, came_high), wide, ids, slope(scales, min(step, 2)), pot, total)
 
     def gather(cell, base, size):
         for i in range(size):
@@ -133,18 +136,28 @@
 
         batches(count, BATCH, take)
         faces[...] = wide[...].astype(faces.dtype)
-    center = (bounds[1] + bounds[0]) * 0.5
+
+
+def settle_kernel(step, last, *refs):
+    if step == 0:
+        bounds, pot, current, summed, out, total = refs
+    else:
+        bounds, pot, current, summed, older, out, *total = refs
+        total = total[0] if total else None
+    center = (bounds[bounds.shape[0] - 1] + bounds[bounds.shape[0] - 2]) * 0.5
     rate = slope(bounds, min(step + 1, 2))
 
-    def end(g, carry):
+    def some(g, carry):
         rows = pl.ds(pl.multiple_of(g * SPAN, SPAN), SPAN)
-        value = rate * (total[rows, :] - center * rounded[rows, :].astype(jnp.float32))
+        value = rate * (summed[rows, :] - center * rounded(current[rows, :]))
         if step:
-            value = value - older[rows, :].astype(jnp.float32)
-        field[rows, :] = value
+            value = value - rounded(older[rows, :])
+        out[rows, :] = value
+        if not last:
+            total[rows, :] = pot[rows, :] * rounded(value)
         return carry
 
-    lax.fori_loop(0, field.shape[0] // SPAN, end, 0)
+    lax.fori_loop(0, current.shape[0] // SPAN, some, 0)
 
 
 def node_rows(field, start, width, tiles):
@@ -233,23 +246,23 @@
     row = lax.broadcasted_iota(jnp.int32, whole.shape, 0)
     column = lax.broadcasted_iota(jnp.int32, whole.shape, 1)
     diagonal = jnp.where(row == column, 1.5, 0.0)
-    iterate = split(whole / scale)
-    factor = diagonal - 0.5 * (whole / scale)
-    inverse = split(factor)
+    iterate = whole / scale
+    factor = diagonal - 0.5 * iterate
+    inverse = None
     for sweep in range(1, NS_ITERS):
-        iterate = split(product(iterate, split(factor)))
-        factor = diagonal - 0.5 * product(inverse, iterate)
+        pieces = split(factor)
+        iterate = product(split(iterate), split(product(pieces, pieces)))
+        factor = diagonal - 0.5 * iterate
+        held[0], held[1] = pieces if inverse is None else inverse
         if sweep == NS_ITERS - 1:
-            held[0] = inverse[0]
-            held[1] = inverse[1]
             columns = held[0, :, pl.ds(start, size)], held[1, :, pl.ds(start, size)]
-            result = product(split(factor), columns)
+            result = product(split(factor), split(product(pieces, columns)))
         else:
-            inverse = split(product(split(factor), inverse))
+            inverse = pieces if inverse is None else split(product(pieces, inverse))
     out[...] = (result / jnp.sqrt(scale)).astype(jnp.bfloat16)
 
 
-def rotate_kernel(at, columns, turned, first, rest_a, rest_b, out):
+def rotate_kernel(at, columns, turned, first, rest, out):
     states, nodes = out.shape
     half = nodes // 2
     own = columns[pl.ds(pl.multiple_of(at[0] * states, states), states), :]
@@ -265,9 +278,7 @@
         out[:, pl.ds(base, width)] = value.astype(out.dtype)
 
     part_of(at[0] * half, first)
-    away = (1 - at[0]) * half
-    part_of(away, rest_a)
-    part_of(away + rest_a.shape[0], rest_b)
+    part_of((1 - at[0]) * half, rest)
 
 
 SMEM = pl.BlockSpec(memory_space=pltpu.SMEM)
@@ -292,26 +303,44 @@
         rows = pot.shape[0]
         tiles = fields[2].shape[0] // count
     face = struct((count * tiles, LANES), bf16)
-    out_shape = [struct((rows, LANES)), struct((rows, LANES), bf16), face, face]
+    whole = struct((rows, LANES))
+    out_shape = [whole, whole, face, face]
     if step == 0:
-        out_shape.append(struct((rows, LANES)))
+        out_shape += [whole, struct(stiff.shape, stiff.dtype)]
     return pl.pallas_call(
         functools.partial(apply_kernel, step),
         out_shape=out_shape,
         in_specs=[SMEM] * 4 + [VMEM] * (2 + len(fields)),
         out_specs=[VMEM] * len(out_shape),
         scratch_shapes=[
-            pltpu.VMEM((rows, LANES), f32),
             pltpu.VMEM((dofs * tiles, LANES), f32),
             pltpu.VMEM((dofs * tiles, LANES), f32),
             pltpu.VMEM((count * tiles, LANES), f32),
         ],
-        input_output_aliases={6: 0} if step else {},
+        input_output_aliases={6: 0, 7: 1} if step else {},
         compiler_params=limit(26),
         name="apply",
     )(*tables, pot, stiff, *fields)
 
 
+def settle_call(step, last, bounds, pot, current, total, older=None):
+    whole = struct(current.shape)
+    fields = [current, total] + ([older] if step else [])
+    aliases = {4: 0} if step else {}
+    if not last:
+        aliases[3] = 1
+    return pl.pallas_call(
+        functools.partial(settle_kernel, step, last),
+        out_shape=[whole] if last else [whole, whole],
+        in_specs=[SMEM] + [VMEM] * (1 + len(fields)),
+        out_specs=[VMEM] * (1 if last else 2),
+        input_output_aliases=aliases,
+        compiler_params=limit(26),
+        cost_estimate=pl.CostEstimate(flops=8 * 10**9, bytes_accessed=10**7, transcendentals=0),
+        name="settle",
+    )(bounds, pot, *fields)
+
+
 def groups_of(devices):
     bits = devices.bit_length() - 1
     return [list(range(b, min(b + 2, bits))) if b else [0] for b in [0] + list(range(1, bits, 2))][:bits]
@@ -322,16 +351,15 @@
         yield m, sum(((m >> i) & 1) << bit for i, bit in enumerate(group))
 
 
-def code_of(group):
-    at = lax.axis_index("dom")
-    return sum(((at >> bit) & 1) << i for i, bit in enumerate(group))
-
-
-def sum_scatter(x):
+def code_of(group, here):
+    return sum(((here >> bit) & 1) << i for i, bit in enumerate(group))
+
+
+def sum_scatter(x, here):
     devices = lax.axis_size("dom")
     for group in groups_of(devices):
         size = x.shape[-2] >> len(group)
-        code = code_of(group)
+        code = code_of(group, here)
         came = [
             lax.ppermute(
                 lax.dynamic_slice_in_dim(x, (code ^ m) * size, size, x.ndim - 2),
@@ -344,11 +372,11 @@
     return x
 
 
-def gather_all(x):
+def gather_all(x, here):
     devices = lax.axis_size("dom")
     for group in reversed(groups_of(devices)):
         size = x.shape[-2]
-        code = code_of(group)
+        code = code_of(group, here)
         pieces = [(0, x)] + [
             (m, lax.ppermute(x, "dom", [(i, i ^ mask) for i in range(devices)])) for m, mask in plan(group)
         ]
@@ -372,23 +400,22 @@
         compiler_params=limit(26), name="turn",
         cost_estimate=pl.CostEstimate(flops=4 * 10**9, bytes_accessed=10**7, transcendentals=0),
     )(ids, at, field)
-    own_sum = sum_scatter(gram)
+    place, gram = lax.optimization_barrier((at, gram))
+    here = place[1]
+    own_sum = sum_scatter(gram, here)
     cross = pl.pallas_call(
         cross_kernel,
         out_shape=struct((states, states)),
         in_specs=[SMEM, VMEM, VMEM], out_specs=VMEM, compiler_params=limit(16), name="cross",
     )(at, own_masked, came)
-    first_rows = half // 4 // LANES * LANES
-    rest, cross = lax.optimization_barrier((own, cross))
-    rest_a = lax.ppermute(rest[:first_rows], "st", swap)
-    cross_sum = sum_scatter(cross)
+    with jax.named_scope("rest"):
+        rest = lax.ppermute(own, "st", swap)
+    cross_sum = sum_scatter(cross, here)
     pair = jnp.stack([own_sum, cross_sum])
     theirs = lax.ppermute(pair, "st", swap)
-    later, theirs = lax.optimization_barrier((rest[first_rows:], theirs))
-    rest_b = lax.ppermute(later, "st", swap)
-    lower = at[0] == 0
+    lower = place[0] == 0
     blocks = gather_all(jnp.stack([
-        jnp.where(lower, pair[0], theirs[0]), jnp.where(lower, theirs[0], pair[0]), pair[1] + theirs[1]]))
+        jnp.where(lower, pair[0], theirs[0]), jnp.where(lower, theirs[0], pair[0]), pair[1] + theirs[1]]), here)
     columns = pl.pallas_call(
         root_kernel,
         out_shape=struct((2 * states, states), bf16),
@@ -399,8 +426,8 @@
     return pl.pallas_call(
         rotate_kernel,
         out_shape=struct((states, nodes), bf16),
-        in_specs=[SMEM] + [VMEM] * 5, out_specs=VMEM, compiler_params=limit(26), name="rotate",
-    )(at, columns, turned, came, rest_a, rest_b)
+        in_specs=[SMEM] + [VMEM] * 4, out_specs=VMEM, compiler_params=limit(26), name="rotate",
+    )(at, columns, turned, came, rest)
 
 
 def rotate_any(current, owned):
@@ -423,28 +450,35 @@
         start_states = jnp.pad(start_states, ((0, states - block_states), (0, 0)))
     conn = connectivity.reshape(-1) * tiles
     ids = shared_nodes.reshape(-1) * tiles
-    tables = conn, ids, cell_scale, filter_bounds
-    stiff = stiffness.T
+    numbers = jnp.concatenate([cell_scale, filter_bounds])
     at = jnp.stack([lax.axis_index("st"), lax.axis_index("dom")])
 
     def exchange(low, high):
-        return passed_along(high, "dom", 1), passed_along(low, "dom", -1)
-
-    field, older, low, high, pot = apply_call(0, tables, potential[None, :], stiff, start_states)
-    for step in range(1, DEGREE):
-        field, newer, low, high = apply_call(
-            step, tables, pot, stiff, field, older, *exchange(low, high))
-        older = newer
+        with jax.named_scope("halo"):
+            return passed_along(high, "dom", 1), passed_along(low, "dom", -1)
+
+    older = None
+    current, total, low, high, pot, stiff = apply_call(
+        0, (conn, ids, numbers, at), potential[None, :], stiffness, start_states)
+    for step in range(DEGREE):
+        came = exchange(low, high)
+        last = step == DEGREE - 1
+        following, *rest = settle_call(step, last, numbers, pot, current, total, older)
+        if not last:
+            older = current
+            current, total, low, high = apply_call(
+                step + 1, (conn, ids, numbers, at), pot, stiff, following, rest[0], *came)
+            continue
     field, away = pl.pallas_call(
         send_kernel,
-        out_shape=[struct(field.shape), struct((nodes // 2, states), jnp.bfloat16)],
+        out_shape=[struct(following.shape), struct((nodes // 2, states), jnp.bfloat16)],
         in_specs=[SMEM] * 3 + [VMEM] * 3,
         out_specs=[VMEM] * 2,
         scratch_shapes=[pltpu.VMEM((ids.shape[0] // 2 * tiles, LANES), jnp.float32)],
         input_output_aliases={3: 0},
-        compiler_params=limit(16),
+        compiler_params=limit(26),
         name="send",
-    )(ids, filter_bounds, at, field, *exchange(low, high))
+    )(ids, numbers, at, following, *came)
     devices = lax.axis_size("dom")
     if lax.axis_size("st") == 2 and states == block_states and devices & (devices - 1) == 0:
         return rotate_pair(field, away, ids, at, states, nodes)

time: 175 us -> 157 us (0.90)
  local copies, waits for them, and re-layouts: 17.9 us -> 7.27 us
  waiting for transfers between devices: 22.2 us -> 17.5 us
  Pallas kernels: 74.8 us -> 70.5 us
  between operations: 0.33 us -> 3.56 us
    pallas_call x3, Pallas kernels: 58.8 us -> 49.6 us  [apply_call(): pl.pallas_call(functools.partial(apply_kernel, step), out_shape=out_shape...]
    unnamed x22 -> x13, local copies, waits for them, and re-layouts: 14.8 us -> 5.57 us
    ppermute x6, waiting for transfers between devices: 8.22 us -> 2.79 us  [passed_along(): return lax.ppermute(x, axis, pairs)]
    pallas_call x1 -> x4, Pallas kernels: 3.64 us -> 8.71 us  [the longest x3 5.51 us: settle_call(): pl.pallas_call(functools.partial(settle_kernel, step, last), out_shape=[w...]
  transfers between devices with their start and end apart: 25 -> 24, of which waited for: 13 -> 13; matrix products, arithmetic and copies ran while one was open for 1% -> 1% of each run, Pallas kernels for 5% -> 9%
where the time goes in v4:
time: 157 us
  Pallas kernels  70.5 us (45%)
  starting transfers between devices  55.8 us (36%)
  waiting for transfers between devices  17.5 us (11%)
  local copies, waits for them, and re-layouts  7.27 us (5%)
  between operations  3.56 us (2%)
  other arithmetic  2.34 us (1%)
    pallas_call x3, Pallas kernels, apply_call(): pl.pallas_call(functools.partial(apply_kernel, step), out_shape=out_shape...  49.6 us
    ppermute x10, starting transfers between devices, sum_scatter(): lax.ppermute(lax.dynamic_slice_in_dim(x, (code ^ m) * size, size, x.ndim...  25.7 us
    ppermute x6, starting transfers between devices, passed_along(): return lax.ppermute(x, axis, pairs)  19.2 us
    ppermute x5, waiting for transfers between devices, gather_all(): lax.ppermute(x, 'dom', [(i, i ^ mask) for i in range(devices)])  7.09 us
    pallas_call x1, Pallas kernels, rotate_pair(): pl.pallas_call(root_kernel, out_shape=struct((2 * states, states), bf16),...  6.46 us
    ppermute x5, starting transfers between devices, gather_all(): lax.ppermute(x, 'dom', [(i, i ^ mask) for i in range(devices)])  6.09 us
    unnamed x13, local copies, waits for them, and re-layouts  5.57 us
    pallas_call x3, Pallas kernels, settle_call(): pl.pallas_call(functools.partial(settle_kernel, step, last), out_shape=[w...  5.51 us
  transfers between devices with their start and end apart: 24, of which 13 were waited for; matrix products, arithmetic and copies ran while one was open for 1% of the time, Pallas kernels for 9%

profile of v4, /device:TPU:0, one launch (start us, length us, event | category | flops | bytes accessed | tf_op | source)
XLA Modules:
  0.0 156.9 jit_solution(1157780715435974668)
XLA Ops:
  0.0 0.7 broadcast_multiply_fusion
  0.7 0.1 mul.64.refs_1_.ids
  0.8 0.7 multiply_bitcast_fusion
  1.5 0.7 broadcast_in_dim.15.refs_4_
  2.2 0.1 pad_add_fusion.refs_3_.at
  2.3 0.7 pad_maximum_fusion.2.refs_2_.refs_0_.bounds
  3.1 1.5 copy-done
  4.6 1.0 copy-done.3
  5.6 15.6 %apply.3 = (f32[7168,128]{1,0:T(8,128)S(1)}, f32[7168,128]{1,0:T(8,128)S(1)}, bf16[870,128]{1,0:T(8,128)(2,1)S(1)}, bf16[870,128]{1,0:T(8,128)(2,1)S(1)}, f32[71...) custom-call(s32[4096]{0:T(1024)S(1)} %bitcast.35, s32[870]{0:T(1024)S(1)} %mul.64.refs_1_.ids, ...), custom_call_target="tpu_custom_call" | custom-call | tf_op jit(solution)/shard_map/apply/pallas_call | solution.py:310
  21.2 2.4 %collective-permute-start = (bf16[870,128]{1,0:T(8,128)(2,1)S(1)}, bf16[870,128]{1,0:T(8,128)(2,1)S(1)}, u32[]{:S(2)}, u32[]{:S(2)}) collective-permute-start(bf16[870,128]{1,0:T(8,128)(2,1)S(1)} %get-tuple-element.37), channel_id=1, source_target_pairs={{0,2},{2,4},{4,6},{6,8},{8,10},{10,12},{12,14},{14,16},{16,18},{18... | collective-permute-start | bytes 668168 | tf_op jit(solution)/shard_map/halo/ppermute | solution.py:21
  23.6 1.3 collective-permute-start.1
  24.9 1.8 %settle.3 = (f32[7168,128]{1,0:T(8,128)S(1)}, f32[7168,128]{1,0:T(8,128)S(1)}) custom-call(f32[10]{0:T(128)S(1)} %pad_maximum_fusion.2.refs_2_.refs_0_.bounds, f32[7168,128]{1,0:T(8,128)S(1)} %get-tuple-element.31.refs_1_.refs_4_, f32[7168,128]{1,0:T(8,128)S(1)} %get-tuple-element.33.refs_2_.refs_4_, ...), custom_call_target="tpu_custom_call", output_to_operand_aliasing={{1}: (3, {})} | custom-call | flops 8000000000 | bytes 10000000 | tf_op jit(solution)/shard_map/settle/pallas_call | solution.py:332
  26.7 0.0 collective-permute-done.refs_8_
  26.7 2.4 %collective-permute-done.1.refs_9_ = bf16[870,128]{1,0:T(8,128)(2,1)S(1)} collective-permute-done((bf16[870,128]{1,0:T(8,128)(2,1)S(1)}, bf16[870,128]{1,0:T(8,128)(2,1)S(1)}, u32[]{:S(2)}, u32[]{:S(2)}) %collective-permute-start.1) | collective-permute-done | bytes 222752 | tf_op jit(solution)/shard_map/halo/ppermute | solution.py:21
  29.1 17.0 %apply.4 = (f32[7168,128]{1,0:T(8,128)S(1)}, f32[7168,128]{1,0:T(8,128)S(1)}, bf16[870,128]{1,0:T(8,128)(2,1)S(1)}, bf16[870,128]{1,0:T(8,128)(2,1)S(1)}) custom-call(s32[4096]{0:T(1024)S(1)} %bitcast.36, s32[870]{0:T(1024)S(1)} %mul.64.refs_1_.ids, f32[10]{0:T(128)S(1)} %pad_maximum_fusion.2.refs_2_.refs_0_.bounds, ...), custom_call_target="tpu_custom_call", output_to_operand_aliasing={{0}: (6, {}), {1}: (7, {})} | custom-call | tf_op jit(solution)/shard_map/apply/pallas_call | solution.py:310
  46.1 6.3 %collective-permute-start.2 = (bf16[870,128]{1,0:T(8,128)(2,1)S(1)}, bf16[870,128]{1,0:T(8,128)(2,1)S(1)}, u32[]{:S(2)}, u32[]{:S(2)}) collective-permute-start(bf16[870,128]{1,0:T(8,128)(2,1)S(1)} %get-tuple-element.43), channel_id=1, source_target_pairs={{0,2},{2,4},{4,6},{6,8},{8,10},{10,12},{12,14},{14,16},{16,18},{18... | collective-permute-start | bytes 668168 | tf_op jit(solution)/shard_map/halo/ppermute | solution.py:21
  52.5 1.3 collective-permute-start.3
  53.8 2.0 %settle.4 = (f32[7168,128]{1,0:T(8,128)S(1)}, f32[7168,128]{1,0:T(8,128)S(1)}) custom-call(f32[10]{0:T(128)S(1)} %pad_maximum_fusion.2.refs_2_.refs_0_.bounds, f32[7168,128]{1,0:T(8,128)S(1)} %get-tuple-element.31.refs_1_.refs_4_, f32[7168,128]{1,0:T(8,128)S(1)} %get-tuple-element.39.refs_2_.refs_4_, ...), custom_call_target="tpu_custom_call", output_to_operand_aliasing={{0}: (4, {}), {1}: (3, {})} | custom-call | flops 8000000000 | bytes 10000000 | tf_op jit(solution)/shard_map/settle/pallas_call | solution.py:332
  55.8 0.1 collective-permute-done.3.refs_9_
  55.8 17.0 %apply.5 = (f32[7168,128]{1,0:T(8,128)S(1)}, f32[7168,128]{1,0:T(8,128)S(1)}, bf16[870,128]{1,0:T(8,128)(2,1)S(1)}, bf16[870,128]{1,0:T(8,128)(2,1)S(1)}) custom-call(s32[4096]{0:T(1024)S(1)} %bitcast.37, s32[870]{0:T(1024)S(1)} %mul.64.refs_1_.ids, f32[10]{0:T(128)S(1)} %pad_maximum_fusion.2.refs_2_.refs_0_.bounds, ...), custom_call_target="tpu_custom_call", output_to_operand_aliasing={{0}: (6, {}), {1}: (7, {})} | custom-call | tf_op jit(solution)/shard_map/apply/pallas_call | solution.py:310
  72.8 6.6 %collective-permute-start.4 = (bf16[870,128]{1,0:T(8,128)(2,1)S(1)}, bf16[870,128]{1,0:T(8,128)(2,1)S(1)}, u32[]{:S(2)}, u32[]{:S(2)}) collective-permute-start(bf16[870,128]{1,0:T(8,128)(2,1)S(1)} %get-tuple-element.47), channel_id=1, source_target_pairs={{0,2},{2,4},{4,6},{6,8},{8,10},{10,12},{12,14},{14,16},{16,18},{18... | collective-permute-start | bytes 668168 | tf_op jit(solution)/shard_map/halo/ppermute | solution.py:21
  79.4 1.3 collective-permute-start.5
  80.7 1.7 %settle.5.before = f32[7168,128]{1,0:T(8,128)S(1)} custom-call(f32[10]{0:T(128)S(1)} %pad_maximum_fusion.2.refs_2_.refs_0_.bounds, f32[7168,128]{1,0:T(8,128)S(1)} %get-tuple-element.31.refs_1_.refs_4_, f32[7168,128]{1,0:T(8,128)S(1)} %get-tuple-element.45.refs_2_, f32[7168,128]{1,0:T(8,128)S(1)} %get-tuple-element.46.refs_3_, ...), custom_call_target="tpu_custom_call", output_to_operand_aliasing={{}: (4, {})} | custom-call | flops 8000000000 | bytes 10000000 | tf_op jit(solution)/shard_map/settle/pallas_call | solution.py:332
  82.5 0.4 collective-permute-done.5.came_high
  82.8 3.2 %send.1 = (f32[7168,128]{1,0:T(8,128)S(1)}, bf16[1792,256]{1,0:T(8,128)(2,1)}) custom-call(s32[870]{0:T(1024)S(1)} %mul.64.refs_1_.ids, f32[10]{0:T(128)S(1)} %pad_maximum_fusion.2.refs_2_.refs_0_.bounds, s32[2]{0:T(128)S(1)} %pad_add_fusion.refs_3_.at, f32[7168,128]{1,0:T(8,128)S(1)} %settle.5.before, ...), custom_call_target="tpu_custom_call", output_to_operand_aliasing={{0}: (3, {})} | custom-call | tf_op jit(solution)/shard_map/send/pallas_call | solution.py:472
  86.0 1.5 collective-permute-start.11
  87.5 1.8 %turn.1 = (f32[7168,128]{1,0:T(8,128)S(1)}, bf16[256,3584]{1,0:T(8,128)(2,1)S(1)}, bf16[1792,256]{1,0:T(8,128)(2,1)S(1)}, bf16[256,1792]{1,0:T(8,128)(2,1)S(1)}, f32[256,256]{1,0:T(8,128)S(1)}) custom-call(s32[870]{0:T(1024)S(1)} %mul.64.refs_1_.ids, s32[2]{0:T(128)S(1)} %pad_add_fusion.refs_3_.at, ...), custom_call_target="tpu_custom_call", output_to_operand_aliasing={{0}: (2, {})} | custom-call | flops 4000000000 | bytes 10000000 | tf_op jit(solution)/shard_map/turn/pallas_call | solution.py:394
  89.3 0.9 copy-done.1
  90.2 0.9 copy-done.4
  91.2 0.6 fusion.3
  92.5 5.1 %collective-permute-start.6 = (f32[128,256]{1,0:T(8,128)S(1)}, f32[128,256]{1,0:T(8,128)S(1)}, u32[]{:S(2)}, u32[]{:S(2)}) collective-permute-start(f32[128,256]{1,0:T(8,128)S(1)} %constant_dynamic-slice_fusion.9), channel_id=1, source_target_pairs={{0,2},{2,0},{4,6},{6,4},{8,10},{10,8},{12,14},{14,12},{16,18},{18,... | collective-permute-start | bytes 393224 | tf_op jit(solution)/shard_map/ppermute | solution.py:364
  99.5 2.6 %collective-permute-start.7 = (f32[32,256]{1,0:T(8,128)S(1)}, f32[32,256]{1,0:T(8,128)S(1)}, u32[]{:S(2)}, u32[]{:S(2)}) collective-permute-start(f32[32,256]{1,0:T(8,128)S(1)} %get-tuple-element.57), channel_id=1, source_target_pairs={{0,4},{2,6},{4,0},{6,2},{8,12},{10,14},{12,8},{14,10},{16,20},{18,... | collective-permute-start | bytes 98312 | tf_op jit(solution)/shard_map/ppermute | solution.py:364
  102.1 1.6 %collective-permute-start.8 = (f32[32,256]{1,0:T(8,128)S(1)}, f32[32,256]{1,0:T(8,128)S(1)}, u32[]{:S(2)}, u32[]{:S(2)}) collective-permute-start(f32[32,256]{1,0:T(8,128)S(1)} %get-tuple-element.59), channel_id=1, source_target_pairs={{0,8},{2,10},{4,12},{6,14},{8,0},{10,2},{12,4},{14,6},{16,24},{18,... | collective-permute-start | bytes 98312 | tf_op jit(solution)/shard_map/ppermute | solution.py:364
  103.7 0.0 collective-permute-start.9
  103.7 1.9 %collective-permute-done.11.came.first = bf16[1792,256]{1,0:T(8,128)(2,1)S(1)} collective-permute-done((bf16[1792,256]{1,0:T(8,128)(2,1)}, bf16[1792,256]{1,0:T(8,128)(2,1)S(1)}, u32[]{:S(2)}, u32[]{:S(2)}) %collective-permute-start.11) | collective-permute-done | bytes 917536 | tf_op jit(solution)/shard_map/ppermute | solution.py:393
  105.6 1.2 copy-done.2
  106.8 1.0 cross.1
  107.8 3.8 %collective-permute-start.12 = (f32[128,256]{1,0:T(8,128)S(1)}, f32[128,256]{1,0:T(8,128)S(1)}, u32[]{:S(2)}, u32[]{:S(2)}) collective-permute-start(f32[128,256]{1,0:T(8,128)S(1)} %constant_dynamic-slice_fusion.4), channel_id=1, source_target_pairs={{0,2},{2,0},{4,6},{6,4},{8,10},{10,8},{12,14},{14,12},{16,18},{18,... | collective-permute-start | bytes 393224 | tf_op jit(solution)/shard_map/ppermute | solution.py:364
  111.5 0.0 collective-permute-done.9
  111.6 1.0 collective-permute-done.12
  112.5 4.6 %collective-permute-start.13 = (f32[32,256]{1,0:T(8,128)S(1)}, f32[32,256]{1,0:T(8,128)S(1)}, u32[]{:S(2)}, u32[]{:S(2)}) collective-permute-start(f32[32,256]{1,0:T(8,128)S(1)} %get-tuple-element.60), channel_id=1, source_target_pairs={{0,4},{2,6},{4,0},{6,2},{8,12},{10,14},{12,8},{14,10},{16,20},{18,... | collective-permute-start | bytes 98312 | tf_op jit(solution)/shard_map/ppermute | solution.py:364
  117.2 1.6 %collective-permute-start.14 = (f32[32,256]{1,0:T(8,128)S(1)}, f32[32,256]{1,0:T(8,128)S(1)}, u32[]{:S(2)}, u32[]{:S(2)}) collective-permute-start(f32[32,256]{1,0:T(8,128)S(1)} %get-tuple-element.62), channel_id=1, source_target_pairs={{0,8},{2,10},{4,12},{6,14},{8,0},{10,2},{12,4},{14,6},{16,24},{18,... | collective-permute-start | bytes 98312 | tf_op jit(solution)/shard_map/ppermute | solution.py:364
  118.8 1.3 collective-permute-start.15
  120.1 3.0 %collective-permute-start.10 = (f32[16,256]{1,0:T(8,128)S(1)}, f32[16,256]{1,0:T(8,128)S(1)}, u32[]{:S(2)}, u32[]{:S(2)}) collective-permute-start(f32[16,256]{1,0:T(8,128)S(1)} %constant_dynamic-slice_fusion.5), channel_id=1, source_target_pairs={{0,16},{2,18},{4,20},{6,22},{8,24},{10,26},{12,28},{14,30},{16,0},... | collective-permute-start | bytes 49160 | tf_op jit(solution)/shard_map/ppermute | solution.py:364
  123.1 0.0 collective-permute-done.13
  123.1 0.6 collective-permute-done.15
  123.7 2.1 %collective-permute-start.16 = (f32[16,256]{1,0:T(8,128)S(1)}, f32[16,256]{1,0:T(8,128)S(1)}, u32[]{:S(2)}, u32[]{:S(2)}) collective-permute-start(f32[16,256]{1,0:T(8,128)S(1)} %constant_dynamic-slice_fusion), channel_id=1, source_target_pairs={{0,16},{2,18},{4,20},{6,22},{8,24},{10,26},{12,28},{14,30},{16,0},... | collective-permute-start | bytes 49160 | tf_op jit(solution)/shard_map/ppermute | solution.py:364
  125.9 2.6 %collective-permute-done.16 = f32[16,256]{1,0:T(8,128)S(1)} collective-permute-done((f32[16,256]{1,0:T(8,128)S(1)}, f32[16,256]{1,0:T(8,128)S(1)}, u32[]{:S(2)}, u32[]{:S(2)}) %collective-permute-start.16) | collective-permute-done | bytes 16416 | tf_op jit(solution)/shard_map/ppermute | solution.py:364
  128.4 1.7 %collective-permute-start.17 = (f32[2,16,256]{2,1,0:T(8,128)S(1)}, f32[2,16,256]{2,1,0:T(8,128)S(1)}, u32[]{:S(2)}, u32[]{:S(2)}) collective-permute-start(f32[2,16,256]{2,1,0:T(8,128)S(1)} %pad_maximum_fusion.1), channel_id=1, source_target_pairs={{0,1},{1,0},{2,3},{3,2},{4,5},{5,4},{6,7},{7,6},{8,9},{9,8},{10,11... | collective-permute-start | bytes 98312 | tf_op jit(solution)/shard_map/ppermute | solution.py:415
  130.8 1.7 %collective-permute-done.17 = f32[2,16,256]{2,1,0:T(8,128)S(1)} collective-permute-done((f32[2,16,256]{2,1,0:T(8,128)S(1)}, f32[2,16,256]{2,1,0:T(8,128)S(1)}, u32[]{:S(2)}, u32[]{:S(2)}) %collective-permute-start.17) | collective-permute-done | bytes 32800 | tf_op jit(solution)/shard_map/ppermute | solution.py:415
  132.5 2.5 %collective-permute-start.18 = (f32[3,16,256]{2,1,0:T(8,128)S(1)}, f32[3,16,256]{2,1,0:T(8,128)S(1)}, u32[]{:S(2)}, u32[]{:S(2)}) collective-permute-start(f32[3,16,256]{2,1,0:T(8,128)S(1)} %get-tuple-element.63), channel_id=1, source_target_pairs={{0,16},{2,18},{4,20},{6,22},{8,24},{10,26},{12,28},{14,30},{16,0},... | collective-permute-start | bytes 147464 | tf_op jit(solution)/shard_map/ppermute | solution.py:381
  134.9 1.6 %collective-permute-start.23 = (bf16[1792,256]{1,0:T(8,128)(2,1)S(1)}, bf16[1792,256]{1,0:T(8,128)(2,1)S(1)}, u32[]{:S(2)}, u32[]{:S(2)}) collective-permute-start(bf16[1792,256]{1,0:T(8,128)(2,1)S(1)} %copy-done.5), channel_id=1, source_target_pairs={{0,1},{1,0},{2,3},{3,2},{4,5},{5,4},{6,7},{7,6},{8,9},{9,8},{10,11... | collective-permute-start | bytes 2752520 | tf_op jit(solution)/shard_map/rest/ppermute | solution.py:412
  136.6 1.6 %collective-permute-done.18 = f32[3,16,256]{2,1,0:T(8,128)S(1)} collective-permute-done((f32[3,16,256]{2,1,0:T(8,128)S(1)}, f32[3,16,256]{2,1,0:T(8,128)S(1)}, u32[]{:S(2)}, u32[]{:S(2)}) %collective-permute-start.18) | collective-permute-done | bytes 49184 | tf_op jit(solution)/shard_map/ppermute | solution.py:381
  138.2 1.7 %collective-permute-start.19 = (f32[3,32,256]{2,1,0:T(8,128)S(1)}, f32[3,32,256]{2,1,0:T(8,128)S(1)}, u32[]{:S(2)}, u32[]{:S(2)}) collective-permute-start(f32[3,32,256]{2,1,0:T(8,128)S(1)} %constant_dynamic-update-slice_fusion.6), channel_id=1, source_target_pairs={{0,4},{2,6},{4,0},{6,2},{8,12},{10,14},{12,8},{14,10},{16,20},{18,... | collective-permute-start | bytes 294920 | tf_op jit(solution)/shard_map/ppermute | solution.py:381
  139.9 0.3 collective-permute-start.20
  140.2 1.5 collective-permute-start.21
  141.8 1.1 collective-permute-done.19
  142.9 1.6 %collective-permute-done.20 = f32[3,32,256]{2,1,0:T(8,128)S(1)} collective-permute-done((f32[3,32,256]{2,1,0:T(8,128)S(1)}, f32[3,32,256]{2,1,0:T(8,128)S(1)}, u32[]{:S(2)}, u32[]{:S(2)}) %collective-permute-start.20) | collective-permute-done | bytes 98336 | tf_op jit(solution)/shard_map/ppermute | solution.py:381
  144.5 1.2 collective-permute-done.21
  145.7 0.1 collective-permute-start.22
  145.8 0.1 broadcast_in_dim.12
  145.9 1.6 %collective-permute-done.22 = f32[3,128,256]{2,1,0:T(8,128)S(1)} collective-permute-done((f32[3,128,256]{2,1,0:T(8,128)S(1)}, f32[3,128,256]{2,1,0:T(8,128)S(1)}, u32[]{:S(2)}, u32[]{:S(2)}) %collective-permute-start.22) | collective-permute-done | bytes 393248 | tf_op jit(solution)/shard_map/ppermute | solution.py:381
  147.5 6.5 %root.1.columns = bf16[512,256]{1,0:T(8,128)(2,1)S(1)} custom-call(s32[2]{0:T(128)S(1)} %pad_add_fusion.refs_3_.at, f32[3,256,256]{2,1,0:T(8,128)S(1)} %constant_dynamic-update-slice_fusion.blocks), custom_call_target="tpu_custom_call" | custom-call | tf_op jit(solution)/shard_map/root/pallas_call | solution.py:419
  154.0 2.9 %rotate.1 = bf16[256,3584]{1,0:T(8,128)(2,1)} custom-call(s32[2]{0:T(128)S(1)} %pad_add_fusion.refs_3_.at, bf16[512,256]{1,0:T(8,128)(2,1)S(1)} %root.1.columns, bf16[256,3584]{1,0:T(8,128)(2,1)S(1)} %get-tuple-element.55.turned, bf16[1792,256]{1,0:T(8,128)(2,1)S(1)} %collective-permute-done.11.came.first, bf16[1792,256]{1,0:T(8,128)(2,1)S(1)} %collective-permute-done.23.rest), custom_call_target="tpu_custom_call" | custom-call | tf_op jit(solution)/shard_map/rotate/pallas_call | solution.py:426
  (40 shorter events, 0.4 us)
Async XLA Ops:
  3.1 1.5 copy-start
  4.6 1.0 copy-start.3
  21.2 5.5 %collective-permute-start = (bf16[870,128]{1,0:T(8,128)(2,1)S(1)}, bf16[870,128]{1,0:T(8,128)(2,1)S(1)}, u32[]{:S(2)}, u32[]{:S(2)}) collective-permute-start(bf16[870,128]{1,0:T(8,128)(2,1)S(1)} %get-tuple-element.37), channel_id=1, source_target_pairs={{0,2},{2,4},{4,6},{6,8},{8,10},{10,12},{12,14},{14,16},{16,18},{18... | collective-permute-start | bytes 668168 | tf_op jit(solution)/shard_map/halo/ppermute | solution.py:21
  23.6 5.5 %collective-permute-start.1 = (bf16[870,128]{1,0:T(8,128)(2,1)S(1)}, bf16[870,128]{1,0:T(8,128)(2,1)S(1)}, u32[]{:S(2)}, u32[]{:S(2)}) collective-permute-start(bf16[870,128]{1,0:T(8,128)(2,1)S(1)} %get-tuple-element.38), channel_id=1, source_target_pairs={{2,0},{4,2},{6,4},{8,6},{10,8},{12,10},{14,12},{16,14},{18,16},{20... | collective-permute-start | bytes 668168 | tf_op jit(solution)/shard_map/halo/ppermute | solution.py:21
  46.1 9.6 %collective-permute-start.2 = (bf16[870,128]{1,0:T(8,128)(2,1)S(1)}, bf16[870,128]{1,0:T(8,128)(2,1)S(1)}, u32[]{:S(2)}, u32[]{:S(2)}) collective-permute-start(bf16[870,128]{1,0:T(8,128)(2,1)S(1)} %get-tuple-element.43), channel_id=1, source_target_pairs={{0,2},{2,4},{4,6},{6,8},{8,10},{10,12},{12,14},{14,16},{16,18},{18... | collective-permute-start | bytes 668168 | tf_op jit(solution)/shard_map/halo/ppermute | solution.py:21
  52.5 3.4 %collective-permute-start.3 = (bf16[870,128]{1,0:T(8,128)(2,1)S(1)}, bf16[870,128]{1,0:T(8,128)(2,1)S(1)}, u32[]{:S(2)}, u32[]{:S(2)}) collective-permute-start(bf16[870,128]{1,0:T(8,128)(2,1)S(1)} %get-tuple-element.44), channel_id=1, source_target_pairs={{2,0},{4,2},{6,4},{8,6},{10,8},{12,10},{14,12},{16,14},{18,16},{20... | collective-permute-start | bytes 668168 | tf_op jit(solution)/shard_map/halo/ppermute | solution.py:21
  72.8 9.6 %collective-permute-start.4 = (bf16[870,128]{1,0:T(8,128)(2,1)S(1)}, bf16[870,128]{1,0:T(8,128)(2,1)S(1)}, u32[]{:S(2)}, u32[]{:S(2)}) collective-permute-start(bf16[870,128]{1,0:T(8,128)(2,1)S(1)} %get-tuple-element.47), channel_id=1, source_target_pairs={{0,2},{2,4},{4,6},{6,8},{8,10},{10,12},{12,14},{14,16},{16,18},{18... | collective-permute-start | bytes 668168 | tf_op jit(solution)/shard_map/halo/ppermute | solution.py:21
  79.4 3.4 %collective-permute-start.5 = (bf16[870,128]{1,0:T(8,128)(2,1)S(1)}, bf16[870,128]{1,0:T(8,128)(2,1)S(1)}, u32[]{:S(2)}, u32[]{:S(2)}) collective-permute-start(bf16[870,128]{1,0:T(8,128)(2,1)S(1)} %get-tuple-element.48), channel_id=1, source_target_pairs={{2,0},{4,2},{6,4},{8,6},{10,8},{12,10},{14,12},{16,14},{18,16},{20... | collective-permute-start | bytes 668168 | tf_op jit(solution)/shard_map/halo/ppermute | solution.py:21
  86.0 19.6 %collective-permute-start.11 = (bf16[1792,256]{1,0:T(8,128)(2,1)}, bf16[1792,256]{1,0:T(8,128)(2,1)S(1)}, u32[]{:S(2)}, u32[]{:S(2)}) collective-permute-start(bf16[1792,256]{1,0:T(8,128)(2,1)} %get-tuple-element.54), channel_id=1, source_target_pairs={{0,1},{1,0},{2,3},{3,2},{4,5},{5,4},{6,7},{7,6},{8,9},{9,8},{10,11... | collective-permute-start | bytes 2752520 | tf_op jit(solution)/shard_map/ppermute | solution.py:393
  89.3 0.9 copy-start.1
  90.2 0.9 copy-start.4
  92.5 7.0 %collective-permute-start.6 = (f32[128,256]{1,0:T(8,128)S(1)}, f32[128,256]{1,0:T(8,128)S(1)}, u32[]{:S(2)}, u32[]{:S(2)}) collective-permute-start(f32[128,256]{1,0:T(8,128)S(1)} %constant_dynamic-slice_fusion.9), channel_id=1, source_target_pairs={{0,2},{2,0},{4,6},{6,4},{8,10},{10,8},{12,14},{14,12},{16,18},{18,... | collective-permute-start | bytes 393224 | tf_op jit(solution)/shard_map/ppermute | solution.py:364
  99.5 12.0 %collective-permute-start.7 = (f32[32,256]{1,0:T(8,128)S(1)}, f32[32,256]{1,0:T(8,128)S(1)}, u32[]{:S(2)}, u32[]{:S(2)}) collective-permute-start(f32[32,256]{1,0:T(8,128)S(1)} %get-tuple-element.57), channel_id=1, source_target_pairs={{0,4},{2,6},{4,0},{6,2},{8,12},{10,14},{12,8},{14,10},{16,20},{18,... | collective-permute-start | bytes 98312 | tf_op jit(solution)/shard_map/ppermute | solution.py:364
  102.1 9.4 %collective-permute-start.8 = (f32[32,256]{1,0:T(8,128)S(1)}, f32[32,256]{1,0:T(8,128)S(1)}, u32[]{:S(2)}, u32[]{:S(2)}) collective-permute-start(f32[32,256]{1,0:T(8,128)S(1)} %get-tuple-element.59), channel_id=1, source_target_pairs={{0,8},{2,10},{4,12},{6,14},{8,0},{10,2},{12,4},{14,6},{16,24},{18,... | collective-permute-start | bytes 98312 | tf_op jit(solution)/shard_map/ppermute | solution.py:364
  103.7 7.8 %collective-permute-start.9 = (f32[32,256]{1,0:T(8,128)S(1)}, f32[32,256]{1,0:T(8,128)S(1)}, u32[]{:S(2)}, u32[]{:S(2)}) collective-permute-start(f32[32,256]{1,0:T(8,128)S(1)} %get-tuple-element.58), channel_id=1, source_target_pairs={{0,12},{2,14},{4,8},{6,10},{8,4},{10,6},{12,0},{14,2},{16,28},{18,... | collective-permute-start | bytes 98312 | tf_op jit(solution)/shard_map/ppermute | solution.py:364
  105.6 1.2 copy-start.2
  106.8 28.2 %copy-start.5 = (bf16[1792,256]{1,0:T(8,128)(2,1)S(1)}, bf16[1792,256]{1,0:T(8,128)(2,1)}, u32[]{:S(2)}) copy-start(bf16[1792,256]{1,0:T(8,128)(2,1)} %copy-done.4) | copy-start | bytes 2752516
  107.8 4.7 %collective-permute-start.12 = (f32[128,256]{1,0:T(8,128)S(1)}, f32[128,256]{1,0:T(8,128)S(1)}, u32[]{:S(2)}, u32[]{:S(2)}) collective-permute-start(f32[128,256]{1,0:T(8,128)S(1)} %constant_dynamic-slice_fusion.4), channel_id=1, source_target_pairs={{0,2},{2,0},{4,6},{6,4},{8,10},{10,8},{12,14},{14,12},{16,18},{18,... | collective-permute-start | bytes 393224 | tf_op jit(solution)/shard_map/ppermute | solution.py:364
  112.5 10.6 %collective-permute-start.13 = (f32[32,256]{1,0:T(8,128)S(1)}, f32[32,256]{1,0:T(8,128)S(1)}, u32[]{:S(2)}, u32[]{:S(2)}) collective-permute-start(f32[32,256]{1,0:T(8,128)S(1)} %get-tuple-element.60), channel_id=1, source_target_pairs={{0,4},{2,6},{4,0},{6,2},{8,12},{10,14},{12,8},{14,10},{16,20},{18,... | collective-permute-start | bytes 98312 | tf_op jit(solution)/shard_map/ppermute | solution.py:364
  117.2 5.9 %collective-permute-start.14 = (f32[32,256]{1,0:T(8,128)S(1)}, f32[32,256]{1,0:T(8,128)S(1)}, u32[]{:S(2)}, u32[]{:S(2)}) collective-permute-start(f32[32,256]{1,0:T(8,128)S(1)} %get-tuple-element.62), channel_id=1, source_target_pairs={{0,8},{2,10},{4,12},{6,14},{8,0},{10,2},{12,4},{14,6},{16,24},{18,... | collective-permute-start | bytes 98312 | tf_op jit(solution)/shard_map/ppermute | solution.py:364
  118.8 4.9 %collective-permute-start.15 = (f32[32,256]{1,0:T(8,128)S(1)}, f32[32,256]{1,0:T(8,128)S(1)}, u32[]{:S(2)}, u32[]{:S(2)}) collective-permute-start(f32[32,256]{1,0:T(8,128)S(1)} %get-tuple-element.61), channel_id=1, source_target_pairs={{0,12},{2,14},{4,8},{6,10},{8,4},{10,6},{12,0},{14,2},{16,28},{18,... | collective-permute-start | bytes 98312 | tf_op jit(solution)/shard_map/ppermute | solution.py:364
  120.1 5.8 %collective-permute-start.10 = (f32[16,256]{1,0:T(8,128)S(1)}, f32[16,256]{1,0:T(8,128)S(1)}, u32[]{:S(2)}, u32[]{:S(2)}) collective-permute-start(f32[16,256]{1,0:T(8,128)S(1)} %constant_dynamic-slice_fusion.5), channel_id=1, source_target_pairs={{0,16},{2,18},{4,20},{6,22},{8,24},{10,26},{12,28},{14,30},{16,0},... | collective-permute-start | bytes 49160 | tf_op jit(solution)/shard_map/ppermute | solution.py:364
  123.7 4.7 %collective-permute-start.16 = (f32[16,256]{1,0:T(8,128)S(1)}, f32[16,256]{1,0:T(8,128)S(1)}, u32[]{:S(2)}, u32[]{:S(2)}) collective-permute-start(f32[16,256]{1,0:T(8,128)S(1)} %constant_dynamic-slice_fusion), channel_id=1, source_target_pairs={{0,16},{2,18},{4,20},{6,22},{8,24},{10,26},{12,28},{14,30},{16,0},... | collective-permute-start | bytes 49160 | tf_op jit(solution)/shard_map/ppermute | solution.py:364
  128.4 4.0 %collective-permute-start.17 = (f32[2,16,256]{2,1,0:T(8,128)S(1)}, f32[2,16,256]{2,1,0:T(8,128)S(1)}, u32[]{:S(2)}, u32[]{:S(2)}) collective-permute-start(f32[2,16,256]{2,1,0:T(8,128)S(1)} %pad_maximum_fusion.1), channel_id=1, source_target_pairs={{0,1},{1,0},{2,3},{3,2},{4,5},{5,4},{6,7},{7,6},{8,9},{9,8},{10,11... | collective-permute-start | bytes 98312 | tf_op jit(solution)/shard_map/ppermute | solution.py:415
  132.5 5.7 %collective-permute-start.18 = (f32[3,16,256]{2,1,0:T(8,128)S(1)}, f32[3,16,256]{2,1,0:T(8,128)S(1)}, u32[]{:S(2)}, u32[]{:S(2)}) collective-permute-start(f32[3,16,256]{2,1,0:T(8,128)S(1)} %get-tuple-element.63), channel_id=1, source_target_pairs={{0,16},{2,18},{4,20},{6,22},{8,24},{10,26},{12,28},{14,30},{16,0},... | collective-permute-start | bytes 147464 | tf_op jit(solution)/shard_map/ppermute | solution.py:381
  134.9 19.0 %collective-permute-start.23 = (bf16[1792,256]{1,0:T(8,128)(2,1)S(1)}, bf16[1792,256]{1,0:T(8,128)(2,1)S(1)}, u32[]{:S(2)}, u32[]{:S(2)}) collective-permute-start(bf16[1792,256]{1,0:T(8,128)(2,1)S(1)} %copy-done.5), channel_id=1, source_target_pairs={{0,1},{1,0},{2,3},{3,2},{4,5},{5,4},{6,7},{7,6},{8,9},{9,8},{10,11... | collective-permute-start | bytes 2752520 | tf_op jit(solution)/shard_map/rest/ppermute | solution.py:412
  138.2 4.7 %collective-permute-start.19 = (f32[3,32,256]{2,1,0:T(8,128)S(1)}, f32[3,32,256]{2,1,0:T(8,128)S(1)}, u32[]{:S(2)}, u32[]{:S(2)}) collective-permute-start(f32[3,32,256]{2,1,0:T(8,128)S(1)} %constant_dynamic-update-slice_fusion.6), channel_id=1, source_target_pairs={{0,4},{2,6},{4,0},{6,2},{8,12},{10,14},{12,8},{14,10},{16,20},{18,... | collective-permute-start | bytes 294920 | tf_op jit(solution)/shard_map/ppermute | solution.py:381
  139.9 4.6 %collective-permute-start.20 = (f32[3,32,256]{2,1,0:T(8,128)S(1)}, f32[3,32,256]{2,1,0:T(8,128)S(1)}, u32[]{:S(2)}, u32[]{:S(2)}) collective-permute-start(f32[3,32,256]{2,1,0:T(8,128)S(1)} %constant_dynamic-update-slice_fusion.6), channel_id=1, source_target_pairs={{0,8},{2,10},{4,12},{6,14},{8,0},{10,2},{12,4},{14,6},{16,24},{18,... | collective-permute-start | bytes 294920 | tf_op jit(solution)/shard_map/ppermute | solution.py:381
  140.2 5.5 %collective-permute-start.21 = (f32[3,32,256]{2,1,0:T(8,128)S(1)}, f32[3,32,256]{2,1,0:T(8,128)S(1)}, u32[]{:S(2)}, u32[]{:S(2)}) collective-permute-start(f32[3,32,256]{2,1,0:T(8,128)S(1)} %constant_dynamic-update-slice_fusion.6), channel_id=1, source_target_pairs={{0,12},{2,14},{4,8},{6,10},{8,4},{10,6},{12,0},{14,2},{16,28},{18,... | collective-permute-start | bytes 294920 | tf_op jit(solution)/shard_map/ppermute | solution.py:381
  145.7 1.8 %collective-permute-start.22 = (f32[3,128,256]{2,1,0:T(8,128)S(1)}, f32[3,128,256]{2,1,0:T(8,128)S(1)}, u32[]{:S(2)}, u32[]{:S(2)}) collective-permute-start(f32[3,128,256]{2,1,0:T(8,128)S(1)} %constant_dynamic-update-slice_fusion.2), channel_id=1, source_target_pairs={{0,2},{2,0},{4,6},{6,4},{8,10},{10,8},{12,14},{14,12},{16,18},{18,... | collective-permute-start | bytes 1179656 | tf_op jit(solution)/shard_map/ppermute | solution.py:381

commit v5 on v4

--- a/solution.py
+++ b/solution.py
@@ -6,6 +6,7 @@
 from jax.experimental.pallas import tpu as pltpu
 from jax.sharding import PartitionSpec as P
 
+
 DEGREE = 3
 NS_ITERS = 3
 LN = 3480
@@ -15,9 +16,10 @@
 WIDTH = 256
 
 
-def passed_along(x, axis, by):
+def paired(x, axis, offset):
     devices = lax.axis_size(axis)
-    pairs = [(i, i + by) for i in range(devices) if 0 <= i + by < devices]
+    firsts = range(offset, devices - 1, 2)
+    pairs = [(i, i + 1) for i in firsts] + [(i + 1, i) for i in firsts]
     return lax.ppermute(x, axis, pairs)
 
 
@@ -26,7 +28,7 @@
     iterate = gram / frobenius
     identity = jnp.eye(gram.shape[0], dtype=jnp.float32)
     inverse = identity
-    for sweep in range(NS_ITERS):
+    for _ in range(NS_ITERS):
         factor = 1.5 * identity - 0.5 * jnp.dot(inverse, iterate, precision=lax.Precision.HIGHEST)
         iterate = jnp.dot(iterate, factor, precision=lax.Precision.HIGHEST)
         inverse = jnp.dot(factor, inverse, precision=lax.Precision.HIGHEST)
@@ -45,24 +47,27 @@
         body(whole * size, rest)
 
 
-def add_faces(field, came, wide, ids, scale, pot=None, total=None):
+def add_faces(field, came, wide, ids, at, scale):
     count = ids.shape[0] // 2
     tiles = wide.shape[0] // count
-    for side in range(2):
-        wide[...] = came[side][...].astype(jnp.float32) * scale
+    for slot in range(2):
+        wide[...] = came[slot][...].astype(jnp.float32) * scale
+        offset = side_of(slot, at) * count
 
         def add(base, size):
-            rows = [pl.ds(ids[side * count + base + i], tiles) for i in range(size)]
+            first = offset + base
+            rows = [pl.ds(ids[first + i], tiles) for i in range(size)]
             old = [field[row, :] for row in rows]
             new = [old[i] + wide[pl.ds((base + i) * tiles, tiles), :] for i in range(size)]
-            if total is not None:
-                diagonal = [pot[rows[i], :] * rounded(new[i]) for i in range(size)]
             for i in range(size):
                 field[rows[i], :] = new[i]
-                if total is not None:
-                    total[rows[i], :] = diagonal[i]
 
         batches(count, BATCH, add)
+
+
+def side_of(slot, at):
+    odd = at[1] % 2
+    return odd if slot else 1 - odd
 
 
 def rounded(x):
@@ -86,21 +91,21 @@
     tiles = gathered.shape[0] // dofs
     nodes = field.shape[0] // tiles
     if step == 0:
-        stiff[...] = stiff_in[...].T
         width = 512
-        for k in range(nodes // width):
+        pieces = nodes // width
+        for k in range(pieces):
+            spread = jnp.broadcast_to(pot_row[k * width:(k + 1) * width].reshape(1, width), (LANES, width)).T
             piece = start[:, k * width:(k + 1) * width].astype(jnp.float32)
             node = lax.broadcasted_iota(jnp.int32, piece.shape, 1) + k * width
             turned = jnp.where(node < LN, piece, 0.0).T
-            spread = jnp.broadcast_to(pot_row[:, k * width:(k + 1) * width], (LANES, width)).T
             for j in range(tiles):
                 rows = pl.ds(k * width * tiles + j, width, tiles)
-                value = turned[:, j * LANES:(j + 1) * LANES]
-                field[rows, :] = value
+                field[rows, :] = turned[:, j * LANES:(j + 1) * LANES]
                 pot[rows, :] = spread
-                total[rows, :] = spread * value
+                total[rows, :] = jnp.zeros_like(spread)
+        stiff[...] = stiff_in[...].T
     else:
-        add_faces(field, (came_low, came_high), wide, ids, slope(scales, min(step, 2)), pot, total)
+        add_faces(field, (came_low, came_high), wide, ids, at, slope(scales, min(step, 2)))
 
     def gather(cell, base, size):
         for i in range(size):
@@ -129,10 +134,14 @@
 
     lax.fori_loop(0, cells, one_cell, 0)
 
-    for side, faces in enumerate((below, above)):
+    for slot, faces in enumerate((below, above)):
+        offset = side_of(slot, at) * count
+
         def take(base, size):
+            first = offset + base
             for i in range(size):
-                wide[pl.ds((base + i) * tiles, tiles), :] = total[pl.ds(ids[side * count + base + i], tiles), :]
+                row = pl.ds(ids[first + i], tiles)
+                wide[pl.ds((base + i) * tiles, tiles), :] = total[row, :] + pot[row, :] * rounded(field[row, :])
 
         batches(count, BATCH, take)
         faces[...] = wide[...].astype(faces.dtype)
@@ -149,12 +158,12 @@
 
     def some(g, carry):
         rows = pl.ds(pl.multiple_of(g * SPAN, SPAN), SPAN)
-        value = rate * (summed[rows, :] - center * rounded(current[rows, :]))
+        value = rate * (summed[rows, :] + (pot[rows, :] - center) * rounded(current[rows, :]))
         if step:
             value = value - rounded(older[rows, :])
         out[rows, :] = value
         if not last:
-            total[rows, :] = pot[rows, :] * rounded(value)
+            total[rows, :] = jnp.zeros_like(value)
         return carry
 
     lax.fori_loop(0, current.shape[0] // SPAN, some, 0)
@@ -169,7 +178,7 @@
     count = ids.shape[0] // 2
     tiles = wide.shape[0] // count
     half = away.shape[0]
-    add_faces(field, (came_low, came_high), wide, ids, slope(bounds, 2))
+    add_faces(field, (came_low, came_high), wide, ids, at, slope(bounds, 2))
     start = (1 - at[0]) * half
     width = WIDTH
     for k in range(half // width):
@@ -177,16 +186,16 @@
             field, start + k * width, width, tiles).astype(away.dtype)
 
 
-def turn_kernel(ids, at, before, field, turned, own, own_masked, gram):
+def turn_kernel(ids, at, before, field, turned, own_first, own_second, own_masked, gram):
     count = ids.shape[0] // 2
     states, nodes = turned.shape
     tiles = states // LANES
-    half = own.shape[0]
+    quarter = own_first.shape[0]
+    half = 2 * quarter
     start = pl.multiple_of(at[0] * half, LANES)
+    for k, own in enumerate((own_first, own_second)):
+        own[...] = node_rows(field, start + k * quarter, quarter, tiles).astype(own.dtype)
     width = WIDTH
-    for k in range(half // width):
-        own[k * width:(k + 1) * width, :] = node_rows(
-            field, start + k * width, width, tiles).astype(own.dtype)
     for k in range(nodes // width):
         turned[:, k * width:(k + 1) * width] = node_rows(field, k * width, width, tiles).T.astype(turned.dtype)
 
@@ -201,7 +210,7 @@
     for k in range(half // width):
         own_masked[:, k * width:(k + 1) * width] = node_rows(
             field, start + k * width, width, tiles).T.astype(own_masked.dtype)
-    total = jnp.zeros(gram.shape, jnp.float32)
+    total = jnp.zeros((states, states), jnp.float32)
     for k in range(nodes // width):
         total += jnp.dot(turned[:, k * width:(k + 1) * width],
                          node_rows(field, k * width, width, tiles).astype(turned.dtype),
@@ -262,7 +271,7 @@
     out[...] = (result / jnp.sqrt(scale)).astype(jnp.bfloat16)
 
 
-def rotate_kernel(at, columns, turned, first, rest, out):
+def rotate_kernel(at, columns, turned, first, rest_first, rest_second, out):
     states, nodes = out.shape
     half = nodes // 2
     own = columns[pl.ds(pl.multiple_of(at[0] * states, states), states), :]
@@ -278,11 +287,23 @@
         out[:, pl.ds(base, width)] = value.astype(out.dtype)
 
     part_of(at[0] * half, first)
-    part_of((1 - at[0]) * half, rest)
+    away = (1 - at[0]) * half
+    part_of(away, rest_first)
+    part_of(away + rest_first.shape[0], rest_second)
+
+
+def rotate_call(at, columns, turned, *came):
+    return pl.pallas_call(
+        rotate_kernel,
+        out_shape=struct(turned.shape, jnp.bfloat16),
+        in_specs=[SMEM] + [VMEM] * 5, out_specs=VMEM, compiler_params=limit(26), name="rotate",
+    )(at, columns, turned, *came)
 
 
 SMEM = pl.BlockSpec(memory_space=pltpu.SMEM)
 VMEM = pl.BlockSpec(memory_space=pltpu.VMEM)
+
+
 def limit(mib):
     return pltpu.CompilerParams(vmem_limit_bytes=mib * 1024 * 1024)
 
@@ -292,7 +313,7 @@
 
 
 def apply_call(step, tables, pot, stiff, *fields):
-    conn, ids = tables[:2]
+    _, ids = tables[:2]
     dofs = stiff.shape[0]
     count = ids.shape[0] // 2
     f32, bf16 = jnp.float32, jnp.bfloat16
@@ -307,16 +328,18 @@
     out_shape = [whole, whole, face, face]
     if step == 0:
         out_shape += [whole, struct(stiff.shape, stiff.dtype)]
+    scratch = [
+        pltpu.VMEM((dofs * tiles, LANES), f32),
+        pltpu.VMEM((dofs * tiles, LANES), f32),
+        pltpu.VMEM((count * tiles, LANES), f32),
+    ]
+    specs = [VMEM] * (2 + len(fields))
     return pl.pallas_call(
         functools.partial(apply_kernel, step),
         out_shape=out_shape,
-        in_specs=[SMEM] * 4 + [VMEM] * (2 + len(fields)),
+        in_specs=[SMEM] * 4 + specs,
         out_specs=[VMEM] * len(out_shape),
-        scratch_shapes=[
-            pltpu.VMEM((dofs * tiles, LANES), f32),
-            pltpu.VMEM((dofs * tiles, LANES), f32),
-            pltpu.VMEM((count * tiles, LANES), f32),
-        ],
+        scratch_shapes=scratch,
         input_output_aliases={6: 0, 7: 1} if step else {},
         compiler_params=limit(26),
         name="apply",
@@ -357,7 +380,7 @@
 
 def sum_scatter(x, here):
     devices = lax.axis_size("dom")
-    for group in groups_of(devices):
+    for group in groups_of(devices)[:-1]:
         size = x.shape[-2] >> len(group)
         code = code_of(group, here)
         came = [
@@ -372,9 +395,26 @@
     return x
 
 
+def sum_last(own, cross, part):
+    devices = lax.axis_size("dom")
+    both = jnp.stack([own, cross])
+    sums = []
+    for flip in range(2):
+        total = None
+        for m, mask in [(0, 0)] + list(plan(groups_of(devices)[-1])):
+            piece = both
+            if mask or flip:
+                piece = lax.ppermute(both, ("dom", "st"), [(i, i ^ (2 * mask + flip)) for i in range(2 * devices)])
+            total = piece if total is None else total + piece
+        sums.append(total)
+    mine, theirs = sums
+    return jnp.stack([jnp.where(part == 0, mine[0], theirs[0]),
+                      jnp.where(part == 0, theirs[0], mine[0]), mine[1] + theirs[1]])
+
+
 def gather_all(x, here):
     devices = lax.axis_size("dom")
-    for group in reversed(groups_of(devices)):
+    for group in reversed(groups_of(devices)[:-1]):
         size = x.shape[-2]
         code = code_of(group, here)
         pieces = [(0, x)] + [
@@ -390,12 +430,14 @@
     f32, bf16 = jnp.float32, jnp.bfloat16
     swap = [(0, 1), (1, 0)]
     half = nodes // 2
+    square = struct((states, states))
     came = lax.ppermute(away, "st", swap)
-    _, turned, own, own_masked, gram = pl.pallas_call(
+    _, turned, own_first, own_second, own_masked, gram = pl.pallas_call(
         turn_kernel,
-        out_shape=[struct(field.shape), struct((states, nodes), bf16), struct((half, states), bf16),
-                   struct((states, half), bf16), struct((states, states))],
-        in_specs=[SMEM, SMEM, VMEM], out_specs=[VMEM] * 5,
+        out_shape=[struct(field.shape), struct((states, nodes), bf16),
+                   struct((half // 2, states), bf16), struct((half // 2, states), bf16),
+                   struct((states, half), bf16), square],
+        in_specs=[SMEM, SMEM, VMEM], out_specs=[VMEM] * 6,
         input_output_aliases={2: 0},
         compiler_params=limit(26), name="turn",
         cost_estimate=pl.CostEstimate(flops=4 * 10**9, bytes_accessed=10**7, transcendentals=0),
@@ -403,19 +445,17 @@
     place, gram = lax.optimization_barrier((at, gram))
     here = place[1]
     own_sum = sum_scatter(gram, here)
+    own_masked, own_sum = lax.optimization_barrier((own_masked, own_sum))
     cross = pl.pallas_call(
         cross_kernel,
-        out_shape=struct((states, states)),
+        out_shape=square,
         in_specs=[SMEM, VMEM, VMEM], out_specs=VMEM, compiler_params=limit(16), name="cross",
     )(at, own_masked, came)
-    with jax.named_scope("rest"):
-        rest = lax.ppermute(own, "st", swap)
+    rest_first = lax.ppermute(own_first, "st", swap)
     cross_sum = sum_scatter(cross, here)
-    pair = jnp.stack([own_sum, cross_sum])
-    theirs = lax.ppermute(pair, "st", swap)
-    lower = place[0] == 0
-    blocks = gather_all(jnp.stack([
-        jnp.where(lower, pair[0], theirs[0]), jnp.where(lower, theirs[0], pair[0]), pair[1] + theirs[1]]), here)
+    sums = sum_last(own_sum, cross_sum, place[0])
+    rest_second = lax.ppermute(own_second, "st", swap)
+    blocks = gather_all(sums, here)
     columns = pl.pallas_call(
         root_kernel,
         out_shape=struct((2 * states, states), bf16),
@@ -423,11 +463,7 @@
         scratch_shapes=[pltpu.VMEM((2 * states, 2 * states), f32), pltpu.VMEM((2, 2 * states, 2 * states), bf16)],
         compiler_params=limit(26), name="root",
     )(at, blocks)
-    return pl.pallas_call(
-        rotate_kernel,
-        out_shape=struct((states, nodes), bf16),
-        in_specs=[SMEM] + [VMEM] * 4, out_specs=VMEM, compiler_params=limit(26), name="rotate",
-    )(at, columns, turned, came, rest)
+    return rotate_call(at, columns, turned, came, rest_first, rest_second)
 
 
 def rotate_any(current, owned):
@@ -454,12 +490,11 @@
     at = jnp.stack([lax.axis_index("st"), lax.axis_index("dom")])
 
     def exchange(low, high):
-        with jax.named_scope("halo"):
-            return passed_along(high, "dom", 1), passed_along(low, "dom", -1)
+        return paired(low, "dom", 0), paired(high, "dom", 1)
 
     older = None
     current, total, low, high, pot, stiff = apply_call(
-        0, (conn, ids, numbers, at), potential[None, :], stiffness, start_states)
+        0, (conn, ids, numbers, at), potential, stiffness, start_states)
     for step in range(DEGREE):
         came = exchange(low, high)
         last = step == DEGREE - 1
@@ -480,7 +515,7 @@
         name="send",
     )(ids, numbers, at, following, *came)
     devices = lax.axis_size("dom")
-    if lax.axis_size("st") == 2 and states == block_states and devices & (devices - 1) == 0:
+    if lax.axis_size("st") == 2 and states == block_states and devices & (devices - 1) == nodes % (4 * LANES):
         return rotate_pair(field, away, ids, at, states, nodes)
     current = field.reshape(nodes, states).T.astype(jnp.bfloat16)[:block_states]
     inside = (jnp.arange(nodes) < LN).astype(jnp.bfloat16)
@@ -491,6 +526,4 @@
 
 def solution(mesh):
     placed = (P("st", "dom"), P(), P("dom"), P("dom"), P("dom", None), P("dom", None, None), P())
-    return jax.shard_map(
-        body, mesh=mesh, in_specs=placed, out_specs=P("st", "dom"), check_vma=False
-    )
+    return jax.shard_map(body, mesh=mesh, in_specs=placed, out_specs=P("st", "dom"), check_vma=False)

time: 157 us -> 171 us (1.089)
  waiting for transfers between devices: 17.5 us -> 33.5 us
  starting transfers between devices: 55.8 us -> 51 us
    ppermute x8 -> x11, waiting for transfers between devices: 4.46 us -> 19 us  [the longest x1 9.29 us: rotate_pair(): rest_second = lax.ppermute(own_second, 'st', swap)]
    ppermute x10 -> x8, waiting for transfers between devices: 4.12 us -> 10.6 us  [sum_scatter(): lax.ppermute(lax.dynamic_slice_in_dim(x, (code ^ m) * size, size, x.ndim...]
    ppermute x10 -> x8, starting transfers between devices: 25.7 us -> 21.8 us  [sum_scatter(): lax.ppermute(lax.dynamic_slice_in_dim(x, (code ^ m) * size, size, x.ndim...]
    ppermute x5 -> x4, waiting for transfers between devices: 7.09 us -> 3.95 us  [gather_all(): lax.ppermute(x, 'dom', [(i, i ^ mask) for i in range(devices)])]
    ppermute x5 -> x4, starting transfers between devices: 6.09 us -> 4.22 us  [gather_all(): lax.ppermute(x, 'dom', [(i, i ^ mask) for i in range(devices)])]
    ppermute x1, waiting for transfers between devices: 1.86 us -> 0.01 us  [rotate_pair(): came = lax.ppermute(away, 'st', swap)]
    unnamed x13 -> x17, local copies, waits for them, and re-layouts: 5.57 us -> 6.8 us
    ppermute x8 -> x11, starting transfers between devices: 22.5 us -> 23.5 us  [the longest x6 16.9 us: paired(): return lax.ppermute(x, axis, pairs)]
  transfers between devices with their start and end apart: 24 -> 24, of which waited for: 13 -> 14; matrix products, arithmetic and copies ran while one was open for 1% -> 2% of each run, Pallas kernels for 9% -> 7%
where the time goes in v5:
time: 171 us; the launch traced here: 170 us
  Pallas kernels  70.7 us (41%)
  starting transfers between devices  51 us (30%)
  waiting for transfers between devices  33.5 us (20%)
  local copies, waits for them, and re-layouts  8.36 us (5%)
  other arithmetic  4.01 us (2%)
  between operations  2.81 us (2%)
    pallas_call x3, Pallas kernels, apply_call(): pl.pallas_call(functools.partial(apply_kernel, step), out_shape=out_shape...  49.4 us
    ppermute x8, starting transfers between devices, sum_scatter(): lax.ppermute(lax.dynamic_slice_in_dim(x, (code ^ m) * size, size, x.ndim...  21.8 us
    ppermute x6, starting transfers between devices, paired(): return lax.ppermute(x, axis, pairs)  16.9 us
    ppermute x8, waiting for transfers between devices, sum_scatter(): lax.ppermute(lax.dynamic_slice_in_dim(x, (code ^ m) * size, size, x.ndim...  10.6 us
    ppermute x1, waiting for transfers between devices, rotate_pair(): rest_second = lax.ppermute(own_second, 'st', swap)  9.29 us
    unnamed x17, local copies, waits for them, and re-layouts  6.8 us
    pallas_call x1, Pallas kernels, rotate_pair(): pl.pallas_call(root_kernel, out_shape=struct((2 * states, states), bf16),...  6.47 us
    pallas_call x3, Pallas kernels, settle_call(): pl.pallas_call(functools.partial(settle_kernel, step, last), out_shape=[w...  5.69 us
  transfers between devices with their start and end apart: 24, of which 14 were waited for; matrix products, arithmetic and copies ran while one was open for 2% of the time, Pallas kernels for 7%

profile of v5, /device:TPU:0, one launch (start us, length us, event | category | flops | bytes accessed | tf_op | source)
XLA Modules:
  0.0 170.4 jit_solution(11010000821368305373)
XLA Ops:
  0.0 0.7 broadcast_multiply_fusion
  0.7 0.1 mul.51.refs_1_.ids
  0.8 0.7 multiply_bitcast_fusion
  1.5 0.1 pad_add_fusion.refs_3_.at
  1.6 0.7 pad_maximum_fusion.2.refs_2_.refs_0_.bounds
  2.3 1.5 copy-done
  3.8 1.0 copy-done.3
  4.9 0.7 copy-done.4
  5.6 16.4 %apply.3 = (f32[7168,128]{1,0:T(8,128)S(1)}, f32[7168,128]{1,0:T(8,128)S(1)}, bf16[870,128]{1,0:T(8,128)(2,1)S(1)}, bf16[870,128]{1,0:T(8,128)(2,1)S(1)}, f32[71...) custom-call(s32[4096]{0:T(1024)S(1)} %bitcast.15, s32[870]{0:T(1024)S(1)} %mul.51.refs_1_.ids, ...), custom_call_target="tpu_custom_call" | custom-call | tf_op jit(solution)/shard_map/apply/pallas_call | solution.py:337
  22.0 0.6 collective-permute-start
  22.6 0.7 collective-permute-start.1
  23.2 1.5 settle.3
  24.8 16.5 %apply.4 = (f32[7168,128]{1,0:T(8,128)S(1)}, f32[7168,128]{1,0:T(8,128)S(1)}, bf16[870,128]{1,0:T(8,128)(2,1)S(1)}, bf16[870,128]{1,0:T(8,128)(2,1)S(1)}) custom-call(s32[4096]{0:T(1024)S(1)} %bitcast.16, s32[870]{0:T(1024)S(1)} %mul.51.refs_1_.ids, f32[10]{0:T(128)S(1)} %pad_maximum_fusion.2.refs_2_.refs_0_.bounds, ...), custom_call_target="tpu_custom_call", output_to_operand_aliasing={{0}: (6, {}), {1}: (7, {})} | custom-call | tf_op jit(solution)/shard_map/apply/pallas_call | solution.py:337
  41.3 7.6 %collective-permute-start.2 = (bf16[870,128]{1,0:T(8,128)(2,1)S(1)}, bf16[870,128]{1,0:T(8,128)(2,1)S(1)}, u32[]{:S(2)}, u32[]{:S(2)}) collective-permute-start(bf16[870,128]{1,0:T(8,128)(2,1)S(1)} %get-tuple-element.46), channel_id=1, source_target_pairs={{0,2},{4,6},{8,10},{12,14},{16,18},{20,22},{24,26},{28,30},{2,0},{... | collective-permute-start | bytes 668168 | tf_op jit(solution)/shard_map/ppermute | solution.py:23
  49.0 0.7 collective-permute-start.3
  49.6 2.3 %settle.4 = (f32[7168,128]{1,0:T(8,128)S(1)}, f32[7168,128]{1,0:T(8,128)S(1)}) custom-call(f32[10]{0:T(128)S(1)} %pad_maximum_fusion.2.refs_2_.refs_0_.bounds, f32[7168,128]{1,0:T(8,128)S(1)} %get-tuple-element.34.refs_1_.refs_4_, f32[7168,128]{1,0:T(8,128)S(1)} %get-tuple-element.42.refs_2_.refs_4_, ...), custom_call_target="tpu_custom_call", output_to_operand_aliasing={{0}: (4, {}), {1}: (3, {})} | custom-call | flops 8000000000 | bytes 10000000 | tf_op jit(solution)/shard_map/settle/pallas_call | solution.py:355
  52.0 16.5 %apply.5 = (f32[7168,128]{1,0:T(8,128)S(1)}, f32[7168,128]{1,0:T(8,128)S(1)}, bf16[870,128]{1,0:T(8,128)(2,1)S(1)}, bf16[870,128]{1,0:T(8,128)(2,1)S(1)}) custom-call(s32[4096]{0:T(1024)S(1)} %bitcast.17, s32[870]{0:T(1024)S(1)} %mul.51.refs_1_.ids, f32[10]{0:T(128)S(1)} %pad_maximum_fusion.2.refs_2_.refs_0_.bounds, ...), custom_call_target="tpu_custom_call", output_to_operand_aliasing={{0}: (6, {}), {1}: (7, {})} | custom-call | tf_op jit(solution)/shard_map/apply/pallas_call | solution.py:337
  68.5 6.7 %collective-permute-start.4 = (bf16[870,128]{1,0:T(8,128)(2,1)S(1)}, bf16[870,128]{1,0:T(8,128)(2,1)S(1)}, u32[]{:S(2)}, u32[]{:S(2)}) collective-permute-start(bf16[870,128]{1,0:T(8,128)(2,1)S(1)} %get-tuple-element.50), channel_id=1, source_target_pairs={{0,2},{4,6},{8,10},{12,14},{16,18},{20,22},{24,26},{28,30},{2,0},{... | collective-permute-start | bytes 668168 | tf_op jit(solution)/shard_map/ppermute | solution.py:23
  75.2 0.7 collective-permute-start.5
  75.9 1.8 %settle.5.before = f32[7168,128]{1,0:T(8,128)S(1)} custom-call(f32[10]{0:T(128)S(1)} %pad_maximum_fusion.2.refs_2_.refs_0_.bounds, f32[7168,128]{1,0:T(8,128)S(1)} %get-tuple-element.34.refs_1_.refs_4_, f32[7168,128]{1,0:T(8,128)S(1)} %get-tuple-element.48.refs_2_, f32[7168,128]{1,0:T(8,128)S(1)} %get-tuple-element.49.refs_3_, ...), custom_call_target="tpu_custom_call", output_to_operand_aliasing={{}: (4, {})} | custom-call | flops 8000000000 | bytes 10000000 | tf_op jit(solution)/shard_map/settle/pallas_call | solution.py:355
  77.7 3.2 %send.1 = (f32[7168,128]{1,0:T(8,128)S(1)}, bf16[1792,256]{1,0:T(8,128)(2,1)}) custom-call(s32[870]{0:T(1024)S(1)} %mul.51.refs_1_.ids, f32[10]{0:T(128)S(1)} %pad_maximum_fusion.2.refs_2_.refs_0_.bounds, s32[2]{0:T(128)S(1)} %pad_add_fusion.refs_3_.at, f32[7168,128]{1,0:T(8,128)S(1)} %settle.5.before, ...), custom_call_target="tpu_custom_call", output_to_operand_aliasing={{0}: (3, {})} | custom-call | tf_op jit(solution)/shard_map/send/pallas_call | solution.py:507
  80.9 1.8 %turn.1 = (f32[7168,128]{1,0:T(8,128)S(1)}, bf16[256,3584]{1,0:T(8,128)(2,1)S(1)}, bf16[896,256]{1,0:T(8,128)(2,1)S(1)}, bf16[896,256]{1,0:T(8,128)(2,1)S(1)}, b...) custom-call(s32[870]{0:T(1024)S(1)} %mul.51.refs_1_.ids, ...), custom_call_target="tpu_custom_call", output_to_operand_aliasing={{0}: (2, {})} | custom-call | flops 4000000000 | bytes 10000000 | tf_op jit(solution)/shard_map/turn/pallas_call | solution.py:435
  82.8 0.9 copy-done.1
  83.7 0.8 copy-done.5
  84.5 1.5 collective-permute-start.10
  86.0 0.6 fusion.1
  87.2 0.7 constant_dynamic-slice_fusion.7
  87.9 7.3 %collective-permute-start.6 = (f32[128,256]{1,0:T(8,128)}, f32[128,256]{1,0:T(8,128)}, u32[]{:S(2)}, u32[]{:S(2)}) collective-permute-start(f32[128,256]{1,0:T(8,128)} %constant_dynamic-slice_fusion.7), channel_id=1, source_target_pairs={{0,2},{2,0},{4,6},{6,4},{8,10},{10,8},{12,14},{14,12},{16,18},{18,... | collective-permute-start | bytes 393224 | tf_op jit(solution)/shard_map/ppermute | solution.py:387
  96.5 0.9 dynamic-slice_add_fusion.1
  97.4 0.6 copy-done.7
  98.1 3.1 %collective-permute-start.7 = (f32[32,256]{1,0:T(8,128)S(1)}, f32[32,256]{1,0:T(8,128)S(1)}, u32[]{:S(2)}, u32[]{:S(2)}) collective-permute-start(f32[32,256]{1,0:T(8,128)S(1)} %get-tuple-element.69), channel_id=1, source_target_pairs={{0,4},{2,6},{4,0},{6,2},{8,12},{10,14},{12,8},{14,10},{16,20},{18,... | collective-permute-start | bytes 98312 | tf_op jit(solution)/shard_map/ppermute | solution.py:387
  101.2 1.6 collective-permute-start.8
  102.7 0.3 collective-permute-done.7
  103.1 2.2 %collective-permute-done.8 = f32[32,256]{1,0:T(8,128)S(1)} collective-permute-done((f32[32,256]{1,0:T(8,128)S(1)}, f32[32,256]{1,0:T(8,128)S(1)}, u32[]{:S(2)}, u32[]{:S(2)}) %collective-permute-start.8) | collective-permute-done | bytes 32800 | tf_op jit(solution)/shard_map/ppermute | solution.py:387
  105.2 2.3 %collective-permute-done.9 = f32[32,256]{1,0:T(8,128)S(1)} collective-permute-done((f32[32,256]{1,0:T(8,128)S(1)}, f32[32,256]{1,0:T(8,128)S(1)}, u32[]{:S(2)}, u32[]{:S(2)}) %collective-permute-start.9) | collective-permute-done | bytes 32800 | tf_op jit(solution)/shard_map/ppermute | solution.py:387
  107.5 0.8 add_add_fusion
  108.3 1.2 copy-done.2
  109.5 1.1 cross.1
  110.7 0.1 collective-permute-start.11
  110.8 1.3 collective-permute-done.11
  112.1 7.7 %collective-permute-start.12 = (f32[32,256]{1,0:T(8,128)S(1)}, f32[32,256]{1,0:T(8,128)S(1)}, u32[]{:S(2)}, u32[]{:S(2)}) collective-permute-start(f32[32,256]{1,0:T(8,128)S(1)} %get-tuple-element.66), channel_id=1, source_target_pairs={{0,4},{2,6},{4,0},{6,2},{8,12},{10,14},{12,8},{14,10},{16,20},{18,... | collective-permute-start | bytes 98312 | tf_op jit(solution)/shard_map/ppermute | solution.py:387
  119.9 1.6 collective-permute-start.13
  121.4 0.4 collective-permute-start.14
  121.9 1.9 %collective-permute-done.13 = f32[32,256]{1,0:T(8,128)S(1)} collective-permute-done((f32[32,256]{1,0:T(8,128)S(1)}, f32[32,256]{1,0:T(8,128)S(1)}, u32[]{:S(2)}, u32[]{:S(2)}) %collective-permute-start.13) | collective-permute-done | bytes 32800 | tf_op jit(solution)/shard_map/ppermute | solution.py:387
  123.8 2.5 %collective-permute-done.14 = f32[32,256]{1,0:T(8,128)S(1)} collective-permute-done((f32[32,256]{1,0:T(8,128)S(1)}, f32[32,256]{1,0:T(8,128)S(1)}, u32[]{:S(2)}, u32[]{:S(2)}) %collective-permute-start.14) | collective-permute-done | bytes 32800 | tf_op jit(solution)/shard_map/ppermute | solution.py:387
  126.3 1.7 collective-permute-start.15
  128.5 1.7 collective-permute-start.16
  130.2 1.1 collective-permute-start.17
  131.4 0.7 collective-permute-done.15
  132.1 0.8 collective-permute-done.16
  132.9 3.4 %collective-permute-done.17 = f32[2,32,256]{2,1,0:T(8,128)S(1)} collective-permute-done((f32[2,32,256]{2,1,0:T(8,128)S(1)}, f32[2,32,256]{2,1,0:T(8,128)S(1)}, u32[]{:S(2)}, u32[]{:S(2)}) %collective-permute-start.17) | collective-permute-done | bytes 65568 | tf_op jit(solution)/shard_map/ppermute | solution.py:407
  136.4 2.6 %collective-permute-start.18 = (f32[3,32,256]{2,1,0:T(8,128)S(1)}, f32[3,32,256]{2,1,0:T(8,128)S(1)}, u32[]{:S(2)}, u32[]{:S(2)}) collective-permute-start(f32[3,32,256]{2,1,0:T(8,128)S(1)} %get-tuple-element.72), channel_id=1, source_target_pairs={{0,4},{2,6},{4,0},{6,2},{8,12},{10,14},{12,8},{14,10},{16,20},{18,... | collective-permute-start | bytes 294920 | tf_op jit(solution)/shard_map/ppermute | solution.py:421
  139.0 1.5 collective-permute-start.20
  140.5 1.1 collective-permute-done.18
  141.6 2.0 %collective-permute-done.19 = f32[3,32,256]{2,1,0:T(8,128)S(1)} collective-permute-done((f32[3,32,256]{2,1,0:T(8,128)S(1)}, f32[3,32,256]{2,1,0:T(8,128)S(1)}, u32[]{:S(2)}, u32[]{:S(2)}) %collective-permute-start.19) | collective-permute-done | bytes 98336 | tf_op jit(solution)/shard_map/ppermute | solution.py:421
  143.6 0.9 collective-permute-done.20
  144.5 0.1 collective-permute-start.21
  144.6 0.5 collective-permute-start.22
  145.1 1.6 collective-permute-start.23
  146.7 0.1 broadcast_in_dim.6
  146.9 6.5 %root.1.columns = bf16[512,256]{1,0:T(8,128)(2,1)S(1)} custom-call(s32[2]{0:T(128)S(1)} %pad_add_fusion.refs_3_.at, f32[3,256,256]{2,1,0:T(8,128)S(1)} %constant_dynamic-update-slice_fusion.blocks), custom_call_target="tpu_custom_call" | custom-call | tf_op jit(solution)/shard_map/root/pallas_call | solution.py:459
  153.3 4.7 %collective-permute-done.22.rest_first = bf16[896,256]{1,0:T(8,128)(2,1)S(1)} collective-permute-done((bf16[896,256]{1,0:T(8,128)(2,1)S(1)}, bf16[896,256]{1,0:T(8,128)(2,1)S(1)}, u32[]{:S(2)}, u32[]{:S(2)}) %collective-permute-start.22) | collective-permute-done | bytes 458784 | tf_op jit(solution)/shard_map/ppermute | solution.py:454
  158.1 9.3 %collective-permute-done.23.rest_second = bf16[896,256]{1,0:T(8,128)(2,1)S(1)} collective-permute-done((bf16[896,256]{1,0:T(8,128)(2,1)S(1)}, bf16[896,256]{1,0:T(8,128)(2,1)S(1)}, u32[]{:S(2)}, u32[]{:S(2)}) %collective-permute-start.23) | collective-permute-done | bytes 458784 | tf_op jit(solution)/shard_map/ppermute | solution.py:457
  167.4 3.0 %rotate.1 = bf16[256,3584]{1,0:T(8,128)(2,1)} custom-call(s32[2]{0:T(128)S(1)} %pad_add_fusion.refs_3_.at, bf16[512,256]{1,0:T(8,128)(2,1)S(1)} %root.1.columns, bf16[256,3584]{1,0:T(8,128)(2,1)S(1)} %get-tuple-element.60.turned, bf16[1792,256]{1,0:T(8,128)(2,1)S(1)} %collective-permute-done.10.came.first, ...), custom_call_target="tpu_custom_call" | custom-call | tf_op jit(solution)/shard_map/rotate/pallas_call | solution.py:296
  (38 shorter events, 0.4 us)
Async XLA Ops:
  2.3 1.5 copy-start
  3.8 1.0 copy-start.3
  4.9 0.7 copy-start.4
  22.0 2.8 %collective-permute-start = (bf16[870,128]{1,0:T(8,128)(2,1)S(1)}, bf16[870,128]{1,0:T(8,128)(2,1)S(1)}, u32[]{:S(2)}, u32[]{:S(2)}) collective-permute-start(bf16[870,128]{1,0:T(8,128)(2,1)S(1)} %get-tuple-element.40), channel_id=1, source_target_pairs={{0,2},{4,6},{8,10},{12,14},{16,18},{20,22},{24,26},{28,30},{2,0},{... | collective-permute-start | bytes 668168 | tf_op jit(solution)/shard_map/ppermute | solution.py:23
  22.6 2.2 %collective-permute-start.1 = (bf16[870,128]{1,0:T(8,128)(2,1)S(1)}, bf16[870,128]{1,0:T(8,128)(2,1)S(1)}, u32[]{:S(2)}, u32[]{:S(2)}) collective-permute-start(bf16[870,128]{1,0:T(8,128)(2,1)S(1)} %get-tuple-element.41), channel_id=1, source_target_pairs={{2,4},{6,8},{10,12},{14,16},{18,20},{22,24},{26,28},{4,2},{8,6},{1... | collective-permute-start | bytes 668168 | tf_op jit(solution)/shard_map/ppermute | solution.py:23
  41.3 10.6 %collective-permute-start.2 = (bf16[870,128]{1,0:T(8,128)(2,1)S(1)}, bf16[870,128]{1,0:T(8,128)(2,1)S(1)}, u32[]{:S(2)}, u32[]{:S(2)}) collective-permute-start(bf16[870,128]{1,0:T(8,128)(2,1)S(1)} %get-tuple-element.46), channel_id=1, source_target_pairs={{0,2},{4,6},{8,10},{12,14},{16,18},{20,22},{24,26},{28,30},{2,0},{... | collective-permute-start | bytes 668168 | tf_op jit(solution)/shard_map/ppermute | solution.py:23
  49.0 3.0 %collective-permute-start.3 = (bf16[870,128]{1,0:T(8,128)(2,1)S(1)}, bf16[870,128]{1,0:T(8,128)(2,1)S(1)}, u32[]{:S(2)}, u32[]{:S(2)}) collective-permute-start(bf16[870,128]{1,0:T(8,128)(2,1)S(1)} %get-tuple-element.47), channel_id=1, source_target_pairs={{2,4},{6,8},{10,12},{14,16},{18,20},{22,24},{26,28},{4,2},{8,6},{1... | collective-permute-start | bytes 668168 | tf_op jit(solution)/shard_map/ppermute | solution.py:23
  68.5 9.3 %collective-permute-start.4 = (bf16[870,128]{1,0:T(8,128)(2,1)S(1)}, bf16[870,128]{1,0:T(8,128)(2,1)S(1)}, u32[]{:S(2)}, u32[]{:S(2)}) collective-permute-start(bf16[870,128]{1,0:T(8,128)(2,1)S(1)} %get-tuple-element.50), channel_id=1, source_target_pairs={{0,2},{4,6},{8,10},{12,14},{16,18},{20,22},{24,26},{28,30},{2,0},{... | collective-permute-start | bytes 668168 | tf_op jit(solution)/shard_map/ppermute | solution.py:23
  75.2 2.5 %collective-permute-start.5 = (bf16[870,128]{1,0:T(8,128)(2,1)S(1)}, bf16[870,128]{1,0:T(8,128)(2,1)S(1)}, u32[]{:S(2)}, u32[]{:S(2)}) collective-permute-start(bf16[870,128]{1,0:T(8,128)(2,1)S(1)} %get-tuple-element.51), channel_id=1, source_target_pairs={{2,4},{6,8},{10,12},{14,16},{18,20},{22,24},{26,28},{4,2},{8,6},{1... | collective-permute-start | bytes 668168 | tf_op jit(solution)/shard_map/ppermute | solution.py:23
  82.8 0.9 copy-start.1
  83.7 0.8 copy-start.5
  84.5 23.8 %collective-permute-start.10 = (bf16[1792,256]{1,0:T(8,128)(2,1)}, bf16[1792,256]{1,0:T(8,128)(2,1)S(1)}, u32[]{:S(2)}, u32[]{:S(2)}) collective-permute-start(bf16[1792,256]{1,0:T(8,128)(2,1)} %get-tuple-element.59), channel_id=1, source_target_pairs={{0,1},{1,0},{2,3},{3,2},{4,5},{5,4},{6,7},{7,6},{8,9},{9,8},{10,11... | collective-permute-start | bytes 2752520 | tf_op jit(solution)/shard_map/ppermute | solution.py:434
  87.9 8.6 %collective-permute-start.6 = (f32[128,256]{1,0:T(8,128)}, f32[128,256]{1,0:T(8,128)}, u32[]{:S(2)}, u32[]{:S(2)}) collective-permute-start(f32[128,256]{1,0:T(8,128)} %constant_dynamic-slice_fusion.7), channel_id=1, source_target_pairs={{0,2},{2,0},{4,6},{6,4},{8,10},{10,8},{12,14},{14,12},{16,18},{18,... | collective-permute-start | bytes 393224 | tf_op jit(solution)/shard_map/ppermute | solution.py:387
  97.4 0.7 copy-start.7
  98.1 5.0 %collective-permute-start.7 = (f32[32,256]{1,0:T(8,128)S(1)}, f32[32,256]{1,0:T(8,128)S(1)}, u32[]{:S(2)}, u32[]{:S(2)}) collective-permute-start(f32[32,256]{1,0:T(8,128)S(1)} %get-tuple-element.69), channel_id=1, source_target_pairs={{0,4},{2,6},{4,0},{6,2},{8,12},{10,14},{12,8},{14,10},{16,20},{18,... | collective-permute-start | bytes 98312 | tf_op jit(solution)/shard_map/ppermute | solution.py:387
  101.2 4.1 %collective-permute-start.8 = (f32[32,256]{1,0:T(8,128)S(1)}, f32[32,256]{1,0:T(8,128)S(1)}, u32[]{:S(2)}, u32[]{:S(2)}) collective-permute-start(f32[32,256]{1,0:T(8,128)S(1)} %get-tuple-element.71), channel_id=1, source_target_pairs={{0,8},{2,10},{4,12},{6,14},{8,0},{10,2},{12,4},{14,6},{16,24},{18,... | collective-permute-start | bytes 98312 | tf_op jit(solution)/shard_map/ppermute | solution.py:387
  102.7 4.8 %collective-permute-start.9 = (f32[32,256]{1,0:T(8,128)S(1)}, f32[32,256]{1,0:T(8,128)S(1)}, u32[]{:S(2)}, u32[]{:S(2)}) collective-permute-start(f32[32,256]{1,0:T(8,128)S(1)} %get-tuple-element.70), channel_id=1, source_target_pairs={{0,12},{2,14},{4,8},{6,10},{8,4},{10,6},{12,0},{14,2},{16,28},{18,... | collective-permute-start | bytes 98312 | tf_op jit(solution)/shard_map/ppermute | solution.py:387
  108.3 1.2 copy-start.2
  109.5 35.1 %copy-start.6 = (bf16[896,256]{1,0:T(8,128)(2,1)S(1)}, bf16[896,256]{1,0:T(8,128)(2,1)}, u32[]{:S(2)}) copy-start(bf16[896,256]{1,0:T(8,128)(2,1)} %copy-done.5) | copy-start | bytes 1376260
  110.7 1.4 collective-permute-start.11
  112.1 9.7 %collective-permute-start.12 = (f32[32,256]{1,0:T(8,128)S(1)}, f32[32,256]{1,0:T(8,128)S(1)}, u32[]{:S(2)}, u32[]{:S(2)}) collective-permute-start(f32[32,256]{1,0:T(8,128)S(1)} %get-tuple-element.66), channel_id=1, source_target_pairs={{0,4},{2,6},{4,0},{6,2},{8,12},{10,14},{12,8},{14,10},{16,20},{18,... | collective-permute-start | bytes 98312 | tf_op jit(solution)/shard_map/ppermute | solution.py:387
  119.9 3.9 %collective-permute-start.13 = (f32[32,256]{1,0:T(8,128)S(1)}, f32[32,256]{1,0:T(8,128)S(1)}, u32[]{:S(2)}, u32[]{:S(2)}) collective-permute-start(f32[32,256]{1,0:T(8,128)S(1)} %get-tuple-element.68), channel_id=1, source_target_pairs={{0,8},{2,10},{4,12},{6,14},{8,0},{10,2},{12,4},{14,6},{16,24},{18,... | collective-permute-start | bytes 98312 | tf_op jit(solution)/shard_map/ppermute | solution.py:387
  121.4 4.8 %collective-permute-start.14 = (f32[32,256]{1,0:T(8,128)S(1)}, f32[32,256]{1,0:T(8,128)S(1)}, u32[]{:S(2)}, u32[]{:S(2)}) collective-permute-start(f32[32,256]{1,0:T(8,128)S(1)} %get-tuple-element.67), channel_id=1, source_target_pairs={{0,12},{2,14},{4,8},{6,10},{8,4},{10,6},{12,0},{14,2},{16,28},{18,... | collective-permute-start | bytes 98312 | tf_op jit(solution)/shard_map/ppermute | solution.py:387
  126.3 5.8 %collective-permute-start.15 = (f32[2,32,256]{2,1,0:T(8,128)S(1)}, f32[2,32,256]{2,1,0:T(8,128)S(1)}, u32[]{:S(2)}, u32[]{:S(2)}) collective-permute-start(f32[2,32,256]{2,1,0:T(8,128)S(1)} %pad_maximum_fusion.1), channel_id=1, source_target_pairs={{0,16},{1,17},{2,18},{3,19},{4,20},{5,21},{6,22},{7,23},{8,24},{9,... | collective-permute-start | bytes 196616 | tf_op jit(solution)/shard_map/ppermute | solution.py:407
  128.5 4.3 %collective-permute-start.16 = (f32[2,32,256]{2,1,0:T(8,128)S(1)}, f32[2,32,256]{2,1,0:T(8,128)S(1)}, u32[]{:S(2)}, u32[]{:S(2)}) collective-permute-start(f32[2,32,256]{2,1,0:T(8,128)S(1)} %pad_maximum_fusion.1), channel_id=1, source_target_pairs={{0,1},{1,0},{2,3},{3,2},{4,5},{5,4},{6,7},{7,6},{8,9},{9,8},{10,11... | collective-permute-start | bytes 196616 | tf_op jit(solution)/shard_map/ppermute | solution.py:407
  130.2 6.1 %collective-permute-start.17 = (f32[2,32,256]{2,1,0:T(8,128)S(1)}, f32[2,32,256]{2,1,0:T(8,128)S(1)}, u32[]{:S(2)}, u32[]{:S(2)}) collective-permute-start(f32[2,32,256]{2,1,0:T(8,128)S(1)} %pad_maximum_fusion.1), channel_id=1, source_target_pairs={{0,17},{1,16},{2,19},{3,18},{4,21},{5,20},{6,23},{7,22},{8,25},{9,... | collective-permute-start | bytes 196616 | tf_op jit(solution)/shard_map/ppermute | solution.py:407
  136.4 5.2 %collective-permute-start.18 = (f32[3,32,256]{2,1,0:T(8,128)S(1)}, f32[3,32,256]{2,1,0:T(8,128)S(1)}, u32[]{:S(2)}, u32[]{:S(2)}) collective-permute-start(f32[3,32,256]{2,1,0:T(8,128)S(1)} %get-tuple-element.72), channel_id=1, source_target_pairs={{0,4},{2,6},{4,0},{6,2},{8,12},{10,14},{12,8},{14,10},{16,20},{18,... | collective-permute-start | bytes 294920 | tf_op jit(solution)/shard_map/ppermute | solution.py:421
  139.0 4.6 %collective-permute-start.19 = (f32[3,32,256]{2,1,0:T(8,128)S(1)}, f32[3,32,256]{2,1,0:T(8,128)S(1)}, u32[]{:S(2)}, u32[]{:S(2)}) collective-permute-start(f32[3,32,256]{2,1,0:T(8,128)S(1)} %get-tuple-element.72), channel_id=1, source_target_pairs={{0,8},{2,10},{4,12},{6,14},{8,0},{10,2},{12,4},{14,6},{16,24},{18,... | collective-permute-start | bytes 294920 | tf_op jit(solution)/shard_map/ppermute | solution.py:421
  139.0 5.5 %collective-permute-start.20 = (f32[3,32,256]{2,1,0:T(8,128)S(1)}, f32[3,32,256]{2,1,0:T(8,128)S(1)}, u32[]{:S(2)}, u32[]{:S(2)}) collective-permute-start(f32[3,32,256]{2,1,0:T(8,128)S(1)} %get-tuple-element.72), channel_id=1, source_target_pairs={{0,12},{2,14},{4,8},{6,10},{8,4},{10,6},{12,0},{14,2},{16,28},{18,... | collective-permute-start | bytes 294920 | tf_op jit(solution)/shard_map/ppermute | solution.py:421
  144.5 2.3 %collective-permute-start.21 = (f32[3,128,256]{2,1,0:T(8,128)S(1)}, f32[3,128,256]{2,1,0:T(8,128)S(1)}, u32[]{:S(2)}, u32[]{:S(2)}) collective-permute-start(f32[3,128,256]{2,1,0:T(8,128)S(1)} %constant_dynamic-update-slice_fusion.2), channel_id=1, source_target_pairs={{0,2},{2,0},{4,6},{6,4},{8,10},{10,8},{12,14},{14,12},{16,18},{18,... | collective-permute-start | bytes 1179656 | tf_op jit(solution)/shard_map/ppermute | solution.py:421
  144.6 13.5 %collective-permute-start.22 = (bf16[896,256]{1,0:T(8,128)(2,1)S(1)}, bf16[896,256]{1,0:T(8,128)(2,1)S(1)}, u32[]{:S(2)}, u32[]{:S(2)}) collective-permute-start(bf16[896,256]{1,0:T(8,128)(2,1)S(1)} %copy-done.6), channel_id=1, source_target_pairs={{0,1},{1,0},{2,3},{3,2},{4,5},{5,4},{6,7},{7,6},{8,9},{9,8},{10,11... | collective-permute-start | bytes 1376264 | tf_op jit(solution)/shard_map/ppermute | solution.py:454
  145.1 22.3 %collective-permute-start.23 = (bf16[896,256]{1,0:T(8,128)(2,1)S(1)}, bf16[896,256]{1,0:T(8,128)(2,1)S(1)}, u32[]{:S(2)}, u32[]{:S(2)}) collective-permute-start(bf16[896,256]{1,0:T(8,128)(2,1)S(1)} %get-tuple-element.62), channel_id=1, source_target_pairs={{0,1},{1,0},{2,3},{3,2},{4,5},{5,4},{6,7},{7,6},{8,9},{9,8},{10,11... | collective-permute-start | bytes 1376264 | tf_op jit(solution)/shard_map/ppermute | solution.py:457

commit v6 on v5

--- a/solution.py
+++ b/solution.py
@@ -12,6 +12,7 @@
 LN = 3480
 LANES = 128
 BATCH = 16
+GROUP = 2
 SPAN = 128
 WIDTH = 256
 
@@ -86,9 +87,9 @@
         (conn, ids, scales, at, pot, stiff, _, _, came_low, came_high,
          field, total, below, above, gathered, products, wide) = refs
     dofs = stiff.shape[0]
-    cells = conn.shape[0] // dofs
+    cells = conn.shape[0] * LANES // dofs
     count = ids.shape[0] // 2
-    tiles = gathered.shape[0] // dofs
+    tiles = gathered.shape[0] // (GROUP * dofs)
     nodes = field.shape[0] // tiles
     if step == 0:
         width = 512
@@ -107,32 +108,53 @@
     else:
         add_faces(field, (came_low, came_high), wide, ids, at, slope(scales, min(step, 2)))
 
-    def gather(cell, base, size):
-        for i in range(size):
-            row = conn[cell * dofs + base + i]
-            gathered[pl.ds((base + i) * tiles, tiles), :] = field[pl.ds(row, tiles), :]
-
-    def scatter_and_gather(cell, following, base, size):
-        rows = [pl.ds(conn[cell * dofs + base + i], tiles) for i in range(size)]
-        old = [total[row, :] for row in rows]
-        new = [old[i] + products[pl.ds((base + i) * tiles, tiles), :] for i in range(size)]
-        for i in range(size):
-            total[rows[i], :] = new[i]
-        gather(following, base, size)
-
-    batches(dofs, BATCH, functools.partial(gather, 0))
-
-    def one_cell(cell, carry):
+    lines = conn.shape[0] // cells * GROUP
+
+    def gather(line, base):
+        for i in range(BATCH):
+            gathered[pl.ds((line % lines * LANES + base + i) * tiles, tiles), :] = field[
+                pl.ds(conn[line, base + i], tiles), :]
+
+    def gather_line(line):
+        for base in range(0, LANES, BATCH):
+            gather(line, base)
+
+    def scatter_line(line, following):
+        for base in range(0, LANES, BATCH):
+            rows = [pl.ds(conn[line, base + i], tiles) for i in range(BATCH)]
+            old = [total[row, :] for row in rows]
+            first = (line % lines * LANES + base) * tiles
+            new = [old[i] + products[pl.ds(first + i * tiles, tiles), :] for i in range(BATCH)]
+            for i in range(BATCH):
+                total[rows[i], :] = new[i]
+            gather(following, base)
+
+    def begin(line, carry):
+        gather_line(line)
+        return carry
+
+    lax.fori_loop(0, lines, begin, 0)
+
+    def some_cells(group, carry):
         values = jnp.concatenate(
-            [gathered[pl.ds(j, dofs, tiles), :].astype(jnp.bfloat16) for j in range(tiles)], axis=1)
-        result = jnp.dot(stiff[...], values, preferred_element_type=jnp.float32) * scales[cell]
-        for j in range(tiles):
-            products[pl.ds(j, dofs, tiles), :] = result[:, j * LANES:(j + 1) * LANES]
-        following = jnp.minimum(cell + 1, cells - 1)
-        batches(dofs, BATCH, functools.partial(scatter_and_gather, cell, following))
+            [gathered[pl.ds(c * dofs * tiles + j, dofs, tiles), :].astype(jnp.bfloat16)
+             for c in range(GROUP) for j in range(tiles)], axis=1)
+        result = jnp.dot(stiff[...], values, preferred_element_type=jnp.float32)
+        for c in range(GROUP):
+            scale = scales[group * GROUP + c]
+            for j in range(tiles):
+                at_lane = (c * tiles + j) * LANES
+                products[pl.ds(c * dofs * tiles + j, dofs, tiles), :] = result[:, at_lane:at_lane + LANES] * scale
+        following = jnp.minimum(group + 1, cells // GROUP - 1)
+
+        def some(r, carried):
+            scatter_line(group * lines + r, following * lines + r)
+            return carried
+
+        lax.fori_loop(0, lines, some, 0)
         return carry
 
-    lax.fori_loop(0, cells, one_cell, 0)
+    lax.fori_loop(0, cells // GROUP, some_cells, 0)
 
     for slot, faces in enumerate((below, above)):
         offset = side_of(slot, at) * count
@@ -186,16 +208,16 @@
             field, start + k * width, width, tiles).astype(away.dtype)
 
 
-def turn_kernel(ids, at, before, field, turned, own_first, own_second, own_masked, gram):
+def turn_kernel(ids, at, before, field, turned, own, own_masked, gram):
     count = ids.shape[0] // 2
     states, nodes = turned.shape
     tiles = states // LANES
-    quarter = own_first.shape[0]
-    half = 2 * quarter
+    half = own.shape[0]
     start = pl.multiple_of(at[0] * half, LANES)
-    for k, own in enumerate((own_first, own_second)):
-        own[...] = node_rows(field, start + k * quarter, quarter, tiles).astype(own.dtype)
     width = WIDTH
+    for k in range(half // width):
+        own[k * width:(k + 1) * width, :] = node_rows(
+            field, start + k * width, width, tiles).astype(own.dtype)
     for k in range(nodes // width):
         turned[:, k * width:(k + 1) * width] = node_rows(field, k * width, width, tiles).T.astype(turned.dtype)
 
@@ -271,7 +293,7 @@
     out[...] = (result / jnp.sqrt(scale)).astype(jnp.bfloat16)
 
 
-def rotate_kernel(at, columns, turned, first, rest_first, rest_second, out):
+def rotate_kernel(at, columns, turned, first, rest, out):
     states, nodes = out.shape
     half = nodes // 2
     own = columns[pl.ds(pl.multiple_of(at[0] * states, states), states), :]
@@ -287,16 +309,14 @@
         out[:, pl.ds(base, width)] = value.astype(out.dtype)
 
     part_of(at[0] * half, first)
-    away = (1 - at[0]) * half
-    part_of(away, rest_first)
-    part_of(away + rest_first.shape[0], rest_second)
+    part_of((1 - at[0]) * half, rest)
 
 
 def rotate_call(at, columns, turned, *came):
     return pl.pallas_call(
         rotate_kernel,
         out_shape=struct(turned.shape, jnp.bfloat16),
-        in_specs=[SMEM] + [VMEM] * 5, out_specs=VMEM, compiler_params=limit(26), name="rotate",
+        in_specs=[SMEM] + [VMEM] * 4, out_specs=VMEM, compiler_params=limit(26), name="rotate",
     )(at, columns, turned, *came)
 
 
@@ -329,8 +349,8 @@
     if step == 0:
         out_shape += [whole, struct(stiff.shape, stiff.dtype)]
     scratch = [
-        pltpu.VMEM((dofs * tiles, LANES), f32),
-        pltpu.VMEM((dofs * tiles, LANES), f32),
+        pltpu.VMEM((GROUP * dofs * tiles, LANES), f32),
+        pltpu.VMEM((GROUP * dofs * tiles, LANES), f32),
         pltpu.VMEM((count * tiles, LANES), f32),
     ]
     specs = [VMEM] * (2 + len(fields))
@@ -432,12 +452,12 @@
     half = nodes // 2
     square = struct((states, states))
     came = lax.ppermute(away, "st", swap)
-    _, turned, own_first, own_second, own_masked, gram = pl.pallas_call(
+    _, turned, own, own_masked, gram = pl.pallas_call(
         turn_kernel,
         out_shape=[struct(field.shape), struct((states, nodes), bf16),
-                   struct((half // 2, states), bf16), struct((half // 2, states), bf16),
+                   struct((half, states), bf16),
                    struct((states, half), bf16), square],
-        in_specs=[SMEM, SMEM, VMEM], out_specs=[VMEM] * 6,
+        in_specs=[SMEM, SMEM, VMEM], out_specs=[VMEM] * 5,
         input_output_aliases={2: 0},
         compiler_params=limit(26), name="turn",
         cost_estimate=pl.CostEstimate(flops=4 * 10**9, bytes_accessed=10**7, transcendentals=0),
@@ -451,10 +471,9 @@
         out_shape=square,
         in_specs=[SMEM, VMEM, VMEM], out_specs=VMEM, compiler_params=limit(16), name="cross",
     )(at, own_masked, came)
-    rest_first = lax.ppermute(own_first, "st", swap)
     cross_sum = sum_scatter(cross, here)
     sums = sum_last(own_sum, cross_sum, place[0])
-    rest_second = lax.ppermute(own_second, "st", swap)
+    rest = lax.ppermute(own, "st", swap)
     blocks = gather_all(sums, here)
     columns = pl.pallas_call(
         root_kernel,
@@ -463,7 +482,7 @@
         scratch_shapes=[pltpu.VMEM((2 * states, 2 * states), f32), pltpu.VMEM((2, 2 * states, 2 * states), bf16)],
         compiler_params=limit(26), name="root",
     )(at, blocks)
-    return rotate_call(at, columns, turned, came, rest_first, rest_second)
+    return rotate_call(at, columns, turned, came, rest)
 
 
 def rotate_any(current, owned):
@@ -484,7 +503,7 @@
     states = tiles * LANES
     if states != block_states:
         start_states = jnp.pad(start_states, ((0, states - block_states), (0, 0)))
-    conn = connectivity.reshape(-1) * tiles
+    conn = connectivity.reshape(-1, LANES) * tiles
     ids = shared_nodes.reshape(-1) * tiles
     numbers = jnp.concatenate([cell_scale, filter_bounds])
     at = jnp.stack([lax.axis_index("st"), lax.axis_index("dom")])

time: 171 us -> 156 us (0.912)
  waiting for transfers between devices: 33.5 us -> 25.1 us
  Pallas kernels: 70.7 us -> 65.6 us
    ppermute x2 -> x1, waiting for transfers between devices: 14 us -> 4.59 us  [rotate_pair(): rest = lax.ppermute(own, 'st', swap)]
    pallas_call x3, Pallas kernels: 49.4 us -> 44.2 us  [apply_call(): pl.pallas_call(functools.partial(apply_kernel, step), out_shape=out_shape...]
    ppermute x8, starting transfers between devices: 21.8 us -> 25.1 us  [sum_scatter(): lax.ppermute(lax.dynamic_slice_in_dim(x, (code ^ m) * size, size, x.ndim...]
    unnamed x17 -> x14, local copies, waits for them, and re-layouts: 6.8 us -> 6.28 us
  transfers between devices with their start and end apart: 24 -> 23, of which waited for: 14 -> 14; matrix products, arithmetic and copies ran while one was open for 2% -> 1% of each run, Pallas kernels for 7% -> 8%
where the time goes in v6:
time: 156 us
  Pallas kernels  65.6 us (42%)
  starting transfers between devices  52.6 us (34%)
  waiting for transfers between devices  25.1 us (16%)
  local copies, waits for them, and re-layouts  7.21 us (5%)
  between operations  2.92 us (2%)
  other arithmetic  2.35 us (2%)
    pallas_call x3, Pallas kernels, apply_call(): pl.pallas_call(functools.partial(apply_kernel, step), out_shape=out_shape...  44.2 us
    ppermute x8, starting transfers between devices, sum_scatter(): lax.ppermute(lax.dynamic_slice_in_dim(x, (code ^ m) * size, size, x.ndim...  25.1 us
    ppermute x6, starting transfers between devices, paired(): return lax.ppermute(x, axis, pairs)  16.8 us
    ppermute x8, waiting for transfers between devices, sum_scatter(): lax.ppermute(lax.dynamic_slice_in_dim(x, (code ^ m) * size, size, x.ndim...  10 us
    pallas_call x1, Pallas kernels, rotate_pair(): pl.pallas_call(root_kernel, out_shape=struct((2 * states, states), bf16),...  6.46 us
    unnamed x14, local copies, waits for them, and re-layouts  6.28 us
    pallas_call x3, Pallas kernels, settle_call(): pl.pallas_call(functools.partial(settle_kernel, step, last), out_shape=[w...  5.87 us
    ppermute x4, waiting for transfers between devices, gather_all(): lax.ppermute(x, 'dom', [(i, i ^ mask) for i in range(devices)])  5.54 us
  transfers between devices with their start and end apart: 23, of which 14 were waited for; matrix products, arithmetic and copies ran while one was open for 1% of the time, Pallas kernels for 8%

profile of v6, /device:TPU:0, one launch (start us, length us, event | category | flops | bytes accessed | tf_op | source)
XLA Modules:
  0.0 155.8 jit_solution(8011165743711980108)
XLA Ops:
  0.0 0.7 broadcast_multiply_fusion.1
  0.7 0.1 mul.51.refs_1_.ids
  0.8 0.7 broadcast_multiply_fusion
  1.5 0.1 pad_add_fusion.refs_3_.at
  1.6 0.7 pad_maximum_fusion.2.refs_2_.refs_0_.bounds
  2.3 1.5 copy-done
  3.8 1.0 copy-done.3
  4.9 0.7 copy-done.4
  5.6 14.5 %apply.3 = (f32[7168,128]{1,0:T(8,128)S(1)}, f32[7168,128]{1,0:T(8,128)S(1)}, bf16[870,128]{1,0:T(8,128)(2,1)S(1)}, bf16[870,128]{1,0:T(8,128)(2,1)S(1)}, f32[71...) custom-call(s32[32,128]{1,0:T(8,128)S(1)} %mul.54.refs_0_, s32[870]{0:T(1024)S(1)} %mul.51.refs_1_.ids, ...), custom_call_target="tpu_custom_call" | custom-call | tf_op jit(solution)/shard_map/apply/pallas_call | solution.py:357
  20.1 0.6 collective-permute-start
  20.7 0.7 collective-permute-start.1
  21.3 1.7 %settle.3 = (f32[7168,128]{1,0:T(8,128)S(1)}, f32[7168,128]{1,0:T(8,128)S(1)}) custom-call(f32[10]{0:T(128)S(1)} %pad_maximum_fusion.2.refs_2_.refs_0_.bounds, f32[7168,128]{1,0:T(8,128)S(1)} %get-tuple-element.33.refs_1_.refs_4_, f32[7168,128]{1,0:T(8,128)S(1)} %get-tuple-element.35.refs_2_.refs_4_, ...), custom_call_target="tpu_custom_call", output_to_operand_aliasing={{1}: (3, {})} | custom-call | flops 8000000000 | bytes 10000000 | tf_op jit(solution)/shard_map/settle/pallas_call | solution.py:375
  23.0 0.0 collective-permute-done.refs_8_
  23.0 14.9 %apply.4 = (f32[7168,128]{1,0:T(8,128)S(1)}, f32[7168,128]{1,0:T(8,128)S(1)}, bf16[870,128]{1,0:T(8,128)(2,1)S(1)}, bf16[870,128]{1,0:T(8,128)(2,1)S(1)}) custom-call(s32[32,128]{1,0:T(8,128)S(1)} %mul.54.refs_0_, s32[870]{0:T(1024)S(1)} %mul.51.refs_1_.ids, ...), custom_call_target="tpu_custom_call", output_to_operand_aliasing={{0}: (6, {}), {1}: (7, {})} | custom-call | tf_op jit(solution)/shard_map/apply/pallas_call | solution.py:357
  37.9 7.5 %collective-permute-start.2 = (bf16[870,128]{1,0:T(8,128)(2,1)S(1)}, bf16[870,128]{1,0:T(8,128)(2,1)S(1)}, u32[]{:S(2)}, u32[]{:S(2)}) collective-permute-start(bf16[870,128]{1,0:T(8,128)(2,1)S(1)} %get-tuple-element.45), channel_id=1, source_target_pairs={{0,2},{4,6},{8,10},{12,14},{16,18},{20,22},{24,26},{28,30},{2,0},{... | collective-permute-start | bytes 668168 | tf_op jit(solution)/shard_map/ppermute | solution.py:24
  45.4 0.7 collective-permute-start.3
  46.1 2.3 %settle.4 = (f32[7168,128]{1,0:T(8,128)S(1)}, f32[7168,128]{1,0:T(8,128)S(1)}) custom-call(f32[10]{0:T(128)S(1)} %pad_maximum_fusion.2.refs_2_.refs_0_.bounds, f32[7168,128]{1,0:T(8,128)S(1)} %get-tuple-element.33.refs_1_.refs_4_, f32[7168,128]{1,0:T(8,128)S(1)} %get-tuple-element.41.refs_2_.refs_4_, ...), custom_call_target="tpu_custom_call", output_to_operand_aliasing={{0}: (4, {}), {1}: (3, {})} | custom-call | flops 8000000000 | bytes 10000000 | tf_op jit(solution)/shard_map/settle/pallas_call | solution.py:375
  48.4 0.0 collective-permute-done.3.refs_9_
  48.4 14.9 %apply.5 = (f32[7168,128]{1,0:T(8,128)S(1)}, f32[7168,128]{1,0:T(8,128)S(1)}, bf16[870,128]{1,0:T(8,128)(2,1)S(1)}, bf16[870,128]{1,0:T(8,128)(2,1)S(1)}) custom-call(s32[32,128]{1,0:T(8,128)S(1)} %mul.54.refs_0_, s32[870]{0:T(1024)S(1)} %mul.51.refs_1_.ids, ...), custom_call_target="tpu_custom_call", output_to_operand_aliasing={{0}: (6, {}), {1}: (7, {})} | custom-call | tf_op jit(solution)/shard_map/apply/pallas_call | solution.py:357
  63.3 6.7 %collective-permute-start.4 = (bf16[870,128]{1,0:T(8,128)(2,1)S(1)}, bf16[870,128]{1,0:T(8,128)(2,1)S(1)}, u32[]{:S(2)}, u32[]{:S(2)}) collective-permute-start(bf16[870,128]{1,0:T(8,128)(2,1)S(1)} %get-tuple-element.49), channel_id=1, source_target_pairs={{0,2},{4,6},{8,10},{12,14},{16,18},{20,22},{24,26},{28,30},{2,0},{... | collective-permute-start | bytes 668168 | tf_op jit(solution)/shard_map/ppermute | solution.py:24
  70.0 0.7 collective-permute-start.5
  70.7 1.9 %settle.5.before = f32[7168,128]{1,0:T(8,128)S(1)} custom-call(f32[10]{0:T(128)S(1)} %pad_maximum_fusion.2.refs_2_.refs_0_.bounds, f32[7168,128]{1,0:T(8,128)S(1)} %get-tuple-element.33.refs_1_.refs_4_, f32[7168,128]{1,0:T(8,128)S(1)} %get-tuple-element.47.refs_2_, f32[7168,128]{1,0:T(8,128)S(1)} %get-tuple-element.48.refs_3_, ...), custom_call_target="tpu_custom_call", output_to_operand_aliasing={{}: (4, {})} | custom-call | flops 8000000000 | bytes 10000000 | tf_op jit(solution)/shard_map/settle/pallas_call | solution.py:375
  72.6 0.0 collective-permute-done.4.came_low
  72.6 0.0 collective-permute-done.5.came_high
  72.6 3.2 %send.1 = (f32[7168,128]{1,0:T(8,128)S(1)}, bf16[1792,256]{1,0:T(8,128)(2,1)}) custom-call(s32[870]{0:T(1024)S(1)} %mul.51.refs_1_.ids, f32[10]{0:T(128)S(1)} %pad_maximum_fusion.2.refs_2_.refs_0_.bounds, s32[2]{0:T(128)S(1)} %pad_add_fusion.refs_3_.at, f32[7168,128]{1,0:T(8,128)S(1)} %settle.5.before, ...), custom_call_target="tpu_custom_call", output_to_operand_aliasing={{0}: (3, {})} | custom-call | tf_op jit(solution)/shard_map/send/pallas_call | solution.py:526
  75.8 1.8 %turn.1 = (f32[7168,128]{1,0:T(8,128)S(1)}, bf16[256,3584]{1,0:T(8,128)(2,1)S(1)}, bf16[1792,256]{1,0:T(8,128)(2,1)S(1)}, bf16[256,1792]{1,0:T(8,128)(2,1)S(1)}, f32[256,256]{1,0:T(8,128)S(1)}) custom-call(s32[870]{0:T(1024)S(1)} %mul.51.refs_1_.ids, s32[2]{0:T(128)S(1)} %pad_add_fusion.refs_3_.at, ...), custom_call_target="tpu_custom_call", output_to_operand_aliasing={{0}: (2, {})} | custom-call | flops 4000000000 | bytes 10000000 | tf_op jit(solution)/shard_map/turn/pallas_call | solution.py:455
  77.6 0.9 copy-done.1
  78.5 0.9 copy-done.5
  79.4 1.5 collective-permute-start.10
  80.9 0.6 fusion.1
  82.2 7.3 %collective-permute-start.6 = (f32[128,256]{1,0:T(8,128)S(1)}, f32[128,256]{1,0:T(8,128)S(1)}, u32[]{:S(2)}, u32[]{:S(2)}) collective-permute-start(f32[128,256]{1,0:T(8,128)S(1)} %constant_dynamic-slice_fusion.7), channel_id=1, source_target_pairs={{0,2},{2,0},{4,6},{6,4},{8,10},{10,8},{12,14},{14,12},{16,18},{18,... | collective-permute-start | bytes 393224 | tf_op jit(solution)/shard_map/ppermute | solution.py:407
  90.9 2.7 %collective-permute-start.7 = (f32[32,256]{1,0:T(8,128)S(1)}, f32[32,256]{1,0:T(8,128)S(1)}, u32[]{:S(2)}, u32[]{:S(2)}) collective-permute-start(f32[32,256]{1,0:T(8,128)S(1)} %get-tuple-element.67), channel_id=1, source_target_pairs={{0,4},{2,6},{4,0},{6,2},{8,12},{10,14},{12,8},{14,10},{16,20},{18,... | collective-permute-start | bytes 98312 | tf_op jit(solution)/shard_map/ppermute | solution.py:407
  93.6 1.6 %collective-permute-start.8 = (f32[32,256]{1,0:T(8,128)S(1)}, f32[32,256]{1,0:T(8,128)S(1)}, u32[]{:S(2)}, u32[]{:S(2)}) collective-permute-start(f32[32,256]{1,0:T(8,128)S(1)} %get-tuple-element.69), channel_id=1, source_target_pairs={{0,8},{2,10},{4,12},{6,14},{8,0},{10,2},{12,4},{14,6},{16,24},{18,... | collective-permute-start | bytes 98312 | tf_op jit(solution)/shard_map/ppermute | solution.py:407
  95.2 0.1 collective-permute-start.9
  95.3 0.3 collective-permute-done.7
  95.7 1.9 %collective-permute-done.8 = f32[32,256]{1,0:T(8,128)S(1)} collective-permute-done((f32[32,256]{1,0:T(8,128)S(1)}, f32[32,256]{1,0:T(8,128)S(1)}, u32[]{:S(2)}, u32[]{:S(2)}) %collective-permute-start.8) | collective-permute-done | bytes 32800 | tf_op jit(solution)/shard_map/ppermute | solution.py:407
  97.6 2.4 %collective-permute-done.9 = f32[32,256]{1,0:T(8,128)S(1)} collective-permute-done((f32[32,256]{1,0:T(8,128)S(1)}, f32[32,256]{1,0:T(8,128)S(1)}, u32[]{:S(2)}, u32[]{:S(2)}) %collective-permute-start.9) | collective-permute-done | bytes 32800 | tf_op jit(solution)/shard_map/ppermute | solution.py:407
  100.1 1.2 copy-done.2
  101.2 1.1 cross.1
  102.4 2.7 %collective-permute-start.11 = (f32[128,256]{1,0:T(8,128)S(1)}, f32[128,256]{1,0:T(8,128)S(1)}, u32[]{:S(2)}, u32[]{:S(2)}) collective-permute-start(f32[128,256]{1,0:T(8,128)S(1)} %constant_dynamic-slice_fusion.3), channel_id=1, source_target_pairs={{0,2},{2,0},{4,6},{6,4},{8,10},{10,8},{12,14},{14,12},{16,18},{18,... | collective-permute-start | bytes 393224 | tf_op jit(solution)/shard_map/ppermute | solution.py:407
  105.1 1.0 collective-permute-done.11
  106.1 8.6 %collective-permute-start.12 = (f32[32,256]{1,0:T(8,128)S(1)}, f32[32,256]{1,0:T(8,128)S(1)}, u32[]{:S(2)}, u32[]{:S(2)}) collective-permute-start(f32[32,256]{1,0:T(8,128)S(1)} %get-tuple-element.64), channel_id=1, source_target_pairs={{0,4},{2,6},{4,0},{6,2},{8,12},{10,14},{12,8},{14,10},{16,20},{18,... | collective-permute-start | bytes 98312 | tf_op jit(solution)/shard_map/ppermute | solution.py:407
  114.8 1.6 %collective-permute-start.13 = (f32[32,256]{1,0:T(8,128)S(1)}, f32[32,256]{1,0:T(8,128)S(1)}, u32[]{:S(2)}, u32[]{:S(2)}) collective-permute-start(f32[32,256]{1,0:T(8,128)S(1)} %get-tuple-element.66), channel_id=1, source_target_pairs={{0,8},{2,10},{4,12},{6,14},{8,0},{10,2},{12,4},{14,6},{16,24},{18,... | collective-permute-start | bytes 98312 | tf_op jit(solution)/shard_map/ppermute | solution.py:407
  116.4 0.4 collective-permute-start.14
  116.8 1.9 %collective-permute-done.13 = f32[32,256]{1,0:T(8,128)S(1)} collective-permute-done((f32[32,256]{1,0:T(8,128)S(1)}, f32[32,256]{1,0:T(8,128)S(1)}, u32[]{:S(2)}, u32[]{:S(2)}) %collective-permute-start.13) | collective-permute-done | bytes 32800 | tf_op jit(solution)/shard_map/ppermute | solution.py:407
  118.7 2.5 %collective-permute-done.14 = f32[32,256]{1,0:T(8,128)S(1)} collective-permute-done((f32[32,256]{1,0:T(8,128)S(1)}, f32[32,256]{1,0:T(8,128)S(1)}, u32[]{:S(2)}, u32[]{:S(2)}) %collective-permute-start.14) | collective-permute-done | bytes 32800 | tf_op jit(solution)/shard_map/ppermute | solution.py:407
  121.2 1.7 %collective-permute-start.15 = (f32[2,32,256]{2,1,0:T(8,128)S(1)}, f32[2,32,256]{2,1,0:T(8,128)S(1)}, u32[]{:S(2)}, u32[]{:S(2)}) collective-permute-start(f32[2,32,256]{2,1,0:T(8,128)S(1)} %pad_maximum_fusion.1), channel_id=1, source_target_pairs={{0,16},{1,17},{2,18},{3,19},{4,20},{5,21},{6,22},{7,23},{8,24},{9,... | collective-permute-start | bytes 196616 | tf_op jit(solution)/shard_map/ppermute | solution.py:427
  123.6 1.7 %collective-permute-start.16 = (f32[2,32,256]{2,1,0:T(8,128)S(1)}, f32[2,32,256]{2,1,0:T(8,128)S(1)}, u32[]{:S(2)}, u32[]{:S(2)}) collective-permute-start(f32[2,32,256]{2,1,0:T(8,128)S(1)} %pad_maximum_fusion.1), channel_id=1, source_target_pairs={{0,1},{1,0},{2,3},{3,2},{4,5},{5,4},{6,7},{7,6},{8,9},{9,8},{10,11... | collective-permute-start | bytes 196616 | tf_op jit(solution)/shard_map/ppermute | solution.py:427
  125.2 1.1 collective-permute-start.17
  126.4 0.7 collective-permute-done.15
  127.0 0.9 collective-permute-done.16
  127.9 3.4 %collective-permute-done.17 = f32[2,32,256]{2,1,0:T(8,128)S(1)} collective-permute-done((f32[2,32,256]{2,1,0:T(8,128)S(1)}, f32[2,32,256]{2,1,0:T(8,128)S(1)}, u32[]{:S(2)}, u32[]{:S(2)}) %collective-permute-start.17) | collective-permute-done | bytes 65568 | tf_op jit(solution)/shard_map/ppermute | solution.py:427
  131.4 2.6 %collective-permute-start.18 = (f32[3,32,256]{2,1,0:T(8,128)S(1)}, f32[3,32,256]{2,1,0:T(8,128)S(1)}, u32[]{:S(2)}, u32[]{:S(2)}) collective-permute-start(f32[3,32,256]{2,1,0:T(8,128)S(1)} %get-tuple-element.70), channel_id=1, source_target_pairs={{0,4},{2,6},{4,0},{6,2},{8,12},{10,14},{12,8},{14,10},{16,20},{18,... | collective-permute-start | bytes 294920 | tf_op jit(solution)/shard_map/ppermute | solution.py:441
  134.0 0.4 collective-permute-start.22
  134.4 1.5 collective-permute-start.20
  136.0 0.7 collective-permute-done.18
  136.6 2.4 %collective-permute-done.19 = f32[3,32,256]{2,1,0:T(8,128)S(1)} collective-permute-done((f32[3,32,256]{2,1,0:T(8,128)S(1)}, f32[3,32,256]{2,1,0:T(8,128)S(1)}, u32[]{:S(2)}, u32[]{:S(2)}) %collective-permute-start.19) | collective-permute-done | bytes 98336 | tf_op jit(solution)/shard_map/ppermute | solution.py:441
  139.1 0.9 collective-permute-done.20
  140.0 0.1 collective-permute-start.21
  140.0 0.1 broadcast_in_dim.6
  140.1 1.6 %collective-permute-done.21 = f32[3,128,256]{2,1,0:T(8,128)S(1)} collective-permute-done((f32[3,128,256]{2,1,0:T(8,128)S(1)}, f32[3,128,256]{2,1,0:T(8,128)S(1)}, u32[]{:S(2)}, u32[]{:S(2)}) %collective-permute-start.21) | collective-permute-done | bytes 393248 | tf_op jit(solution)/shard_map/ppermute | solution.py:441
  141.8 6.5 %root.1.columns = bf16[512,256]{1,0:T(8,128)(2,1)S(1)} custom-call(s32[2]{0:T(128)S(1)} %pad_add_fusion.refs_3_.at, f32[3,256,256]{2,1,0:T(8,128)S(1)} %constant_dynamic-update-slice_fusion.blocks), custom_call_target="tpu_custom_call" | custom-call | tf_op jit(solution)/shard_map/root/pallas_call | solution.py:478
  148.2 4.6 %collective-permute-done.22.rest = bf16[1792,256]{1,0:T(8,128)(2,1)S(1)} collective-permute-done((bf16[1792,256]{1,0:T(8,128)(2,1)S(1)}, bf16[1792,256]{1,0:T(8,128)(2,1)S(1)}, u32[]{:S(2)}, u32[]{:S(2)}) %collective-permute-start.22) | collective-permute-done | bytes 917536 | tf_op jit(solution)/shard_map/ppermute | solution.py:476
  152.8 2.9 %rotate.1 = bf16[256,3584]{1,0:T(8,128)(2,1)} custom-call(s32[2]{0:T(128)S(1)} %pad_add_fusion.refs_3_.at, bf16[512,256]{1,0:T(8,128)(2,1)S(1)} %root.1.columns, bf16[256,3584]{1,0:T(8,128)(2,1)S(1)} %get-tuple-element.59.turned, bf16[1792,256]{1,0:T(8,128)(2,1)S(1)} %collective-permute-done.10.came.first, bf16[1792,256]{1,0:T(8,128)(2,1)S(1)} %collective-permute-done.22.rest), custom_call_target="tpu_custom_call" | custom-call | tf_op jit(solution)/shard_map/rotate/pallas_call | solution.py:316
  (34 shorter events, 0.3 us)
Async XLA Ops:
  2.3 1.5 copy-start
  3.8 1.0 copy-start.3
  4.9 0.7 copy-start.4
  20.1 2.9 %collective-permute-start = (bf16[870,128]{1,0:T(8,128)(2,1)S(1)}, bf16[870,128]{1,0:T(8,128)(2,1)S(1)}, u32[]{:S(2)}, u32[]{:S(2)}) collective-permute-start(bf16[870,128]{1,0:T(8,128)(2,1)S(1)} %get-tuple-element.39), channel_id=1, source_target_pairs={{0,2},{4,6},{8,10},{12,14},{16,18},{20,22},{24,26},{28,30},{2,0},{... | collective-permute-start | bytes 668168 | tf_op jit(solution)/shard_map/ppermute | solution.py:24
  20.7 2.4 %collective-permute-start.1 = (bf16[870,128]{1,0:T(8,128)(2,1)S(1)}, bf16[870,128]{1,0:T(8,128)(2,1)S(1)}, u32[]{:S(2)}, u32[]{:S(2)}) collective-permute-start(bf16[870,128]{1,0:T(8,128)(2,1)S(1)} %get-tuple-element.40), channel_id=1, source_target_pairs={{2,4},{6,8},{10,12},{14,16},{18,20},{22,24},{26,28},{4,2},{8,6},{1... | collective-permute-start | bytes 668168 | tf_op jit(solution)/shard_map/ppermute | solution.py:24
  37.9 10.5 %collective-permute-start.2 = (bf16[870,128]{1,0:T(8,128)(2,1)S(1)}, bf16[870,128]{1,0:T(8,128)(2,1)S(1)}, u32[]{:S(2)}, u32[]{:S(2)}) collective-permute-start(bf16[870,128]{1,0:T(8,128)(2,1)S(1)} %get-tuple-element.45), channel_id=1, source_target_pairs={{0,2},{4,6},{8,10},{12,14},{16,18},{20,22},{24,26},{28,30},{2,0},{... | collective-permute-start | bytes 668168 | tf_op jit(solution)/shard_map/ppermute | solution.py:24
  45.4 3.0 %collective-permute-start.3 = (bf16[870,128]{1,0:T(8,128)(2,1)S(1)}, bf16[870,128]{1,0:T(8,128)(2,1)S(1)}, u32[]{:S(2)}, u32[]{:S(2)}) collective-permute-start(bf16[870,128]{1,0:T(8,128)(2,1)S(1)} %get-tuple-element.46), channel_id=1, source_target_pairs={{2,4},{6,8},{10,12},{14,16},{18,20},{22,24},{26,28},{4,2},{8,6},{1... | collective-permute-start | bytes 668168 | tf_op jit(solution)/shard_map/ppermute | solution.py:24
  63.3 9.3 %collective-permute-start.4 = (bf16[870,128]{1,0:T(8,128)(2,1)S(1)}, bf16[870,128]{1,0:T(8,128)(2,1)S(1)}, u32[]{:S(2)}, u32[]{:S(2)}) collective-permute-start(bf16[870,128]{1,0:T(8,128)(2,1)S(1)} %get-tuple-element.49), channel_id=1, source_target_pairs={{0,2},{4,6},{8,10},{12,14},{16,18},{20,22},{24,26},{28,30},{2,0},{... | collective-permute-start | bytes 668168 | tf_op jit(solution)/shard_map/ppermute | solution.py:24
  70.0 2.6 %collective-permute-start.5 = (bf16[870,128]{1,0:T(8,128)(2,1)S(1)}, bf16[870,128]{1,0:T(8,128)(2,1)S(1)}, u32[]{:S(2)}, u32[]{:S(2)}) collective-permute-start(bf16[870,128]{1,0:T(8,128)(2,1)S(1)} %get-tuple-element.50), channel_id=1, source_target_pairs={{2,4},{6,8},{10,12},{14,16},{18,20},{22,24},{26,28},{4,2},{8,6},{1... | collective-permute-start | bytes 668168 | tf_op jit(solution)/shard_map/ppermute | solution.py:24
  77.6 0.9 copy-start.1
  78.5 0.9 copy-start.5
  79.4 20.6 %collective-permute-start.10 = (bf16[1792,256]{1,0:T(8,128)(2,1)}, bf16[1792,256]{1,0:T(8,128)(2,1)S(1)}, u32[]{:S(2)}, u32[]{:S(2)}) collective-permute-start(bf16[1792,256]{1,0:T(8,128)(2,1)} %get-tuple-element.58), channel_id=1, source_target_pairs={{0,1},{1,0},{2,3},{3,2},{4,5},{5,4},{6,7},{7,6},{8,9},{9,8},{10,11... | collective-permute-start | bytes 2752520 | tf_op jit(solution)/shard_map/ppermute | solution.py:454
  82.2 8.6 %collective-permute-start.6 = (f32[128,256]{1,0:T(8,128)S(1)}, f32[128,256]{1,0:T(8,128)S(1)}, u32[]{:S(2)}, u32[]{:S(2)}) collective-permute-start(f32[128,256]{1,0:T(8,128)S(1)} %constant_dynamic-slice_fusion.7), channel_id=1, source_target_pairs={{0,2},{2,0},{4,6},{6,4},{8,10},{10,8},{12,14},{14,12},{16,18},{18,... | collective-permute-start | bytes 393224 | tf_op jit(solution)/shard_map/ppermute | solution.py:407
  90.9 4.8 %collective-permute-start.7 = (f32[32,256]{1,0:T(8,128)S(1)}, f32[32,256]{1,0:T(8,128)S(1)}, u32[]{:S(2)}, u32[]{:S(2)}) collective-permute-start(f32[32,256]{1,0:T(8,128)S(1)} %get-tuple-element.67), channel_id=1, source_target_pairs={{0,4},{2,6},{4,0},{6,2},{8,12},{10,14},{12,8},{14,10},{16,20},{18,... | collective-permute-start | bytes 98312 | tf_op jit(solution)/shard_map/ppermute | solution.py:407
  93.6 3.9 %collective-permute-start.8 = (f32[32,256]{1,0:T(8,128)S(1)}, f32[32,256]{1,0:T(8,128)S(1)}, u32[]{:S(2)}, u32[]{:S(2)}) collective-permute-start(f32[32,256]{1,0:T(8,128)S(1)} %get-tuple-element.69), channel_id=1, source_target_pairs={{0,8},{2,10},{4,12},{6,14},{8,0},{10,2},{12,4},{14,6},{16,24},{18,... | collective-permute-start | bytes 98312 | tf_op jit(solution)/shard_map/ppermute | solution.py:407
  95.2 4.8 %collective-permute-start.9 = (f32[32,256]{1,0:T(8,128)S(1)}, f32[32,256]{1,0:T(8,128)S(1)}, u32[]{:S(2)}, u32[]{:S(2)}) collective-permute-start(f32[32,256]{1,0:T(8,128)S(1)} %get-tuple-element.68), channel_id=1, source_target_pairs={{0,12},{2,14},{4,8},{6,10},{8,4},{10,6},{12,0},{14,2},{16,28},{18,... | collective-permute-start | bytes 98312 | tf_op jit(solution)/shard_map/ppermute | solution.py:407
  100.1 1.2 copy-start.2
  101.2 32.8 %copy-start.6 = (bf16[1792,256]{1,0:T(8,128)(2,1)S(1)}, bf16[1792,256]{1,0:T(8,128)(2,1)}, u32[]{:S(2)}) copy-start(bf16[1792,256]{1,0:T(8,128)(2,1)} %copy-done.5) | copy-start | bytes 2752516
  102.4 3.7 %collective-permute-start.11 = (f32[128,256]{1,0:T(8,128)S(1)}, f32[128,256]{1,0:T(8,128)S(1)}, u32[]{:S(2)}, u32[]{:S(2)}) collective-permute-start(f32[128,256]{1,0:T(8,128)S(1)} %constant_dynamic-slice_fusion.3), channel_id=1, source_target_pairs={{0,2},{2,0},{4,6},{6,4},{8,10},{10,8},{12,14},{14,12},{16,18},{18,... | collective-permute-start | bytes 393224 | tf_op jit(solution)/shard_map/ppermute | solution.py:407
  106.1 10.7 %collective-permute-start.12 = (f32[32,256]{1,0:T(8,128)S(1)}, f32[32,256]{1,0:T(8,128)S(1)}, u32[]{:S(2)}, u32[]{:S(2)}) collective-permute-start(f32[32,256]{1,0:T(8,128)S(1)} %get-tuple-element.64), channel_id=1, source_target_pairs={{0,4},{2,6},{4,0},{6,2},{8,12},{10,14},{12,8},{14,10},{16,20},{18,... | collective-permute-start | bytes 98312 | tf_op jit(solution)/shard_map/ppermute | solution.py:407
  114.8 3.9 %collective-permute-start.13 = (f32[32,256]{1,0:T(8,128)S(1)}, f32[32,256]{1,0:T(8,128)S(1)}, u32[]{:S(2)}, u32[]{:S(2)}) collective-permute-start(f32[32,256]{1,0:T(8,128)S(1)} %get-tuple-element.66), channel_id=1, source_target_pairs={{0,8},{2,10},{4,12},{6,14},{8,0},{10,2},{12,4},{14,6},{16,24},{18,... | collective-permute-start | bytes 98312 | tf_op jit(solution)/shard_map/ppermute | solution.py:407
  116.4 4.8 %collective-permute-start.14 = (f32[32,256]{1,0:T(8,128)S(1)}, f32[32,256]{1,0:T(8,128)S(1)}, u32[]{:S(2)}, u32[]{:S(2)}) collective-permute-start(f32[32,256]{1,0:T(8,128)S(1)} %get-tuple-element.65), channel_id=1, source_target_pairs={{0,12},{2,14},{4,8},{6,10},{8,4},{10,6},{12,0},{14,2},{16,28},{18,... | collective-permute-start | bytes 98312 | tf_op jit(solution)/shard_map/ppermute | solution.py:407
  121.2 5.8 %collective-permute-start.15 = (f32[2,32,256]{2,1,0:T(8,128)S(1)}, f32[2,32,256]{2,1,0:T(8,128)S(1)}, u32[]{:S(2)}, u32[]{:S(2)}) collective-permute-start(f32[2,32,256]{2,1,0:T(8,128)S(1)} %pad_maximum_fusion.1), channel_id=1, source_target_pairs={{0,16},{1,17},{2,18},{3,19},{4,20},{5,21},{6,22},{7,23},{8,24},{9,... | collective-permute-start | bytes 196616 | tf_op jit(solution)/shard_map/ppermute | solution.py:427
  123.6 4.3 %collective-permute-start.16 = (f32[2,32,256]{2,1,0:T(8,128)S(1)}, f32[2,32,256]{2,1,0:T(8,128)S(1)}, u32[]{:S(2)}, u32[]{:S(2)}) collective-permute-start(f32[2,32,256]{2,1,0:T(8,128)S(1)} %pad_maximum_fusion.1), channel_id=1, source_target_pairs={{0,1},{1,0},{2,3},{3,2},{4,5},{5,4},{6,7},{7,6},{8,9},{9,8},{10,11... | collective-permute-start | bytes 196616 | tf_op jit(solution)/shard_map/ppermute | solution.py:427
  125.2 6.1 %collective-permute-start.17 = (f32[2,32,256]{2,1,0:T(8,128)S(1)}, f32[2,32,256]{2,1,0:T(8,128)S(1)}, u32[]{:S(2)}, u32[]{:S(2)}) collective-permute-start(f32[2,32,256]{2,1,0:T(8,128)S(1)} %pad_maximum_fusion.1), channel_id=1, source_target_pairs={{0,17},{1,16},{2,19},{3,18},{4,21},{5,20},{6,23},{7,22},{8,25},{9,... | collective-permute-start | bytes 196616 | tf_op jit(solution)/shard_map/ppermute | solution.py:427
  131.4 5.2 %collective-permute-start.18 = (f32[3,32,256]{2,1,0:T(8,128)S(1)}, f32[3,32,256]{2,1,0:T(8,128)S(1)}, u32[]{:S(2)}, u32[]{:S(2)}) collective-permute-start(f32[3,32,256]{2,1,0:T(8,128)S(1)} %get-tuple-element.70), channel_id=1, source_target_pairs={{0,4},{2,6},{4,0},{6,2},{8,12},{10,14},{12,8},{14,10},{16,20},{18,... | collective-permute-start | bytes 294920 | tf_op jit(solution)/shard_map/ppermute | solution.py:441
  134.0 18.8 %collective-permute-start.22 = (bf16[1792,256]{1,0:T(8,128)(2,1)S(1)}, bf16[1792,256]{1,0:T(8,128)(2,1)S(1)}, u32[]{:S(2)}, u32[]{:S(2)}) collective-permute-start(bf16[1792,256]{1,0:T(8,128)(2,1)S(1)} %copy-done.6), channel_id=1, source_target_pairs={{0,1},{1,0},{2,3},{3,2},{4,5},{5,4},{6,7},{7,6},{8,9},{9,8},{10,11... | collective-permute-start | bytes 2752520 | tf_op jit(solution)/shard_map/ppermute | solution.py:476
  134.4 4.6 %collective-permute-start.19 = (f32[3,32,256]{2,1,0:T(8,128)S(1)}, f32[3,32,256]{2,1,0:T(8,128)S(1)}, u32[]{:S(2)}, u32[]{:S(2)}) collective-permute-start(f32[3,32,256]{2,1,0:T(8,128)S(1)} %get-tuple-element.70), channel_id=1, source_target_pairs={{0,8},{2,10},{4,12},{6,14},{8,0},{10,2},{12,4},{14,6},{16,24},{18,... | collective-permute-start | bytes 294920 | tf_op jit(solution)/shard_map/ppermute | solution.py:441
  134.4 5.5 %collective-permute-start.20 = (f32[3,32,256]{2,1,0:T(8,128)S(1)}, f32[3,32,256]{2,1,0:T(8,128)S(1)}, u32[]{:S(2)}, u32[]{:S(2)}) collective-permute-start(f32[3,32,256]{2,1,0:T(8,128)S(1)} %get-tuple-element.70), channel_id=1, source_target_pairs={{0,12},{2,14},{4,8},{6,10},{8,4},{10,6},{12,0},{14,2},{16,28},{18,... | collective-permute-start | bytes 294920 | tf_op jit(solution)/shard_map/ppermute | solution.py:441
  140.0 1.8 %collective-permute-start.21 = (f32[3,128,256]{2,1,0:T(8,128)S(1)}, f32[3,128,256]{2,1,0:T(8,128)S(1)}, u32[]{:S(2)}, u32[]{:S(2)}) collective-permute-start(f32[3,128,256]{2,1,0:T(8,128)S(1)} %constant_dynamic-update-slice_fusion.2), channel_id=1, source_target_pairs={{0,2},{2,0},{4,6},{6,4},{8,10},{10,8},{12,14},{14,12},{16,18},{18,... | collective-permute-start | bytes 1179656 | tf_op jit(solution)/shard_map/ppermute | solution.py:441

commit v7 on v6

--- a/solution.py
+++ b/solution.py
@@ -508,8 +508,9 @@
     numbers = jnp.concatenate([cell_scale, filter_bounds])
     at = jnp.stack([lax.axis_index("st"), lax.axis_index("dom")])
 
-    def exchange(low, high):
-        return paired(low, "dom", 0), paired(high, "dom", 1)
+    def exchange(near, far):
+        far = paired(far, "dom", 1)
+        return paired(near, "dom", 0), far
 
     older = None
     current, total, low, high, pot, stiff = apply_call(

time: 156 us -> 156 us (level)
  no operation moved by 1% of the time
where the time goes in v7:
time: 156 us
  Pallas kernels  65.6 us (42%)
  starting transfers between devices  52.6 us (34%)
  waiting for transfers between devices  25.1 us (16%)
  local copies, waits for them, and re-layouts  7.21 us (5%)
  between operations  2.92 us (2%)
  other arithmetic  2.35 us (2%)
    pallas_call x3, Pallas kernels, apply_call(): pl.pallas_call(functools.partial(apply_kernel, step), out_shape=out_shape...  44.2 us
    ppermute x8, starting transfers between devices, sum_scatter(): lax.ppermute(lax.dynamic_slice_in_dim(x, (code ^ m) * size, size, x.ndim...  25.1 us
    ppermute x6, starting transfers between devices, paired(): return lax.ppermute(x, axis, pairs)  16.8 us
    ppermute x8, waiting for transfers between devices, sum_scatter(): lax.ppermute(lax.dynamic_slice_in_dim(x, (code ^ m) * size, size, x.ndim...  10 us
    pallas_call x1, Pallas kernels, rotate_pair(): pl.pallas_call(root_kernel, out_shape=struct((2 * states, states), bf16),...  6.46 us
    unnamed x14, local copies, waits for them, and re-layouts  6.28 us
    pallas_call x3, Pallas kernels, settle_call(): pl.pallas_call(functools.partial(settle_kernel, step, last), out_shape=[w...  5.87 us
    ppermute x4, waiting for transfers between devices, gather_all(): lax.ppermute(x, 'dom', [(i, i ^ mask) for i in range(devices)])  5.54 us
  transfers between devices with their start and end apart: 23, of which 14 were waited for; matrix products, arithmetic and copies ran while one was open for 1% of the time, Pallas kernels for 8%

profile of v7, /device:TPU:0, one launch (start us, length us, event | category | flops | bytes accessed | tf_op | source)
XLA Modules:
  0.0 155.8 jit_solution(8011165743711980108)
XLA Ops:
  0.0 0.7 broadcast_multiply_fusion.1
  0.7 0.1 mul.51.refs_1_.ids
  0.8 0.7 broadcast_multiply_fusion
  1.5 0.1 pad_add_fusion.refs_3_.at
  1.6 0.7 pad_maximum_fusion.2.refs_2_.refs_0_.bounds
  2.3 1.5 copy-done
  3.8 1.0 copy-done.3
  4.9 0.7 copy-done.4
  5.6 14.5 %apply.3 = (f32[7168,128]{1,0:T(8,128)S(1)}, f32[7168,128]{1,0:T(8,128)S(1)}, bf16[870,128]{1,0:T(8,128)(2,1)S(1)}, bf16[870,128]{1,0:T(8,128)(2,1)S(1)}, f32[71...) custom-call(s32[32,128]{1,0:T(8,128)S(1)} %mul.54.refs_0_, s32[870]{0:T(1024)S(1)} %mul.51.refs_1_.ids, ...), custom_call_target="tpu_custom_call" | custom-call | tf_op jit(solution)/shard_map/apply/pallas_call | solution.py:357
  20.1 0.6 collective-permute-start
  20.7 0.7 collective-permute-start.1
  21.3 1.7 %settle.3 = (f32[7168,128]{1,0:T(8,128)S(1)}, f32[7168,128]{1,0:T(8,128)S(1)}) custom-call(f32[10]{0:T(128)S(1)} %pad_maximum_fusion.2.refs_2_.refs_0_.bounds, f32[7168,128]{1,0:T(8,128)S(1)} %get-tuple-element.33.refs_1_.refs_4_, f32[7168,128]{1,0:T(8,128)S(1)} %get-tuple-element.35.refs_2_.refs_4_, ...), custom_call_target="tpu_custom_call", output_to_operand_aliasing={{1}: (3, {})} | custom-call | flops 8000000000 | bytes 10000000 | tf_op jit(solution)/shard_map/settle/pallas_call | solution.py:375
  23.0 0.0 collective-permute-done.refs_8_
  23.0 14.9 %apply.4 = (f32[7168,128]{1,0:T(8,128)S(1)}, f32[7168,128]{1,0:T(8,128)S(1)}, bf16[870,128]{1,0:T(8,128)(2,1)S(1)}, bf16[870,128]{1,0:T(8,128)(2,1)S(1)}) custom-call(s32[32,128]{1,0:T(8,128)S(1)} %mul.54.refs_0_, s32[870]{0:T(1024)S(1)} %mul.51.refs_1_.ids, ...), custom_call_target="tpu_custom_call", output_to_operand_aliasing={{0}: (6, {}), {1}: (7, {})} | custom-call | tf_op jit(solution)/shard_map/apply/pallas_call | solution.py:357
  37.9 7.5 %collective-permute-start.2 = (bf16[870,128]{1,0:T(8,128)(2,1)S(1)}, bf16[870,128]{1,0:T(8,128)(2,1)S(1)}, u32[]{:S(2)}, u32[]{:S(2)}) collective-permute-start(bf16[870,128]{1,0:T(8,128)(2,1)S(1)} %get-tuple-element.45), channel_id=1, source_target_pairs={{0,2},{4,6},{8,10},{12,14},{16,18},{20,22},{24,26},{28,30},{2,0},{... | collective-permute-start | bytes 668168 | tf_op jit(solution)/shard_map/ppermute | solution.py:24
  45.4 0.7 collective-permute-start.3
  46.1 2.3 %settle.4 = (f32[7168,128]{1,0:T(8,128)S(1)}, f32[7168,128]{1,0:T(8,128)S(1)}) custom-call(f32[10]{0:T(128)S(1)} %pad_maximum_fusion.2.refs_2_.refs_0_.bounds, f32[7168,128]{1,0:T(8,128)S(1)} %get-tuple-element.33.refs_1_.refs_4_, f32[7168,128]{1,0:T(8,128)S(1)} %get-tuple-element.41.refs_2_.refs_4_, ...), custom_call_target="tpu_custom_call", output_to_operand_aliasing={{0}: (4, {}), {1}: (3, {})} | custom-call | flops 8000000000 | bytes 10000000 | tf_op jit(solution)/shard_map/settle/pallas_call | solution.py:375
  48.4 0.0 collective-permute-done.3.refs_9_
  48.4 14.9 %apply.5 = (f32[7168,128]{1,0:T(8,128)S(1)}, f32[7168,128]{1,0:T(8,128)S(1)}, bf16[870,128]{1,0:T(8,128)(2,1)S(1)}, bf16[870,128]{1,0:T(8,128)(2,1)S(1)}) custom-call(s32[32,128]{1,0:T(8,128)S(1)} %mul.54.refs_0_, s32[870]{0:T(1024)S(1)} %mul.51.refs_1_.ids, ...), custom_call_target="tpu_custom_call", output_to_operand_aliasing={{0}: (6, {}), {1}: (7, {})} | custom-call | tf_op jit(solution)/shard_map/apply/pallas_call | solution.py:357
  63.3 6.7 %collective-permute-start.4 = (bf16[870,128]{1,0:T(8,128)(2,1)S(1)}, bf16[870,128]{1,0:T(8,128)(2,1)S(1)}, u32[]{:S(2)}, u32[]{:S(2)}) collective-permute-start(bf16[870,128]{1,0:T(8,128)(2,1)S(1)} %get-tuple-element.49), channel_id=1, source_target_pairs={{0,2},{4,6},{8,10},{12,14},{16,18},{20,22},{24,26},{28,30},{2,0},{... | collective-permute-start | bytes 668168 | tf_op jit(solution)/shard_map/ppermute | solution.py:24
  70.0 0.7 collective-permute-start.5
  70.7 1.9 %settle.5.before = f32[7168,128]{1,0:T(8,128)S(1)} custom-call(f32[10]{0:T(128)S(1)} %pad_maximum_fusion.2.refs_2_.refs_0_.bounds, f32[7168,128]{1,0:T(8,128)S(1)} %get-tuple-element.33.refs_1_.refs_4_, f32[7168,128]{1,0:T(8,128)S(1)} %get-tuple-element.47.refs_2_, f32[7168,128]{1,0:T(8,128)S(1)} %get-tuple-element.48.refs_3_, ...), custom_call_target="tpu_custom_call", output_to_operand_aliasing={{}: (4, {})} | custom-call | flops 8000000000 | bytes 10000000 | tf_op jit(solution)/shard_map/settle/pallas_call | solution.py:375
  72.6 0.0 collective-permute-done.4.came_low
  72.6 0.0 collective-permute-done.5.came_high
  72.6 3.2 %send.1 = (f32[7168,128]{1,0:T(8,128)S(1)}, bf16[1792,256]{1,0:T(8,128)(2,1)}) custom-call(s32[870]{0:T(1024)S(1)} %mul.51.refs_1_.ids, f32[10]{0:T(128)S(1)} %pad_maximum_fusion.2.refs_2_.refs_0_.bounds, s32[2]{0:T(128)S(1)} %pad_add_fusion.refs_3_.at, f32[7168,128]{1,0:T(8,128)S(1)} %settle.5.before, ...), custom_call_target="tpu_custom_call", output_to_operand_aliasing={{0}: (3, {})} | custom-call | tf_op jit(solution)/shard_map/send/pallas_call | solution.py:527
  75.8 1.8 %turn.1 = (f32[7168,128]{1,0:T(8,128)S(1)}, bf16[256,3584]{1,0:T(8,128)(2,1)S(1)}, bf16[1792,256]{1,0:T(8,128)(2,1)S(1)}, bf16[256,1792]{1,0:T(8,128)(2,1)S(1)}, f32[256,256]{1,0:T(8,128)S(1)}) custom-call(s32[870]{0:T(1024)S(1)} %mul.51.refs_1_.ids, s32[2]{0:T(128)S(1)} %pad_add_fusion.refs_3_.at, ...), custom_call_target="tpu_custom_call", output_to_operand_aliasing={{0}: (2, {})} | custom-call | flops 4000000000 | bytes 10000000 | tf_op jit(solution)/shard_map/turn/pallas_call | solution.py:455
  77.6 0.9 copy-done.1
  78.5 0.9 copy-done.5
  79.4 1.5 collective-permute-start.10
  80.9 0.6 fusion.1
  82.2 7.3 %collective-permute-start.6 = (f32[128,256]{1,0:T(8,128)S(1)}, f32[128,256]{1,0:T(8,128)S(1)}, u32[]{:S(2)}, u32[]{:S(2)}) collective-permute-start(f32[128,256]{1,0:T(8,128)S(1)} %constant_dynamic-slice_fusion.7), channel_id=1, source_target_pairs={{0,2},{2,0},{4,6},{6,4},{8,10},{10,8},{12,14},{14,12},{16,18},{18,... | collective-permute-start | bytes 393224 | tf_op jit(solution)/shard_map/ppermute | solution.py:407
  90.9 2.7 %collective-permute-start.7 = (f32[32,256]{1,0:T(8,128)S(1)}, f32[32,256]{1,0:T(8,128)S(1)}, u32[]{:S(2)}, u32[]{:S(2)}) collective-permute-start(f32[32,256]{1,0:T(8,128)S(1)} %get-tuple-element.67), channel_id=1, source_target_pairs={{0,4},{2,6},{4,0},{6,2},{8,12},{10,14},{12,8},{14,10},{16,20},{18,... | collective-permute-start | bytes 98312 | tf_op jit(solution)/shard_map/ppermute | solution.py:407
  93.6 1.6 %collective-permute-start.8 = (f32[32,256]{1,0:T(8,128)S(1)}, f32[32,256]{1,0:T(8,128)S(1)}, u32[]{:S(2)}, u32[]{:S(2)}) collective-permute-start(f32[32,256]{1,0:T(8,128)S(1)} %get-tuple-element.69), channel_id=1, source_target_pairs={{0,8},{2,10},{4,12},{6,14},{8,0},{10,2},{12,4},{14,6},{16,24},{18,... | collective-permute-start | bytes 98312 | tf_op jit(solution)/shard_map/ppermute | solution.py:407
  95.2 0.1 collective-permute-start.9
  95.3 0.3 collective-permute-done.7
  95.7 1.9 %collective-permute-done.8 = f32[32,256]{1,0:T(8,128)S(1)} collective-permute-done((f32[32,256]{1,0:T(8,128)S(1)}, f32[32,256]{1,0:T(8,128)S(1)}, u32[]{:S(2)}, u32[]{:S(2)}) %collective-permute-start.8) | collective-permute-done | bytes 32800 | tf_op jit(solution)/shard_map/ppermute | solution.py:407
  97.6 2.4 %collective-permute-done.9 = f32[32,256]{1,0:T(8,128)S(1)} collective-permute-done((f32[32,256]{1,0:T(8,128)S(1)}, f32[32,256]{1,0:T(8,128)S(1)}, u32[]{:S(2)}, u32[]{:S(2)}) %collective-permute-start.9) | collective-permute-done | bytes 32800 | tf_op jit(solution)/shard_map/ppermute | solution.py:407
  100.1 1.2 copy-done.2
  101.2 1.1 cross.1
  102.4 2.7 %collective-permute-start.11 = (f32[128,256]{1,0:T(8,128)S(1)}, f32[128,256]{1,0:T(8,128)S(1)}, u32[]{:S(2)}, u32[]{:S(2)}) collective-permute-start(f32[128,256]{1,0:T(8,128)S(1)} %constant_dynamic-slice_fusion.3), channel_id=1, source_target_pairs={{0,2},{2,0},{4,6},{6,4},{8,10},{10,8},{12,14},{14,12},{16,18},{18,... | collective-permute-start | bytes 393224 | tf_op jit(solution)/shard_map/ppermute | solution.py:407
  105.1 1.0 collective-permute-done.11
  106.1 8.6 %collective-permute-start.12 = (f32[32,256]{1,0:T(8,128)S(1)}, f32[32,256]{1,0:T(8,128)S(1)}, u32[]{:S(2)}, u32[]{:S(2)}) collective-permute-start(f32[32,256]{1,0:T(8,128)S(1)} %get-tuple-element.64), channel_id=1, source_target_pairs={{0,4},{2,6},{4,0},{6,2},{8,12},{10,14},{12,8},{14,10},{16,20},{18,... | collective-permute-start | bytes 98312 | tf_op jit(solution)/shard_map/ppermute | solution.py:407
  114.8 1.6 %collective-permute-start.13 = (f32[32,256]{1,0:T(8,128)S(1)}, f32[32,256]{1,0:T(8,128)S(1)}, u32[]{:S(2)}, u32[]{:S(2)}) collective-permute-start(f32[32,256]{1,0:T(8,128)S(1)} %get-tuple-element.66), channel_id=1, source_target_pairs={{0,8},{2,10},{4,12},{6,14},{8,0},{10,2},{12,4},{14,6},{16,24},{18,... | collective-permute-start | bytes 98312 | tf_op jit(solution)/shard_map/ppermute | solution.py:407
  116.4 0.4 collective-permute-start.14
  116.8 1.9 %collective-permute-done.13 = f32[32,256]{1,0:T(8,128)S(1)} collective-permute-done((f32[32,256]{1,0:T(8,128)S(1)}, f32[32,256]{1,0:T(8,128)S(1)}, u32[]{:S(2)}, u32[]{:S(2)}) %collective-permute-start.13) | collective-permute-done | bytes 32800 | tf_op jit(solution)/shard_map/ppermute | solution.py:407
  118.7 2.5 %collective-permute-done.14 = f32[32,256]{1,0:T(8,128)S(1)} collective-permute-done((f32[32,256]{1,0:T(8,128)S(1)}, f32[32,256]{1,0:T(8,128)S(1)}, u32[]{:S(2)}, u32[]{:S(2)}) %collective-permute-start.14) | collective-permute-done | bytes 32800 | tf_op jit(solution)/shard_map/ppermute | solution.py:407
  121.2 1.7 %collective-permute-start.15 = (f32[2,32,256]{2,1,0:T(8,128)S(1)}, f32[2,32,256]{2,1,0:T(8,128)S(1)}, u32[]{:S(2)}, u32[]{:S(2)}) collective-permute-start(f32[2,32,256]{2,1,0:T(8,128)S(1)} %pad_maximum_fusion.1), channel_id=1, source_target_pairs={{0,16},{1,17},{2,18},{3,19},{4,20},{5,21},{6,22},{7,23},{8,24},{9,... | collective-permute-start | bytes 196616 | tf_op jit(solution)/shard_map/ppermute | solution.py:427
  123.6 1.7 %collective-permute-start.16 = (f32[2,32,256]{2,1,0:T(8,128)S(1)}, f32[2,32,256]{2,1,0:T(8,128)S(1)}, u32[]{:S(2)}, u32[]{:S(2)}) collective-permute-start(f32[2,32,256]{2,1,0:T(8,128)S(1)} %pad_maximum_fusion.1), channel_id=1, source_target_pairs={{0,1},{1,0},{2,3},{3,2},{4,5},{5,4},{6,7},{7,6},{8,9},{9,8},{10,11... | collective-permute-start | bytes 196616 | tf_op jit(solution)/shard_map/ppermute | solution.py:427
  125.2 1.1 collective-permute-start.17
  126.4 0.7 collective-permute-done.15
  127.0 0.9 collective-permute-done.16
  127.9 3.4 %collective-permute-done.17 = f32[2,32,256]{2,1,0:T(8,128)S(1)} collective-permute-done((f32[2,32,256]{2,1,0:T(8,128)S(1)}, f32[2,32,256]{2,1,0:T(8,128)S(1)}, u32[]{:S(2)}, u32[]{:S(2)}) %collective-permute-start.17) | collective-permute-done | bytes 65568 | tf_op jit(solution)/shard_map/ppermute | solution.py:427
  131.4 2.6 %collective-permute-start.18 = (f32[3,32,256]{2,1,0:T(8,128)S(1)}, f32[3,32,256]{2,1,0:T(8,128)S(1)}, u32[]{:S(2)}, u32[]{:S(2)}) collective-permute-start(f32[3,32,256]{2,1,0:T(8,128)S(1)} %get-tuple-element.70), channel_id=1, source_target_pairs={{0,4},{2,6},{4,0},{6,2},{8,12},{10,14},{12,8},{14,10},{16,20},{18,... | collective-permute-start | bytes 294920 | tf_op jit(solution)/shard_map/ppermute | solution.py:441
  134.0 0.4 collective-permute-start.22
  134.4 1.5 collective-permute-start.20
  136.0 0.7 collective-permute-done.18
  136.6 2.4 %collective-permute-done.19 = f32[3,32,256]{2,1,0:T(8,128)S(1)} collective-permute-done((f32[3,32,256]{2,1,0:T(8,128)S(1)}, f32[3,32,256]{2,1,0:T(8,128)S(1)}, u32[]{:S(2)}, u32[]{:S(2)}) %collective-permute-start.19) | collective-permute-done | bytes 98336 | tf_op jit(solution)/shard_map/ppermute | solution.py:441
  139.1 0.9 collective-permute-done.20
  140.0 0.1 collective-permute-start.21
  140.0 0.1 broadcast_in_dim.6
  140.1 1.6 %collective-permute-done.21 = f32[3,128,256]{2,1,0:T(8,128)S(1)} collective-permute-done((f32[3,128,256]{2,1,0:T(8,128)S(1)}, f32[3,128,256]{2,1,0:T(8,128)S(1)}, u32[]{:S(2)}, u32[]{:S(2)}) %collective-permute-start.21) | collective-permute-done | bytes 393248 | tf_op jit(solution)/shard_map/ppermute | solution.py:441
  141.8 6.5 %root.1.columns = bf16[512,256]{1,0:T(8,128)(2,1)S(1)} custom-call(s32[2]{0:T(128)S(1)} %pad_add_fusion.refs_3_.at, f32[3,256,256]{2,1,0:T(8,128)S(1)} %constant_dynamic-update-slice_fusion.blocks), custom_call_target="tpu_custom_call" | custom-call | tf_op jit(solution)/shard_map/root/pallas_call | solution.py:478
  148.2 4.6 %collective-permute-done.22.rest = bf16[1792,256]{1,0:T(8,128)(2,1)S(1)} collective-permute-done((bf16[1792,256]{1,0:T(8,128)(2,1)S(1)}, bf16[1792,256]{1,0:T(8,128)(2,1)S(1)}, u32[]{:S(2)}, u32[]{:S(2)}) %collective-permute-start.22) | collective-permute-done | bytes 917536 | tf_op jit(solution)/shard_map/ppermute | solution.py:476
  152.8 2.9 %rotate.1 = bf16[256,3584]{1,0:T(8,128)(2,1)} custom-call(s32[2]{0:T(128)S(1)} %pad_add_fusion.refs_3_.at, bf16[512,256]{1,0:T(8,128)(2,1)S(1)} %root.1.columns, bf16[256,3584]{1,0:T(8,128)(2,1)S(1)} %get-tuple-element.59.turned, bf16[1792,256]{1,0:T(8,128)(2,1)S(1)} %collective-permute-done.10.came.first, bf16[1792,256]{1,0:T(8,128)(2,1)S(1)} %collective-permute-done.22.rest), custom_call_target="tpu_custom_call" | custom-call | tf_op jit(solution)/shard_map/rotate/pallas_call | solution.py:316
  (34 shorter events, 0.3 us)
Async XLA Ops:
  2.3 1.5 copy-start
  3.8 1.0 copy-start.3
  4.9 0.7 copy-start.4
  20.1 2.9 %collective-permute-start = (bf16[870,128]{1,0:T(8,128)(2,1)S(1)}, bf16[870,128]{1,0:T(8,128)(2,1)S(1)}, u32[]{:S(2)}, u32[]{:S(2)}) collective-permute-start(bf16[870,128]{1,0:T(8,128)(2,1)S(1)} %get-tuple-element.39), channel_id=1, source_target_pairs={{0,2},{4,6},{8,10},{12,14},{16,18},{20,22},{24,26},{28,30},{2,0},{... | collective-permute-start | bytes 668168 | tf_op jit(solution)/shard_map/ppermute | solution.py:24
  20.7 2.4 %collective-permute-start.1 = (bf16[870,128]{1,0:T(8,128)(2,1)S(1)}, bf16[870,128]{1,0:T(8,128)(2,1)S(1)}, u32[]{:S(2)}, u32[]{:S(2)}) collective-permute-start(bf16[870,128]{1,0:T(8,128)(2,1)S(1)} %get-tuple-element.40), channel_id=1, source_target_pairs={{2,4},{6,8},{10,12},{14,16},{18,20},{22,24},{26,28},{4,2},{8,6},{1... | collective-permute-start | bytes 668168 | tf_op jit(solution)/shard_map/ppermute | solution.py:24
  37.9 10.5 %collective-permute-start.2 = (bf16[870,128]{1,0:T(8,128)(2,1)S(1)}, bf16[870,128]{1,0:T(8,128)(2,1)S(1)}, u32[]{:S(2)}, u32[]{:S(2)}) collective-permute-start(bf16[870,128]{1,0:T(8,128)(2,1)S(1)} %get-tuple-element.45), channel_id=1, source_target_pairs={{0,2},{4,6},{8,10},{12,14},{16,18},{20,22},{24,26},{28,30},{2,0},{... | collective-permute-start | bytes 668168 | tf_op jit(solution)/shard_map/ppermute | solution.py:24
  45.4 3.0 %collective-permute-start.3 = (bf16[870,128]{1,0:T(8,128)(2,1)S(1)}, bf16[870,128]{1,0:T(8,128)(2,1)S(1)}, u32[]{:S(2)}, u32[]{:S(2)}) collective-permute-start(bf16[870,128]{1,0:T(8,128)(2,1)S(1)} %get-tuple-element.46), channel_id=1, source_target_pairs={{2,4},{6,8},{10,12},{14,16},{18,20},{22,24},{26,28},{4,2},{8,6},{1... | collective-permute-start | bytes 668168 | tf_op jit(solution)/shard_map/ppermute | solution.py:24
  63.3 9.3 %collective-permute-start.4 = (bf16[870,128]{1,0:T(8,128)(2,1)S(1)}, bf16[870,128]{1,0:T(8,128)(2,1)S(1)}, u32[]{:S(2)}, u32[]{:S(2)}) collective-permute-start(bf16[870,128]{1,0:T(8,128)(2,1)S(1)} %get-tuple-element.49), channel_id=1, source_target_pairs={{0,2},{4,6},{8,10},{12,14},{16,18},{20,22},{24,26},{28,30},{2,0},{... | collective-permute-start | bytes 668168 | tf_op jit(solution)/shard_map/ppermute | solution.py:24
  70.0 2.6 %collective-permute-start.5 = (bf16[870,128]{1,0:T(8,128)(2,1)S(1)}, bf16[870,128]{1,0:T(8,128)(2,1)S(1)}, u32[]{:S(2)}, u32[]{:S(2)}) collective-permute-start(bf16[870,128]{1,0:T(8,128)(2,1)S(1)} %get-tuple-element.50), channel_id=1, source_target_pairs={{2,4},{6,8},{10,12},{14,16},{18,20},{22,24},{26,28},{4,2},{8,6},{1... | collective-permute-start | bytes 668168 | tf_op jit(solution)/shard_map/ppermute | solution.py:24
  77.6 0.9 copy-start.1
  78.5 0.9 copy-start.5
  79.4 20.6 %collective-permute-start.10 = (bf16[1792,256]{1,0:T(8,128)(2,1)}, bf16[1792,256]{1,0:T(8,128)(2,1)S(1)}, u32[]{:S(2)}, u32[]{:S(2)}) collective-permute-start(bf16[1792,256]{1,0:T(8,128)(2,1)} %get-tuple-element.58), channel_id=1, source_target_pairs={{0,1},{1,0},{2,3},{3,2},{4,5},{5,4},{6,7},{7,6},{8,9},{9,8},{10,11... | collective-permute-start | bytes 2752520 | tf_op jit(solution)/shard_map/ppermute | solution.py:454
  82.2 8.6 %collective-permute-start.6 = (f32[128,256]{1,0:T(8,128)S(1)}, f32[128,256]{1,0:T(8,128)S(1)}, u32[]{:S(2)}, u32[]{:S(2)}) collective-permute-start(f32[128,256]{1,0:T(8,128)S(1)} %constant_dynamic-slice_fusion.7), channel_id=1, source_target_pairs={{0,2},{2,0},{4,6},{6,4},{8,10},{10,8},{12,14},{14,12},{16,18},{18,... | collective-permute-start | bytes 393224 | tf_op jit(solution)/shard_map/ppermute | solution.py:407
  90.9 4.8 %collective-permute-start.7 = (f32[32,256]{1,0:T(8,128)S(1)}, f32[32,256]{1,0:T(8,128)S(1)}, u32[]{:S(2)}, u32[]{:S(2)}) collective-permute-start(f32[32,256]{1,0:T(8,128)S(1)} %get-tuple-element.67), channel_id=1, source_target_pairs={{0,4},{2,6},{4,0},{6,2},{8,12},{10,14},{12,8},{14,10},{16,20},{18,... | collective-permute-start | bytes 98312 | tf_op jit(solution)/shard_map/ppermute | solution.py:407
  93.6 3.9 %collective-permute-start.8 = (f32[32,256]{1,0:T(8,128)S(1)}, f32[32,256]{1,0:T(8,128)S(1)}, u32[]{:S(2)}, u32[]{:S(2)}) collective-permute-start(f32[32,256]{1,0:T(8,128)S(1)} %get-tuple-element.69), channel_id=1, source_target_pairs={{0,8},{2,10},{4,12},{6,14},{8,0},{10,2},{12,4},{14,6},{16,24},{18,... | collective-permute-start | bytes 98312 | tf_op jit(solution)/shard_map/ppermute | solution.py:407
  95.2 4.8 %collective-permute-start.9 = (f32[32,256]{1,0:T(8,128)S(1)}, f32[32,256]{1,0:T(8,128)S(1)}, u32[]{:S(2)}, u32[]{:S(2)}) collective-permute-start(f32[32,256]{1,0:T(8,128)S(1)} %get-tuple-element.68), channel_id=1, source_target_pairs={{0,12},{2,14},{4,8},{6,10},{8,4},{10,6},{12,0},{14,2},{16,28},{18,... | collective-permute-start | bytes 98312 | tf_op jit(solution)/shard_map/ppermute | solution.py:407
  100.1 1.2 copy-start.2
  101.2 32.8 %copy-start.6 = (bf16[1792,256]{1,0:T(8,128)(2,1)S(1)}, bf16[1792,256]{1,0:T(8,128)(2,1)}, u32[]{:S(2)}) copy-start(bf16[1792,256]{1,0:T(8,128)(2,1)} %copy-done.5) | copy-start | bytes 2752516
  102.4 3.7 %collective-permute-start.11 = (f32[128,256]{1,0:T(8,128)S(1)}, f32[128,256]{1,0:T(8,128)S(1)}, u32[]{:S(2)}, u32[]{:S(2)}) collective-permute-start(f32[128,256]{1,0:T(8,128)S(1)} %constant_dynamic-slice_fusion.3), channel_id=1, source_target_pairs={{0,2},{2,0},{4,6},{6,4},{8,10},{10,8},{12,14},{14,12},{16,18},{18,... | collective-permute-start | bytes 393224 | tf_op jit(solution)/shard_map/ppermute | solution.py:407
  106.1 10.7 %collective-permute-start.12 = (f32[32,256]{1,0:T(8,128)S(1)}, f32[32,256]{1,0:T(8,128)S(1)}, u32[]{:S(2)}, u32[]{:S(2)}) collective-permute-start(f32[32,256]{1,0:T(8,128)S(1)} %get-tuple-element.64), channel_id=1, source_target_pairs={{0,4},{2,6},{4,0},{6,2},{8,12},{10,14},{12,8},{14,10},{16,20},{18,... | collective-permute-start | bytes 98312 | tf_op jit(solution)/shard_map/ppermute | solution.py:407
  114.8 3.9 %collective-permute-start.13 = (f32[32,256]{1,0:T(8,128)S(1)}, f32[32,256]{1,0:T(8,128)S(1)}, u32[]{:S(2)}, u32[]{:S(2)}) collective-permute-start(f32[32,256]{1,0:T(8,128)S(1)} %get-tuple-element.66), channel_id=1, source_target_pairs={{0,8},{2,10},{4,12},{6,14},{8,0},{10,2},{12,4},{14,6},{16,24},{18,... | collective-permute-start | bytes 98312 | tf_op jit(solution)/shard_map/ppermute | solution.py:407
  116.4 4.8 %collective-permute-start.14 = (f32[32,256]{1,0:T(8,128)S(1)}, f32[32,256]{1,0:T(8,128)S(1)}, u32[]{:S(2)}, u32[]{:S(2)}) collective-permute-start(f32[32,256]{1,0:T(8,128)S(1)} %get-tuple-element.65), channel_id=1, source_target_pairs={{0,12},{2,14},{4,8},{6,10},{8,4},{10,6},{12,0},{14,2},{16,28},{18,... | collective-permute-start | bytes 98312 | tf_op jit(solution)/shard_map/ppermute | solution.py:407
  121.2 5.8 %collective-permute-start.15 = (f32[2,32,256]{2,1,0:T(8,128)S(1)}, f32[2,32,256]{2,1,0:T(8,128)S(1)}, u32[]{:S(2)}, u32[]{:S(2)}) collective-permute-start(f32[2,32,256]{2,1,0:T(8,128)S(1)} %pad_maximum_fusion.1), channel_id=1, source_target_pairs={{0,16},{1,17},{2,18},{3,19},{4,20},{5,21},{6,22},{7,23},{8,24},{9,... | collective-permute-start | bytes 196616 | tf_op jit(solution)/shard_map/ppermute | solution.py:427
  123.6 4.3 %collective-permute-start.16 = (f32[2,32,256]{2,1,0:T(8,128)S(1)}, f32[2,32,256]{2,1,0:T(8,128)S(1)}, u32[]{:S(2)}, u32[]{:S(2)}) collective-permute-start(f32[2,32,256]{2,1,0:T(8,128)S(1)} %pad_maximum_fusion.1), channel_id=1, source_target_pairs={{0,1},{1,0},{2,3},{3,2},{4,5},{5,4},{6,7},{7,6},{8,9},{9,8},{10,11... | collective-permute-start | bytes 196616 | tf_op jit(solution)/shard_map/ppermute | solution.py:427
  125.2 6.1 %collective-permute-start.17 = (f32[2,32,256]{2,1,0:T(8,128)S(1)}, f32[2,32,256]{2,1,0:T(8,128)S(1)}, u32[]{:S(2)}, u32[]{:S(2)}) collective-permute-start(f32[2,32,256]{2,1,0:T(8,128)S(1)} %pad_maximum_fusion.1), channel_id=1, source_target_pairs={{0,17},{1,16},{2,19},{3,18},{4,21},{5,20},{6,23},{7,22},{8,25},{9,... | collective-permute-start | bytes 196616 | tf_op jit(solution)/shard_map/ppermute | solution.py:427
  131.4 5.2 %collective-permute-start.18 = (f32[3,32,256]{2,1,0:T(8,128)S(1)}, f32[3,32,256]{2,1,0:T(8,128)S(1)}, u32[]{:S(2)}, u32[]{:S(2)}) collective-permute-start(f32[3,32,256]{2,1,0:T(8,128)S(1)} %get-tuple-element.70), channel_id=1, source_target_pairs={{0,4},{2,6},{4,0},{6,2},{8,12},{10,14},{12,8},{14,10},{16,20},{18,... | collective-permute-start | bytes 294920 | tf_op jit(solution)/shard_map/ppermute | solution.py:441
  134.0 18.8 %collective-permute-start.22 = (bf16[1792,256]{1,0:T(8,128)(2,1)S(1)}, bf16[1792,256]{1,0:T(8,128)(2,1)S(1)}, u32[]{:S(2)}, u32[]{:S(2)}) collective-permute-start(bf16[1792,256]{1,0:T(8,128)(2,1)S(1)} %copy-done.6), channel_id=1, source_target_pairs={{0,1},{1,0},{2,3},{3,2},{4,5},{5,4},{6,7},{7,6},{8,9},{9,8},{10,11... | collective-permute-start | bytes 2752520 | tf_op jit(solution)/shard_map/ppermute | solution.py:476
  134.4 4.6 %collective-permute-start.19 = (f32[3,32,256]{2,1,0:T(8,128)S(1)}, f32[3,32,256]{2,1,0:T(8,128)S(1)}, u32[]{:S(2)}, u32[]{:S(2)}) collective-permute-start(f32[3,32,256]{2,1,0:T(8,128)S(1)} %get-tuple-element.70), channel_id=1, source_target_pairs={{0,8},{2,10},{4,12},{6,14},{8,0},{10,2},{12,4},{14,6},{16,24},{18,... | collective-permute-start | bytes 294920 | tf_op jit(solution)/shard_map/ppermute | solution.py:441
  134.4 5.5 %collective-permute-start.20 = (f32[3,32,256]{2,1,0:T(8,128)S(1)}, f32[3,32,256]{2,1,0:T(8,128)S(1)}, u32[]{:S(2)}, u32[]{:S(2)}) collective-permute-start(f32[3,32,256]{2,1,0:T(8,128)S(1)} %get-tuple-element.70), channel_id=1, source_target_pairs={{0,12},{2,14},{4,8},{6,10},{8,4},{10,6},{12,0},{14,2},{16,28},{18,... | collective-permute-start | bytes 294920 | tf_op jit(solution)/shard_map/ppermute | solution.py:441
  140.0 1.8 %collective-permute-start.21 = (f32[3,128,256]{2,1,0:T(8,128)S(1)}, f32[3,128,256]{2,1,0:T(8,128)S(1)}, u32[]{:S(2)}, u32[]{:S(2)}) collective-permute-start(f32[3,128,256]{2,1,0:T(8,128)S(1)} %constant_dynamic-update-slice_fusion.2), channel_id=1, source_target_pairs={{0,2},{2,0},{4,6},{6,4},{8,10},{10,8},{12,14},{14,12},{16,18},{18,... | collective-permute-start | bytes 1179656 | tf_op jit(solution)/shard_map/ppermute | solution.py:441

commit v8 on v7

--- a/solution.py
+++ b/solution.py
@@ -389,6 +389,10 @@
     return [list(range(b, min(b + 2, bits))) if b else [0] for b in [0] + list(range(1, bits, 2))][:bits]
 
 
+def hop(x, pairs):
+    return lax.ppermute(x, "dom", pairs)
+
+
 def plan(group):
     for m in range(1, 1 << len(group)):
         yield m, sum(((m >> i) & 1) << bit for i, bit in enumerate(group))
@@ -404,9 +408,8 @@
         size = x.shape[-2] >> len(group)
         code = code_of(group, here)
         came = [
-            lax.ppermute(
-                lax.dynamic_slice_in_dim(x, (code ^ m) * size, size, x.ndim - 2),
-                "dom", [(i, i ^ mask) for i in range(devices)])
+            hop(lax.dynamic_slice_in_dim(x, (code ^ m) * size, size, x.ndim - 2),
+                [(i, i ^ mask) for i in range(devices)])
             for m, mask in plan(group)
         ]
         x = lax.dynamic_slice_in_dim(x, code * size, size, x.ndim - 2)
@@ -437,9 +440,7 @@
     for group in reversed(groups_of(devices)[:-1]):
         size = x.shape[-2]
         code = code_of(group, here)
-        pieces = [(0, x)] + [
-            (m, lax.ppermute(x, "dom", [(i, i ^ mask) for i in range(devices)])) for m, mask in plan(group)
-        ]
+        pieces = [(0, x)] + [(m, hop(x, [(i, i ^ mask) for i in range(devices)])) for m, mask in plan(group)]
         x = jnp.zeros(x.shape[:-2] + (size << len(group), x.shape[-1]), x.dtype)
         for m, piece in pieces:
             x = lax.dynamic_update_slice_in_dim(x, piece, (code ^ m) * size, x.ndim - 2)

time: 156 us -> 156 us (level)
  no operation moved by 1% of the time
where the time goes in v8:
time: 156 us
  Pallas kernels  65.6 us (42%)
  starting transfers between devices  52.6 us (34%)
  waiting for transfers between devices  25.1 us (16%)
  local copies, waits for them, and re-layouts  7.21 us (5%)
  between operations  2.92 us (2%)
  other arithmetic  2.35 us (2%)
    pallas_call x3, Pallas kernels, apply_call(): pl.pallas_call(functools.partial(apply_kernel, step), out_shape=out_shape...  44.2 us
    ppermute x12, starting transfers between devices, hop(): return lax.ppermute(x, 'dom', pairs)  29.3 us
    ppermute x6, starting transfers between devices, paired(): return lax.ppermute(x, axis, pairs)  16.8 us
    ppermute x12, waiting for transfers between devices, hop(): return lax.ppermute(x, 'dom', pairs)  15.6 us
    pallas_call x1, Pallas kernels, rotate_pair(): pl.pallas_call(root_kernel, out_shape=struct((2 * states, states), bf16),...  6.46 us
    unnamed x14, local copies, waits for them, and re-layouts  6.28 us
    pallas_call x3, Pallas kernels, settle_call(): pl.pallas_call(functools.partial(settle_kernel, step, last), out_shape=[w...  5.87 us
    ppermute x3, waiting for transfers between devices, sum_last(): lax.ppermute(both, ('dom', 'st'), [(i, i ^ 2 * mask + flip) for i in rang...  4.92 us
  transfers between devices with their start and end apart: 23, of which 14 were waited for; matrix products, arithmetic and copies ran while one was open for 1% of the time, Pallas kernels for 8%

profile of v8, /device:TPU:0, one launch (start us, length us, event | category | flops | bytes accessed | tf_op | source)
XLA Modules:
  0.0 155.8 jit_solution(8011165743711980108)
XLA Ops:
  0.0 0.7 broadcast_multiply_fusion.1
  0.7 0.1 mul.51.refs_1_.ids
  0.8 0.7 broadcast_multiply_fusion
  1.5 0.1 pad_add_fusion.refs_3_.at
  1.6 0.7 pad_maximum_fusion.2.refs_2_.refs_0_.bounds
  2.3 1.5 copy-done
  3.8 1.0 copy-done.3
  4.9 0.7 copy-done.4
  5.6 14.5 %apply.3 = (f32[7168,128]{1,0:T(8,128)S(1)}, f32[7168,128]{1,0:T(8,128)S(1)}, bf16[870,128]{1,0:T(8,128)(2,1)S(1)}, bf16[870,128]{1,0:T(8,128)(2,1)S(1)}, f32[71...) custom-call(s32[32,128]{1,0:T(8,128)S(1)} %mul.54.refs_0_, s32[870]{0:T(1024)S(1)} %mul.51.refs_1_.ids, ...), custom_call_target="tpu_custom_call" | custom-call | tf_op jit(solution)/shard_map/apply/pallas_call | solution.py:357
  20.1 0.6 collective-permute-start
  20.7 0.7 collective-permute-start.1
  21.3 1.7 %settle.3 = (f32[7168,128]{1,0:T(8,128)S(1)}, f32[7168,128]{1,0:T(8,128)S(1)}) custom-call(f32[10]{0:T(128)S(1)} %pad_maximum_fusion.2.refs_2_.refs_0_.bounds, f32[7168,128]{1,0:T(8,128)S(1)} %get-tuple-element.33.refs_1_.refs_4_, f32[7168,128]{1,0:T(8,128)S(1)} %get-tuple-element.35.refs_2_.refs_4_, ...), custom_call_target="tpu_custom_call", output_to_operand_aliasing={{1}: (3, {})} | custom-call | flops 8000000000 | bytes 10000000 | tf_op jit(solution)/shard_map/settle/pallas_call | solution.py:375
  23.0 0.0 collective-permute-done.refs_8_
  23.0 14.9 %apply.4 = (f32[7168,128]{1,0:T(8,128)S(1)}, f32[7168,128]{1,0:T(8,128)S(1)}, bf16[870,128]{1,0:T(8,128)(2,1)S(1)}, bf16[870,128]{1,0:T(8,128)(2,1)S(1)}) custom-call(s32[32,128]{1,0:T(8,128)S(1)} %mul.54.refs_0_, s32[870]{0:T(1024)S(1)} %mul.51.refs_1_.ids, ...), custom_call_target="tpu_custom_call", output_to_operand_aliasing={{0}: (6, {}), {1}: (7, {})} | custom-call | tf_op jit(solution)/shard_map/apply/pallas_call | solution.py:357
  37.9 7.5 %collective-permute-start.2 = (bf16[870,128]{1,0:T(8,128)(2,1)S(1)}, bf16[870,128]{1,0:T(8,128)(2,1)S(1)}, u32[]{:S(2)}, u32[]{:S(2)}) collective-permute-start(bf16[870,128]{1,0:T(8,128)(2,1)S(1)} %get-tuple-element.45), channel_id=1, source_target_pairs={{0,2},{4,6},{8,10},{12,14},{16,18},{20,22},{24,26},{28,30},{2,0},{... | collective-permute-start | bytes 668168 | tf_op jit(solution)/shard_map/ppermute | solution.py:24
  45.4 0.7 collective-permute-start.3
  46.1 2.3 %settle.4 = (f32[7168,128]{1,0:T(8,128)S(1)}, f32[7168,128]{1,0:T(8,128)S(1)}) custom-call(f32[10]{0:T(128)S(1)} %pad_maximum_fusion.2.refs_2_.refs_0_.bounds, f32[7168,128]{1,0:T(8,128)S(1)} %get-tuple-element.33.refs_1_.refs_4_, f32[7168,128]{1,0:T(8,128)S(1)} %get-tuple-element.41.refs_2_.refs_4_, ...), custom_call_target="tpu_custom_call", output_to_operand_aliasing={{0}: (4, {}), {1}: (3, {})} | custom-call | flops 8000000000 | bytes 10000000 | tf_op jit(solution)/shard_map/settle/pallas_call | solution.py:375
  48.4 0.0 collective-permute-done.3.refs_9_
  48.4 14.9 %apply.5 = (f32[7168,128]{1,0:T(8,128)S(1)}, f32[7168,128]{1,0:T(8,128)S(1)}, bf16[870,128]{1,0:T(8,128)(2,1)S(1)}, bf16[870,128]{1,0:T(8,128)(2,1)S(1)}) custom-call(s32[32,128]{1,0:T(8,128)S(1)} %mul.54.refs_0_, s32[870]{0:T(1024)S(1)} %mul.51.refs_1_.ids, ...), custom_call_target="tpu_custom_call", output_to_operand_aliasing={{0}: (6, {}), {1}: (7, {})} | custom-call | tf_op jit(solution)/shard_map/apply/pallas_call | solution.py:357
  63.3 6.7 %collective-permute-start.4 = (bf16[870,128]{1,0:T(8,128)(2,1)S(1)}, bf16[870,128]{1,0:T(8,128)(2,1)S(1)}, u32[]{:S(2)}, u32[]{:S(2)}) collective-permute-start(bf16[870,128]{1,0:T(8,128)(2,1)S(1)} %get-tuple-element.49), channel_id=1, source_target_pairs={{0,2},{4,6},{8,10},{12,14},{16,18},{20,22},{24,26},{28,30},{2,0},{... | collective-permute-start | bytes 668168 | tf_op jit(solution)/shard_map/ppermute | solution.py:24
  70.0 0.7 collective-permute-start.5
  70.7 1.9 %settle.5.before = f32[7168,128]{1,0:T(8,128)S(1)} custom-call(f32[10]{0:T(128)S(1)} %pad_maximum_fusion.2.refs_2_.refs_0_.bounds, f32[7168,128]{1,0:T(8,128)S(1)} %get-tuple-element.33.refs_1_.refs_4_, f32[7168,128]{1,0:T(8,128)S(1)} %get-tuple-element.47.refs_2_, f32[7168,128]{1,0:T(8,128)S(1)} %get-tuple-element.48.refs_3_, ...), custom_call_target="tpu_custom_call", output_to_operand_aliasing={{}: (4, {})} | custom-call | flops 8000000000 | bytes 10000000 | tf_op jit(solution)/shard_map/settle/pallas_call | solution.py:375
  72.6 0.0 collective-permute-done.4.came_low
  72.6 0.0 collective-permute-done.5.came_high
  72.6 3.2 %send.1 = (f32[7168,128]{1,0:T(8,128)S(1)}, bf16[1792,256]{1,0:T(8,128)(2,1)}) custom-call(s32[870]{0:T(1024)S(1)} %mul.51.refs_1_.ids, f32[10]{0:T(128)S(1)} %pad_maximum_fusion.2.refs_2_.refs_0_.bounds, s32[2]{0:T(128)S(1)} %pad_add_fusion.refs_3_.at, f32[7168,128]{1,0:T(8,128)S(1)} %settle.5.before, ...), custom_call_target="tpu_custom_call", output_to_operand_aliasing={{0}: (3, {})} | custom-call | tf_op jit(solution)/shard_map/send/pallas_call | solution.py:528
  75.8 1.8 %turn.1 = (f32[7168,128]{1,0:T(8,128)S(1)}, bf16[256,3584]{1,0:T(8,128)(2,1)S(1)}, bf16[1792,256]{1,0:T(8,128)(2,1)S(1)}, bf16[256,1792]{1,0:T(8,128)(2,1)S(1)}, f32[256,256]{1,0:T(8,128)S(1)}) custom-call(s32[870]{0:T(1024)S(1)} %mul.51.refs_1_.ids, s32[2]{0:T(128)S(1)} %pad_add_fusion.refs_3_.at, ...), custom_call_target="tpu_custom_call", output_to_operand_aliasing={{0}: (2, {})} | custom-call | flops 4000000000 | bytes 10000000 | tf_op jit(solution)/shard_map/turn/pallas_call | solution.py:456
  77.6 0.9 copy-done.1
  78.5 0.9 copy-done.5
  79.4 1.5 collective-permute-start.10
  80.9 0.6 fusion.1
  82.2 7.3 %collective-permute-start.6 = (f32[128,256]{1,0:T(8,128)S(1)}, f32[128,256]{1,0:T(8,128)S(1)}, u32[]{:S(2)}, u32[]{:S(2)}) collective-permute-start(f32[128,256]{1,0:T(8,128)S(1)} %constant_dynamic-slice_fusion.7), channel_id=1, source_target_pairs={{0,2},{2,0},{4,6},{6,4},{8,10},{10,8},{12,14},{14,12},{16,18},{18,... | collective-permute-start | bytes 393224 | tf_op jit(solution)/shard_map/ppermute | solution.py:393
  90.9 2.7 %collective-permute-start.7 = (f32[32,256]{1,0:T(8,128)S(1)}, f32[32,256]{1,0:T(8,128)S(1)}, u32[]{:S(2)}, u32[]{:S(2)}) collective-permute-start(f32[32,256]{1,0:T(8,128)S(1)} %get-tuple-element.67), channel_id=1, source_target_pairs={{0,4},{2,6},{4,0},{6,2},{8,12},{10,14},{12,8},{14,10},{16,20},{18,... | collective-permute-start | bytes 98312 | tf_op jit(solution)/shard_map/ppermute | solution.py:393
  93.6 1.6 %collective-permute-start.8 = (f32[32,256]{1,0:T(8,128)S(1)}, f32[32,256]{1,0:T(8,128)S(1)}, u32[]{:S(2)}, u32[]{:S(2)}) collective-permute-start(f32[32,256]{1,0:T(8,128)S(1)} %get-tuple-element.69), channel_id=1, source_target_pairs={{0,8},{2,10},{4,12},{6,14},{8,0},{10,2},{12,4},{14,6},{16,24},{18,... | collective-permute-start | bytes 98312 | tf_op jit(solution)/shard_map/ppermute | solution.py:393
  95.2 0.1 collective-permute-start.9
  95.3 0.3 collective-permute-done.7
  95.7 1.9 %collective-permute-done.8 = f32[32,256]{1,0:T(8,128)S(1)} collective-permute-done((f32[32,256]{1,0:T(8,128)S(1)}, f32[32,256]{1,0:T(8,128)S(1)}, u32[]{:S(2)}, u32[]{:S(2)}) %collective-permute-start.8) | collective-permute-done | bytes 32800 | tf_op jit(solution)/shard_map/ppermute | solution.py:393
  97.6 2.4 %collective-permute-done.9 = f32[32,256]{1,0:T(8,128)S(1)} collective-permute-done((f32[32,256]{1,0:T(8,128)S(1)}, f32[32,256]{1,0:T(8,128)S(1)}, u32[]{:S(2)}, u32[]{:S(2)}) %collective-permute-start.9) | collective-permute-done | bytes 32800 | tf_op jit(solution)/shard_map/ppermute | solution.py:393
  100.1 1.2 copy-done.2
  101.2 1.1 cross.1
  102.4 2.7 %collective-permute-start.11 = (f32[128,256]{1,0:T(8,128)S(1)}, f32[128,256]{1,0:T(8,128)S(1)}, u32[]{:S(2)}, u32[]{:S(2)}) collective-permute-start(f32[128,256]{1,0:T(8,128)S(1)} %constant_dynamic-slice_fusion.3), channel_id=1, source_target_pairs={{0,2},{2,0},{4,6},{6,4},{8,10},{10,8},{12,14},{14,12},{16,18},{18,... | collective-permute-start | bytes 393224 | tf_op jit(solution)/shard_map/ppermute | solution.py:393
  105.1 1.0 collective-permute-done.11
  106.1 8.6 %collective-permute-start.12 = (f32[32,256]{1,0:T(8,128)S(1)}, f32[32,256]{1,0:T(8,128)S(1)}, u32[]{:S(2)}, u32[]{:S(2)}) collective-permute-start(f32[32,256]{1,0:T(8,128)S(1)} %get-tuple-element.64), channel_id=1, source_target_pairs={{0,4},{2,6},{4,0},{6,2},{8,12},{10,14},{12,8},{14,10},{16,20},{18,... | collective-permute-start | bytes 98312 | tf_op jit(solution)/shard_map/ppermute | solution.py:393
  114.8 1.6 %collective-permute-start.13 = (f32[32,256]{1,0:T(8,128)S(1)}, f32[32,256]{1,0:T(8,128)S(1)}, u32[]{:S(2)}, u32[]{:S(2)}) collective-permute-start(f32[32,256]{1,0:T(8,128)S(1)} %get-tuple-element.66), channel_id=1, source_target_pairs={{0,8},{2,10},{4,12},{6,14},{8,0},{10,2},{12,4},{14,6},{16,24},{18,... | collective-permute-start | bytes 98312 | tf_op jit(solution)/shard_map/ppermute | solution.py:393
  116.4 0.4 collective-permute-start.14
  116.8 1.9 %collective-permute-done.13 = f32[32,256]{1,0:T(8,128)S(1)} collective-permute-done((f32[32,256]{1,0:T(8,128)S(1)}, f32[32,256]{1,0:T(8,128)S(1)}, u32[]{:S(2)}, u32[]{:S(2)}) %collective-permute-start.13) | collective-permute-done | bytes 32800 | tf_op jit(solution)/shard_map/ppermute | solution.py:393
  118.7 2.5 %collective-permute-done.14 = f32[32,256]{1,0:T(8,128)S(1)} collective-permute-done((f32[32,256]{1,0:T(8,128)S(1)}, f32[32,256]{1,0:T(8,128)S(1)}, u32[]{:S(2)}, u32[]{:S(2)}) %collective-permute-start.14) | collective-permute-done | bytes 32800 | tf_op jit(solution)/shard_map/ppermute | solution.py:393
  121.2 1.7 %collective-permute-start.15 = (f32[2,32,256]{2,1,0:T(8,128)S(1)}, f32[2,32,256]{2,1,0:T(8,128)S(1)}, u32[]{:S(2)}, u32[]{:S(2)}) collective-permute-start(f32[2,32,256]{2,1,0:T(8,128)S(1)} %pad_maximum_fusion.1), channel_id=1, source_target_pairs={{0,16},{1,17},{2,18},{3,19},{4,20},{5,21},{6,22},{7,23},{8,24},{9,... | collective-permute-start | bytes 196616 | tf_op jit(solution)/shard_map/ppermute | solution.py:430
  123.6 1.7 %collective-permute-start.16 = (f32[2,32,256]{2,1,0:T(8,128)S(1)}, f32[2,32,256]{2,1,0:T(8,128)S(1)}, u32[]{:S(2)}, u32[]{:S(2)}) collective-permute-start(f32[2,32,256]{2,1,0:T(8,128)S(1)} %pad_maximum_fusion.1), channel_id=1, source_target_pairs={{0,1},{1,0},{2,3},{3,2},{4,5},{5,4},{6,7},{7,6},{8,9},{9,8},{10,11... | collective-permute-start | bytes 196616 | tf_op jit(solution)/shard_map/ppermute | solution.py:430
  125.2 1.1 collective-permute-start.17
  126.4 0.7 collective-permute-done.15
  127.0 0.9 collective-permute-done.16
  127.9 3.4 %collective-permute-done.17 = f32[2,32,256]{2,1,0:T(8,128)S(1)} collective-permute-done((f32[2,32,256]{2,1,0:T(8,128)S(1)}, f32[2,32,256]{2,1,0:T(8,128)S(1)}, u32[]{:S(2)}, u32[]{:S(2)}) %collective-permute-start.17) | collective-permute-done | bytes 65568 | tf_op jit(solution)/shard_map/ppermute | solution.py:430
  131.4 2.6 %collective-permute-start.18 = (f32[3,32,256]{2,1,0:T(8,128)S(1)}, f32[3,32,256]{2,1,0:T(8,128)S(1)}, u32[]{:S(2)}, u32[]{:S(2)}) collective-permute-start(f32[3,32,256]{2,1,0:T(8,128)S(1)} %get-tuple-element.70), channel_id=1, source_target_pairs={{0,4},{2,6},{4,0},{6,2},{8,12},{10,14},{12,8},{14,10},{16,20},{18,... | collective-permute-start | bytes 294920 | tf_op jit(solution)/shard_map/ppermute | solution.py:393
  134.0 0.4 collective-permute-start.22
  134.4 1.5 collective-permute-start.20
  136.0 0.7 collective-permute-done.18
  136.6 2.4 %collective-permute-done.19 = f32[3,32,256]{2,1,0:T(8,128)S(1)} collective-permute-done((f32[3,32,256]{2,1,0:T(8,128)S(1)}, f32[3,32,256]{2,1,0:T(8,128)S(1)}, u32[]{:S(2)}, u32[]{:S(2)}) %collective-permute-start.19) | collective-permute-done | bytes 98336 | tf_op jit(solution)/shard_map/ppermute | solution.py:393
  139.1 0.9 collective-permute-done.20
  140.0 0.1 collective-permute-start.21
  140.0 0.1 broadcast_in_dim.6
  140.1 1.6 %collective-permute-done.21 = f32[3,128,256]{2,1,0:T(8,128)S(1)} collective-permute-done((f32[3,128,256]{2,1,0:T(8,128)S(1)}, f32[3,128,256]{2,1,0:T(8,128)S(1)}, u32[]{:S(2)}, u32[]{:S(2)}) %collective-permute-start.21) | collective-permute-done | bytes 393248 | tf_op jit(solution)/shard_map/ppermute | solution.py:393
  141.8 6.5 %root.1.columns = bf16[512,256]{1,0:T(8,128)(2,1)S(1)} custom-call(s32[2]{0:T(128)S(1)} %pad_add_fusion.refs_3_.at, f32[3,256,256]{2,1,0:T(8,128)S(1)} %constant_dynamic-update-slice_fusion.blocks), custom_call_target="tpu_custom_call" | custom-call | tf_op jit(solution)/shard_map/root/pallas_call | solution.py:479
  148.2 4.6 %collective-permute-done.22.rest = bf16[1792,256]{1,0:T(8,128)(2,1)S(1)} collective-permute-done((bf16[1792,256]{1,0:T(8,128)(2,1)S(1)}, bf16[1792,256]{1,0:T(8,128)(2,1)S(1)}, u32[]{:S(2)}, u32[]{:S(2)}) %collective-permute-start.22) | collective-permute-done | bytes 917536 | tf_op jit(solution)/shard_map/ppermute | solution.py:477
  152.8 2.9 %rotate.1 = bf16[256,3584]{1,0:T(8,128)(2,1)} custom-call(s32[2]{0:T(128)S(1)} %pad_add_fusion.refs_3_.at, bf16[512,256]{1,0:T(8,128)(2,1)S(1)} %root.1.columns, bf16[256,3584]{1,0:T(8,128)(2,1)S(1)} %get-tuple-element.59.turned, bf16[1792,256]{1,0:T(8,128)(2,1)S(1)} %collective-permute-done.10.came.first, bf16[1792,256]{1,0:T(8,128)(2,1)S(1)} %collective-permute-done.22.rest), custom_call_target="tpu_custom_call" | custom-call | tf_op jit(solution)/shard_map/rotate/pallas_call | solution.py:316
  (34 shorter events, 0.3 us)
Async XLA Ops:
  2.3 1.5 copy-start
  3.8 1.0 copy-start.3
  4.9 0.7 copy-start.4
  20.1 2.9 %collective-permute-start = (bf16[870,128]{1,0:T(8,128)(2,1)S(1)}, bf16[870,128]{1,0:T(8,128)(2,1)S(1)}, u32[]{:S(2)}, u32[]{:S(2)}) collective-permute-start(bf16[870,128]{1,0:T(8,128)(2,1)S(1)} %get-tuple-element.39), channel_id=1, source_target_pairs={{0,2},{4,6},{8,10},{12,14},{16,18},{20,22},{24,26},{28,30},{2,0},{... | collective-permute-start | bytes 668168 | tf_op jit(solution)/shard_map/ppermute | solution.py:24
  20.7 2.4 %collective-permute-start.1 = (bf16[870,128]{1,0:T(8,128)(2,1)S(1)}, bf16[870,128]{1,0:T(8,128)(2,1)S(1)}, u32[]{:S(2)}, u32[]{:S(2)}) collective-permute-start(bf16[870,128]{1,0:T(8,128)(2,1)S(1)} %get-tuple-element.40), channel_id=1, source_target_pairs={{2,4},{6,8},{10,12},{14,16},{18,20},{22,24},{26,28},{4,2},{8,6},{1... | collective-permute-start | bytes 668168 | tf_op jit(solution)/shard_map/ppermute | solution.py:24
  37.9 10.5 %collective-permute-start.2 = (bf16[870,128]{1,0:T(8,128)(2,1)S(1)}, bf16[870,128]{1,0:T(8,128)(2,1)S(1)}, u32[]{:S(2)}, u32[]{:S(2)}) collective-permute-start(bf16[870,128]{1,0:T(8,128)(2,1)S(1)} %get-tuple-element.45), channel_id=1, source_target_pairs={{0,2},{4,6},{8,10},{12,14},{16,18},{20,22},{24,26},{28,30},{2,0},{... | collective-permute-start | bytes 668168 | tf_op jit(solution)/shard_map/ppermute | solution.py:24
  45.4 3.0 %collective-permute-start.3 = (bf16[870,128]{1,0:T(8,128)(2,1)S(1)}, bf16[870,128]{1,0:T(8,128)(2,1)S(1)}, u32[]{:S(2)}, u32[]{:S(2)}) collective-permute-start(bf16[870,128]{1,0:T(8,128)(2,1)S(1)} %get-tuple-element.46), channel_id=1, source_target_pairs={{2,4},{6,8},{10,12},{14,16},{18,20},{22,24},{26,28},{4,2},{8,6},{1... | collective-permute-start | bytes 668168 | tf_op jit(solution)/shard_map/ppermute | solution.py:24
  63.3 9.3 %collective-permute-start.4 = (bf16[870,128]{1,0:T(8,128)(2,1)S(1)}, bf16[870,128]{1,0:T(8,128)(2,1)S(1)}, u32[]{:S(2)}, u32[]{:S(2)}) collective-permute-start(bf16[870,128]{1,0:T(8,128)(2,1)S(1)} %get-tuple-element.49), channel_id=1, source_target_pairs={{0,2},{4,6},{8,10},{12,14},{16,18},{20,22},{24,26},{28,30},{2,0},{... | collective-permute-start | bytes 668168 | tf_op jit(solution)/shard_map/ppermute | solution.py:24
  70.0 2.6 %collective-permute-start.5 = (bf16[870,128]{1,0:T(8,128)(2,1)S(1)}, bf16[870,128]{1,0:T(8,128)(2,1)S(1)}, u32[]{:S(2)}, u32[]{:S(2)}) collective-permute-start(bf16[870,128]{1,0:T(8,128)(2,1)S(1)} %get-tuple-element.50), channel_id=1, source_target_pairs={{2,4},{6,8},{10,12},{14,16},{18,20},{22,24},{26,28},{4,2},{8,6},{1... | collective-permute-start | bytes 668168 | tf_op jit(solution)/shard_map/ppermute | solution.py:24
  77.6 0.9 copy-start.1
  78.5 0.9 copy-start.5
  79.4 20.6 %collective-permute-start.10 = (bf16[1792,256]{1,0:T(8,128)(2,1)}, bf16[1792,256]{1,0:T(8,128)(2,1)S(1)}, u32[]{:S(2)}, u32[]{:S(2)}) collective-permute-start(bf16[1792,256]{1,0:T(8,128)(2,1)} %get-tuple-element.58), channel_id=1, source_target_pairs={{0,1},{1,0},{2,3},{3,2},{4,5},{5,4},{6,7},{7,6},{8,9},{9,8},{10,11... | collective-permute-start | bytes 2752520 | tf_op jit(solution)/shard_map/ppermute | solution.py:455
  82.2 8.6 %collective-permute-start.6 = (f32[128,256]{1,0:T(8,128)S(1)}, f32[128,256]{1,0:T(8,128)S(1)}, u32[]{:S(2)}, u32[]{:S(2)}) collective-permute-start(f32[128,256]{1,0:T(8,128)S(1)} %constant_dynamic-slice_fusion.7), channel_id=1, source_target_pairs={{0,2},{2,0},{4,6},{6,4},{8,10},{10,8},{12,14},{14,12},{16,18},{18,... | collective-permute-start | bytes 393224 | tf_op jit(solution)/shard_map/ppermute | solution.py:393
  90.9 4.8 %collective-permute-start.7 = (f32[32,256]{1,0:T(8,128)S(1)}, f32[32,256]{1,0:T(8,128)S(1)}, u32[]{:S(2)}, u32[]{:S(2)}) collective-permute-start(f32[32,256]{1,0:T(8,128)S(1)} %get-tuple-element.67), channel_id=1, source_target_pairs={{0,4},{2,6},{4,0},{6,2},{8,12},{10,14},{12,8},{14,10},{16,20},{18,... | collective-permute-start | bytes 98312 | tf_op jit(solution)/shard_map/ppermute | solution.py:393
  93.6 3.9 %collective-permute-start.8 = (f32[32,256]{1,0:T(8,128)S(1)}, f32[32,256]{1,0:T(8,128)S(1)}, u32[]{:S(2)}, u32[]{:S(2)}) collective-permute-start(f32[32,256]{1,0:T(8,128)S(1)} %get-tuple-element.69), channel_id=1, source_target_pairs={{0,8},{2,10},{4,12},{6,14},{8,0},{10,2},{12,4},{14,6},{16,24},{18,... | collective-permute-start | bytes 98312 | tf_op jit(solution)/shard_map/ppermute | solution.py:393
  95.2 4.8 %collective-permute-start.9 = (f32[32,256]{1,0:T(8,128)S(1)}, f32[32,256]{1,0:T(8,128)S(1)}, u32[]{:S(2)}, u32[]{:S(2)}) collective-permute-start(f32[32,256]{1,0:T(8,128)S(1)} %get-tuple-element.68), channel_id=1, source_target_pairs={{0,12},{2,14},{4,8},{6,10},{8,4},{10,6},{12,0},{14,2},{16,28},{18,... | collective-permute-start | bytes 98312 | tf_op jit(solution)/shard_map/ppermute | solution.py:393
  100.1 1.2 copy-start.2
  101.2 32.8 %copy-start.6 = (bf16[1792,256]{1,0:T(8,128)(2,1)S(1)}, bf16[1792,256]{1,0:T(8,128)(2,1)}, u32[]{:S(2)}) copy-start(bf16[1792,256]{1,0:T(8,128)(2,1)} %copy-done.5) | copy-start | bytes 2752516
  102.4 3.7 %collective-permute-start.11 = (f32[128,256]{1,0:T(8,128)S(1)}, f32[128,256]{1,0:T(8,128)S(1)}, u32[]{:S(2)}, u32[]{:S(2)}) collective-permute-start(f32[128,256]{1,0:T(8,128)S(1)} %constant_dynamic-slice_fusion.3), channel_id=1, source_target_pairs={{0,2},{2,0},{4,6},{6,4},{8,10},{10,8},{12,14},{14,12},{16,18},{18,... | collective-permute-start | bytes 393224 | tf_op jit(solution)/shard_map/ppermute | solution.py:393
  106.1 10.7 %collective-permute-start.12 = (f32[32,256]{1,0:T(8,128)S(1)}, f32[32,256]{1,0:T(8,128)S(1)}, u32[]{:S(2)}, u32[]{:S(2)}) collective-permute-start(f32[32,256]{1,0:T(8,128)S(1)} %get-tuple-element.64), channel_id=1, source_target_pairs={{0,4},{2,6},{4,0},{6,2},{8,12},{10,14},{12,8},{14,10},{16,20},{18,... | collective-permute-start | bytes 98312 | tf_op jit(solution)/shard_map/ppermute | solution.py:393
  114.8 3.9 %collective-permute-start.13 = (f32[32,256]{1,0:T(8,128)S(1)}, f32[32,256]{1,0:T(8,128)S(1)}, u32[]{:S(2)}, u32[]{:S(2)}) collective-permute-start(f32[32,256]{1,0:T(8,128)S(1)} %get-tuple-element.66), channel_id=1, source_target_pairs={{0,8},{2,10},{4,12},{6,14},{8,0},{10,2},{12,4},{14,6},{16,24},{18,... | collective-permute-start | bytes 98312 | tf_op jit(solution)/shard_map/ppermute | solution.py:393
  116.4 4.8 %collective-permute-start.14 = (f32[32,256]{1,0:T(8,128)S(1)}, f32[32,256]{1,0:T(8,128)S(1)}, u32[]{:S(2)}, u32[]{:S(2)}) collective-permute-start(f32[32,256]{1,0:T(8,128)S(1)} %get-tuple-element.65), channel_id=1, source_target_pairs={{0,12},{2,14},{4,8},{6,10},{8,4},{10,6},{12,0},{14,2},{16,28},{18,... | collective-permute-start | bytes 98312 | tf_op jit(solution)/shard_map/ppermute | solution.py:393
  121.2 5.8 %collective-permute-start.15 = (f32[2,32,256]{2,1,0:T(8,128)S(1)}, f32[2,32,256]{2,1,0:T(8,128)S(1)}, u32[]{:S(2)}, u32[]{:S(2)}) collective-permute-start(f32[2,32,256]{2,1,0:T(8,128)S(1)} %pad_maximum_fusion.1), channel_id=1, source_target_pairs={{0,16},{1,17},{2,18},{3,19},{4,20},{5,21},{6,22},{7,23},{8,24},{9,... | collective-permute-start | bytes 196616 | tf_op jit(solution)/shard_map/ppermute | solution.py:430
  123.6 4.3 %collective-permute-start.16 = (f32[2,32,256]{2,1,0:T(8,128)S(1)}, f32[2,32,256]{2,1,0:T(8,128)S(1)}, u32[]{:S(2)}, u32[]{:S(2)}) collective-permute-start(f32[2,32,256]{2,1,0:T(8,128)S(1)} %pad_maximum_fusion.1), channel_id=1, source_target_pairs={{0,1},{1,0},{2,3},{3,2},{4,5},{5,4},{6,7},{7,6},{8,9},{9,8},{10,11... | collective-permute-start | bytes 196616 | tf_op jit(solution)/shard_map/ppermute | solution.py:430
  125.2 6.1 %collective-permute-start.17 = (f32[2,32,256]{2,1,0:T(8,128)S(1)}, f32[2,32,256]{2,1,0:T(8,128)S(1)}, u32[]{:S(2)}, u32[]{:S(2)}) collective-permute-start(f32[2,32,256]{2,1,0:T(8,128)S(1)} %pad_maximum_fusion.1), channel_id=1, source_target_pairs={{0,17},{1,16},{2,19},{3,18},{4,21},{5,20},{6,23},{7,22},{8,25},{9,... | collective-permute-start | bytes 196616 | tf_op jit(solution)/shard_map/ppermute | solution.py:430
  131.4 5.2 %collective-permute-start.18 = (f32[3,32,256]{2,1,0:T(8,128)S(1)}, f32[3,32,256]{2,1,0:T(8,128)S(1)}, u32[]{:S(2)}, u32[]{:S(2)}) collective-permute-start(f32[3,32,256]{2,1,0:T(8,128)S(1)} %get-tuple-element.70), channel_id=1, source_target_pairs={{0,4},{2,6},{4,0},{6,2},{8,12},{10,14},{12,8},{14,10},{16,20},{18,... | collective-permute-start | bytes 294920 | tf_op jit(solution)/shard_map/ppermute | solution.py:393
  134.0 18.8 %collective-permute-start.22 = (bf16[1792,256]{1,0:T(8,128)(2,1)S(1)}, bf16[1792,256]{1,0:T(8,128)(2,1)S(1)}, u32[]{:S(2)}, u32[]{:S(2)}) collective-permute-start(bf16[1792,256]{1,0:T(8,128)(2,1)S(1)} %copy-done.6), channel_id=1, source_target_pairs={{0,1},{1,0},{2,3},{3,2},{4,5},{5,4},{6,7},{7,6},{8,9},{9,8},{10,11... | collective-permute-start | bytes 2752520 | tf_op jit(solution)/shard_map/ppermute | solution.py:477
  134.4 4.6 %collective-permute-start.19 = (f32[3,32,256]{2,1,0:T(8,128)S(1)}, f32[3,32,256]{2,1,0:T(8,128)S(1)}, u32[]{:S(2)}, u32[]{:S(2)}) collective-permute-start(f32[3,32,256]{2,1,0:T(8,128)S(1)} %get-tuple-element.70), channel_id=1, source_target_pairs={{0,8},{2,10},{4,12},{6,14},{8,0},{10,2},{12,4},{14,6},{16,24},{18,... | collective-permute-start | bytes 294920 | tf_op jit(solution)/shard_map/ppermute | solution.py:393
  134.4 5.5 %collective-permute-start.20 = (f32[3,32,256]{2,1,0:T(8,128)S(1)}, f32[3,32,256]{2,1,0:T(8,128)S(1)}, u32[]{:S(2)}, u32[]{:S(2)}) collective-permute-start(f32[3,32,256]{2,1,0:T(8,128)S(1)} %get-tuple-element.70), channel_id=1, source_target_pairs={{0,12},{2,14},{4,8},{6,10},{8,4},{10,6},{12,0},{14,2},{16,28},{18,... | collective-permute-start | bytes 294920 | tf_op jit(solution)/shard_map/ppermute | solution.py:393
  140.0 1.8 %collective-permute-start.21 = (f32[3,128,256]{2,1,0:T(8,128)S(1)}, f32[3,128,256]{2,1,0:T(8,128)S(1)}, u32[]{:S(2)}, u32[]{:S(2)}) collective-permute-start(f32[3,128,256]{2,1,0:T(8,128)S(1)} %constant_dynamic-update-slice_fusion.2), channel_id=1, source_target_pairs={{0,2},{2,0},{4,6},{6,4},{8,10},{10,8},{12,14},{14,12},{16,18},{18,... | collective-permute-start | bytes 1179656 | tf_op jit(solution)/shard_map/ppermute | solution.py:393
